TPU v7x, 32 devices: a whole 2x2x4 slice. The times are simulated.
32 devices in a mesh: slab: 8 (over y, x, core), lev: 4 (over z).
Axes of the slice: x: 2, y: 2, z: 4, core: 2. Of those that a mesh axis runs over, the one named last changes fastest.
Arguments:
- ensemble: float32 [80, 16, 18432], P(None, 'lev', 'slab'), may hold values from -6 to 6
- obs_cell: int32 [2, 256], replicated, may hold values from 0 to 294911, as said below
- obs_value: float32 [2, 256], replicated, may hold values from -6 to 6
- obs_var: float32 [2, 256], replicated, may hold values from 0.3 to 3
- obs_frac: float32 [2, 256], replicated, may hold values from 0 to 1
- loc_column: bfloat16 [2, 256, 18432], P(None, 'lev', 'slab'), may hold values from 0 to 1
- loc_level: float32 [2, 256, 16], P(None, None, 'lev'), may hold values from 0.2 to 1
Outputs:
- analysis: float32 [80, 16, 18432], P(None, 'lev', 'slab')
- prior_mean: float32 [2, 256], replicated
Inputs may be any that keep to these rules, and one draw needn't show every extreme that they name: `obs_cell`: in each block, every device's cells (a level band of 4 levels and a slab of 2304 columns) hold at least one observation, and one of them lies in the slab's last column.
All inputs are finite; a program needn't handle non-finite values.
Results may differ from a plain program's by a relative error of at most 0.0055.
Values may be sent and summed in bfloat16 or wider, within the bound.
No kernel may reach another device: no remote copies, remote signals or barrier semaphores. Data moves between devices by JAX's collectives and lax.ppermute only.
A program may use at most 64 MiB of HBM per device.

v0:
```python
import jax
import jax.numpy as jnp
from jax import lax
from jax.sharding import PartitionSpec as P


def obs_stats(prior_obs, obs_val, variance):
    members = prior_obs.shape[1]
    obs_mean = jnp.mean(prior_obs, axis=1)
    deviation = prior_obs - obs_mean[:, None]
    spread = jnp.sum(deviation * deviation, axis=1) / (members - 1.0)
    total_var = spread + variance
    shrink = 1.0 / (1.0 + jnp.sqrt(variance / total_var))
    gain_rows = ((obs_val - obs_mean)[:, None] - deviation * shrink[:, None]) / (
        total_var * (members - 1.0)
    )[:, None]
    return (obs_mean, deviation.astype(jnp.bfloat16), gain_rows.astype(jnp.bfloat16))


def cell_values(current, levels, columns):
    members, lev_rows, slab_cols = current.shape
    local_row = levels - lax.axis_index("lev") * lev_rows
    local_col = columns - lax.axis_index("slab") * slab_cols
    inside = (local_row >= 0) & (local_row < lev_rows) & (local_col >= 0) & (local_col < slab_cols)
    row_safe = jnp.clip(local_row, 0, lev_rows - 1)
    col_safe = jnp.clip(local_col, 0, slab_cols - 1)
    flattened = current.reshape(members, lev_rows * slab_cols)
    picked = jnp.take(flattened, row_safe * slab_cols + col_safe, axis=1)
    return jnp.where(inside[None, :], picked, 0.0).T


def column_table(loc_block, columns):
    rows_local, slab_cols = loc_block.shape
    local_col = columns - lax.axis_index("slab") * slab_cols
    inside = (local_col >= 0) & (local_col < slab_cols)
    col_safe = jnp.clip(local_col, 0, slab_cols - 1)
    picked = jnp.take(loc_block, col_safe, axis=1).astype(jnp.float32)
    picked = jnp.where(inside[None, :], picked, 0.0)
    holder = jnp.zeros((rows_local * lax.axis_size("lev"), columns.shape[0]), jnp.float32)
    return lax.dynamic_update_slice(
        holder, picked, (lax.axis_index("lev") * rows_local, jnp.int32(0))
    )


def level_table(lev_block, levels):
    lev_rows = lev_block.shape[1]
    local_row = levels - lax.axis_index("lev") * lev_rows
    inside = (local_row >= 0) & (local_row < lev_rows) & (lax.axis_index("slab") == 0)
    row_safe = jnp.clip(local_row, 0, lev_rows - 1)
    picked = jnp.take(lev_block, row_safe, axis=1)
    return jnp.where(inside[None, :], picked, 0.0)


def cell_update(values, dev_b, gain_b, col_table, lev_table):
    centred_cells = (values - jnp.mean(values, axis=1)[:, None]).astype(jnp.bfloat16)
    cross_cov = jnp.dot(dev_b, centred_cells.T, preferred_element_type=jnp.float32)
    mixed_rows = (lev_table * col_table * cross_cov).astype(jnp.bfloat16)
    return values + jnp.dot(gain_b.T, mixed_rows, preferred_element_type=jnp.float32).T


def regress_rows(running, loc_piece, centred, dev_b, gain_b, lev_weights):
    row_total = loc_piece.shape[0]
    row_step = min(row_total, 64)
    lev_rows = lev_weights.shape[1]
    slab_cols = loc_piece.shape[1]
    for offset in range(0, row_total, row_step):
        row_count = min(row_step, row_total - offset)
        row_piece = loc_piece[offset : offset + row_count]
        dev_rows = lax.dynamic_slice_in_dim(dev_b, offset, row_count, 0)
        gain_rows = lax.dynamic_slice_in_dim(gain_b, offset, row_count, 0)
        level_loc = lax.dynamic_slice_in_dim(lev_weights, offset, row_count, 0)
        cross_cov = jnp.dot(dev_rows, centred, preferred_element_type=jnp.float32).reshape(
            row_count, lev_rows, slab_cols
        )
        weights = level_loc[:, :, None] * row_piece[:, None, :].astype(jnp.float32)
        mixed_rows = (
            (weights * cross_cov).astype(jnp.bfloat16).reshape(row_count, lev_rows * slab_cols)
        )
        running = running + jnp.dot(gain_rows.T, mixed_rows, preferred_element_type=jnp.float32)
    return running


def on_device(ensemble, obs_cell, obs_value, obs_var, obs_frac, loc_column, loc_level):
    members, lev_rows, slab_cols = ensemble.shape
    n_blocks = obs_cell.shape[0]
    total_cols = slab_cols * lax.axis_size("slab")
    pair_index = {}
    pieces = []
    for later in range(n_blocks):
        levels = obs_cell[later] // total_cols
        columns = obs_cell[later] % total_cols
        next_cols = (columns + 1) % total_cols
        pieces.append(cell_values(ensemble, levels, columns))
        pieces.append(cell_values(ensemble, levels, next_cols))
        for earlier in range(later):
            pair_index[earlier, later] = len(pieces)
            pieces.append(column_table(loc_column[earlier], columns))
            pieces.append(column_table(loc_column[earlier], next_cols))
            pieces.append(level_table(loc_level[earlier], levels))
    summed = lax.psum(tuple(pieces), ("slab", "lev"))
    raw_first = []
    raw_second = []
    position = 0
    for later in range(n_blocks):
        raw_first.append(summed[position])
        raw_second.append(summed[position + 1])
        position = position + 2 + 3 * later
    current = ensemble
    prior_means = []
    for block_index in range(n_blocks):
        fraction = obs_frac[block_index]
        prior_obs = (1.0 - fraction)[:, None] * raw_first[block_index] + fraction[
            :, None
        ] * raw_second[block_index]
        obs_mean, dev_b, gain_b = obs_stats(prior_obs, obs_value[block_index], obs_var[block_index])
        prior_means.append(obs_mean)
        centred = (
            (current - jnp.mean(current, axis=0))
            .astype(jnp.bfloat16)
            .reshape(members, lev_rows * slab_cols)
        )
        lev_weights = loc_level[block_index]
        zero_incr = jnp.zeros((members, lev_rows * slab_cols), jnp.float32)
        increment = regress_rows(
            zero_incr,
            lax.all_gather(loc_column[block_index], "lev", axis=0, tiled=True),
            centred,
            dev_b,
            gain_b,
            lev_weights,
        )
        for later in range(block_index + 1, n_blocks):
            start_at = pair_index[block_index, later]
            col_first = summed[start_at]
            col_second = summed[start_at + 1]
            lev_table = summed[start_at + 2]
            raw_first[later] = cell_update(raw_first[later], dev_b, gain_b, col_first, lev_table)
            raw_second[later] = cell_update(raw_second[later], dev_b, gain_b, col_second, lev_table)
        current = current + increment.reshape(members, lev_rows, slab_cols)
    return (current, jnp.stack(prior_means))


def solution(mesh):
    in_specs = (
        P(None, "lev", "slab"),
        P(),
        P(),
        P(),
        P(),
        P(None, "lev", "slab"),
        P(None, None, "lev"),
    )
    out_specs = (P(None, "lev", "slab"), P())
    return jax.shard_map(
        on_device, mesh=mesh, in_specs=in_specs, out_specs=out_specs, check_vma=False
    )
```

profile of v0, /device:TPU:0, one launch (start us, length us, event | category | flops | bytes accessed | tf_op | source)
XLA Modules:
  0.0 248.2 jit_solution(5838560874919320193)
XLA Ops:
  9.5 0.8 fusion.80
  10.2 0.8 and_reduce_fusion.6
  11.2 5.2 %copy.43 = f32[80,4,2304]{0,2,1:T(8,128)} copy(f32[80,4,2304]{2,1,0:T(4,128)} %param.11) | data formatting | bytes 5898240 | tf_op args[0]
  16.3 3.1 %gather_fusion.3 = f32[256,80]{1,0:T(8,128)S(1)} fusion(f32[80,9216]{0,1:T(8,128)} %bitcast.227, s32[1024]{0:T(1024)S(1)} %pad_clamp_fusion.4), kind=kCustom, calls=%fused_computation.3.clone | custom fusion | bytes 164864 | tf_op jit(solution)/shard_map/jit(_take)/gather | solution.py:28
  19.5 3.1 %gather_fusion.5 = f32[256,80]{1,0:T(8,128)S(1)} fusion(f32[80,9216]{0,1:T(8,128)} %bitcast.228, s32[1024]{0:T(1024)S(1)} %pad_clamp_fusion.1), kind=kCustom, calls=%fused_computation.4.clone | custom fusion | bytes 164864 | tf_op jit(solution)/shard_map/jit(_take)/gather | solution.py:28
  23.7 0.9 gather_fusion.4
  24.7 1.0 gather_fusion
  25.8 0.9 gather_fusion.6
  26.8 3.1 %gather_fusion.2 = f32[256,80]{1,0:T(8,128)S(1)} fusion(f32[80,9216]{0,1:T(8,128)} %bitcast.229, s32[1024]{0:T(1024)S(1)} %pad_clamp_fusion.5), kind=kCustom, calls=%fused_computation.2.clone | custom fusion | bytes 164864 | tf_op jit(solution)/shard_map/jit(_take)/gather | solution.py:28
  29.8 3.1 %gather_fusion.1 = f32[256,80]{1,0:T(8,128)S(1)} fusion(f32[80,9216]{0,1:T(8,128)} %bitcast.230, s32[1024]{0:T(1024)S(1)} %pad_clamp_fusion.6), kind=kCustom, calls=%fused_computation.clone | custom fusion | bytes 164864 | tf_op jit(solution)/shard_map/jit(_take)/gather | solution.py:28
  32.9 0.8 fusion.52
  33.7 0.8 fusion.51
  35.2 0.8 fusion.53
  36.0 0.8 fusion.54
  38.9 0.8 fusion.94
  39.7 0.8 fusion.92
  41.7 1.6 subtract_convert_fusion.1
  43.3 154.2 %all-reduce.3.cloned.1.call-done = (f32[256,80]{1,0:T(8,128)}, f32[256,80]{1,0:T(8,128)}, f32[256,80]{1,0:T(8,128)}, f32[256,256]{1,0:T(8,128)}, f32[256,256]{1,...) async-done(((f32[256,80]{1,0:T(8,128)}, f32[256,80]{1,0:T(8,128)}, f32[256,80]{1,0:T(8,128)}, f32[256,256]{1,0:T(8,128)}, f32[256,256]{1,0:T(8,128)}, ...) | async-done | bytes 1114128 | tf_op jit(solution)/shard_map/psum | solution.py:100
  197.6 1.0 reduce_sum.75
  198.6 1.0 reduce_sum.76
  199.7 1.2 fusion.88
  201.3 2.3 fusion.32
  203.6 1.7 fusion.95
  206.4 1.5 fusion.45
  212.4 2.2 convolution_add_fusion.3
  214.6 4.5 %reshape.310 = f32[80,4,2304]{2,1,0:T(4,128)} reshape(f32[80,9216]{1,0:T(8,128)} %convolution_add_fusion.3) | data formatting | bytes 5898240 | tf_op jit(solution)/shard_map/reshape | solution.py:139
  219.1 2.8 %fusion.87 = (f32[4,2304]{1,0:T(4,128)S(1)}, f32[80,4,2304]{2,1,0:T(4,128)S(1)}) fusion(f32[80,4,2304]{2,1,0:T(4,128)S(1)} %copy-done, f32[80,4,2304]{2,1,0:T(4,128)} %reshape.310), kind=kLoop, calls=%fused_computation.218 | loop fusion | flops 1465344 | bytes 8884224 | tf_op jit(solution)/shard_map/reduce_sum | solution.py:118
  221.9 1.6 copy-done.2
  224.0 1.4 fusion.41
  229.8 2.2 convolution_add_fusion
  231.9 4.6 %reshape.316 = f32[80,4,2304]{2,1,0:T(4,128)} reshape(f32[80,9216]{1,0:T(8,128)} %convolution_add_fusion) | data formatting | bytes 5898240 | tf_op jit(solution)/shard_map/reshape | solution.py:139
  236.6 4.2 %add.227 = f32[80,4,2304]{2,1,0:T(4,128)} add(f32[80,4,2304]{2,1,0:T(4,128)S(1)} %copy-done.3, f32[80,4,2304]{2,1,0:T(4,128)} %reshape.316) | non-fusion elementwise | flops 737280 | bytes 8847360 | tf_op jit(solution)/shard_map/add | solution.py:139
  (93 shorter events, 17.8 us)
Async XLA Ops:
  8.0 189.6 %all-reduce.3.cloned.1.call-start = ((), (), s32[]{:S(2)}) async-start(), calls=%async_computation.2 | async-start | bytes 2621440 | tf_op jit(solution)/shard_map/psum | solution.py:100
  16.3 6.2 %copy-start.8 = (bf16[2,64,2304]{2,1,0:T(8,128)(2,1)S(1)}, bf16[2,64,2304]{2,1,0:T(8,128)(2,1)}, u32[]{:S(2)}) copy-start(bf16[2,64,2304]{2,1,0:T(8,128)(2,1)} %param.16) | copy-start | bytes 1769476
  19.5 5.2 %copy-start.9 = (f32[2,256,4]{1,2,0:T(4,128)S(1)}, f32[2,256,4]{1,2,0:T(4,128)}, u32[]{:S(2)}) copy-start(f32[2,256,4]{1,2,0:T(4,128)} %param.17) | copy-start | bytes 24580
  23.3 2.3 copy-start.4
  36.0 5.2 %copy-start = (f32[80,4,2304]{2,1,0:T(4,128)S(1)}, f32[80,4,2304]{2,1,0:T(4,128)}, u32[]{:S(2)}) copy-start(f32[80,4,2304]{2,1,0:T(4,128)} %param.11) | copy-start | bytes 8847364
  36.8 0.7 copy-start.7
  36.9 0.7 copy-start.6
  37.7 168.7 %all-gather.5.cloned.1.call-start = ((), (), s32[]{:S(2)}) async-start(), calls=%async_computation | async-start | bytes 1474560 | tf_op jit(solution)/shard_map/all_gather | solution.py:126
  38.2 185.7 %all-gather.7.cloned.1.call-start = ((), (), s32[]{:S(2)}) async-start(), calls=%async_computation.1 | async-start | bytes 1474560 | tf_op jit(solution)/shard_map/all_gather | solution.py:126
  197.6 6.0 %copy-start.5 = (f32[256,256]{1,0:T(8,128)S(1)}, f32[256,256]{1,0:T(8,128)}, u32[]{:S(2)}) copy-start(f32[256,256]{1,0:T(8,128)} %get-tuple-element.16) | copy-start | bytes 786436
  206.4 1.7 copy-start.1
  221.8 1.6 copy-start.2
  231.9 4.7 %copy-start.3 = (f32[80,4,2304]{2,1,0:T(4,128)S(1)}, f32[80,4,2304]{2,1,0:T(4,128)}, u32[]{:S(2)}) copy-start(f32[80,4,2304]{2,1,0:T(4,128)} %copy-done.2) | copy-start | bytes 8847364
Sparse Core Ops, SparseCore 0:
  37.8 159.7 all-reduce.2
Sparse Core Ops, SparseCore 1:
  39.7 35.3 all-gather.4
  76.5 30.3 all-gather.6
where the time goes:
time: 249 us; the launch traced here: 248 us
  waiting for transfers between devices  155 us (62%)
  local copies, waits for them, and re-layouts  36.3 us (15%)
  other arithmetic  24.3 us (10%)
  matrix products  16.2 us (7%)
  between operations  16 us (6%)
    psum x1, waiting for transfers between devices, on_device(): summed = lax.psum(tuple(pieces), ('slab', 'lev'))  154 us
    gather x4, local copies, waits for them, and re-layouts, cell_values(): picked = jnp.take(flattened, row_safe * slab_cols + col_safe, axis=1)  12.3 us
    reshape x2, local copies, waits for them, and re-layouts, on_device(): current = current + increment.reshape(members, lev_rows, slab_cols)  9.14 us
    unnamed x22, local copies, waits for them, and re-layouts  8.05 us
    dot_general x8, matrix products, regress_rows(): jnp.dot(gain_rows.T, mixed_rows, preferred_element_type=jnp.float32)  7.72 us
  transfers between devices with their start and end apart: 3, of which 1 were waited for; matrix products, arithmetic and copies ran while one was open for 12% of the time, Pallas kernels for 0%

commit v1 on v0

v1 whole, which is shorter than its diff:
```python
import functools

import jax
import jax.numpy as jnp
from jax import lax
from jax.experimental import pallas as pl
from jax.experimental.pallas import tpu as pltpu
from jax.sharding import PartitionSpec as P

LANES = 128
CELL_BITS = 16


def swap(value, axis, bit):
    size = lax.axis_size(axis)
    return lax.ppermute(value, axis, [(i, i ^ bit) for i in range(size)])


def add_over(value, axes):
    for axis in axes:
        size = lax.axis_size(axis)
        if size & (size - 1):
            value = lax.psum(value, axis)
            continue
        bit = 1
        while bit < size:
            value = value + swap(value, axis, bit)
            bit *= 2
    return value


def rows_over(own, axis):
    size = lax.axis_size(axis)
    shards = {0: own}
    bit = size // 2
    order = sorted(range(1, size), key=lambda p: (bin(p).count("1"), -p))
    for p in order:
        low = p & -p
        shards[p] = swap(shards[p ^ low], axis, low)
    return [shards[p] for p in range(size)]


def list_owned(key_ref, list_ref, count):
    def step(o, found):
        key = key_ref[0, o]
        list_ref[found] = o
        return found + (key >= 0).astype(jnp.int32)

    return lax.fori_loop(0, count, step, jnp.int32(0), unroll=8)


def gather_priors(key_ref, frac_ref, list_ref, found, source_ref, out_ref):
    members = out_ref.shape[0]
    slab_cols = source_ref.shape[2]
    lane = lax.broadcasted_iota(jnp.int32, (members, LANES), 1)
    out_ref[...] = jnp.zeros(out_ref.shape, jnp.float32)

    def step(i, carry):
        o = list_ref[i]
        key = key_ref[0, o]
        fraction = frac_ref[0, o]
        row = key >> CELL_BITS
        col = (key & ((1 << CELL_BITS) - 1)) - 1
        first = jnp.maximum(col, 0)
        second = jnp.minimum(col + 1, slab_cols - 1)
        weight_first = jnp.where(col >= 0, 1.0 - fraction, 0.0)
        weight_second = jnp.where(col + 1 < slab_cols, fraction, 0.0)
        slot = o & (LANES - 1)

        def picked(c):
            tile = source_ref[row, :, pl.ds(pl.multiple_of((c >> 7) * LANES, LANES), LANES)]
            return pltpu.roll(tile, (slot - c) & (LANES - 1), 1)

        value = weight_first * picked(first) + weight_second * picked(second)
        where_out = pl.ds(pl.multiple_of((o >> 7) * LANES, LANES), LANES)
        out_ref[:, where_out] = jnp.where(lane == slot, value, out_ref[:, where_out])
        return carry

    lax.fori_loop(0, found, step, 0)


def load_levels(ens_ref, cur_ref, sems):
    return [
        pltpu.make_async_copy(ens_ref.at[:, l, :], cur_ref.at[l], sems.at[l])
        for l in range(cur_ref.shape[0])
    ]


def prior_kernel(key_ref, frac_ref, ens_ref, out_ref, cur_ref, list_ref, sems):
    copies = load_levels(ens_ref, cur_ref, sems)
    for copy in copies:
        copy.start()
    found = list_owned(key_ref, list_ref, key_ref.shape[1])
    for copy in copies:
        copy.wait()
    gather_priors(key_ref, frac_ref, list_ref, found, cur_ref, out_ref)


def regroup(value, lev_index, groups):
    total = value.shape[1]
    lane = lax.broadcasted_iota(jnp.int32, value.shape, 1)
    bit = 1
    while bit < groups:
        span = (total // groups) * bit
        other = jnp.where(
            (lane & span) != 0, pltpu.roll(value, span, 1), pltpu.roll(value, total - span, 1)
        )
        value = jnp.where((lev_index & bit) != 0, other, value)
        bit *= 2
    return value


def observe(lev_index, groups, prior_ref, value_ref, var_ref, level_ref, mean_ref, dev_ref, gain_ref, level_b_ref):
    prior = prior_ref[...]
    members, n_obs = prior.shape
    lev_rows = level_ref.shape[1]
    variance = var_ref[0]
    obs_mean = jnp.sum(prior, axis=0, keepdims=True) / members
    mean_ref[...] = obs_mean
    deviation = prior - obs_mean
    spread = jnp.sum(deviation * deviation, axis=0, keepdims=True) / (members - 1.0)
    total_var = spread + variance
    shrink = 1.0 / (1.0 + jnp.sqrt(variance / total_var))
    gain = ((value_ref[0] - obs_mean) - deviation * shrink) / (total_var * (members - 1.0))
    gain_ref[...] = regroup(gain, lev_index, groups).astype(jnp.bfloat16)
    pad = jnp.zeros((LANES - members, n_obs), jnp.float32)
    dev_all = jnp.concatenate([regroup(deviation, lev_index, groups), pad], axis=0)
    dev_ref[...] = dev_all.T[:, :members].astype(jnp.bfloat16)
    level_all = jnp.concatenate(
        [regroup(level_ref[0], lev_index, groups), jnp.zeros((LANES - lev_rows, n_obs), jnp.float32)], axis=0
    ).T
    for l in range(lev_rows):
        level_b_ref[l] = jnp.broadcast_to(level_all[:, l : l + 1], (n_obs, LANES))


def regress(cur_of, put, shards, dev_ref, gain_ref, level_b_ref, l, slab_cols, width):
    dev = dev_ref[...]
    gain = gain_ref[...]
    reps = width // LANES

    def step(i, carry):
        cols = pl.ds(pl.multiple_of(i * width, width), width)
        field = cur_of(cols)
        members = field.shape[0]
        centred = (field - jnp.sum(field, axis=0, keepdims=True) / members).astype(jnp.bfloat16)
        cross = jnp.dot(dev, centred, preferred_element_type=jnp.float32)
        weights = jnp.concatenate([s[0, :, cols] if len(s.shape) == 3 else s[:, cols] for s in shards], axis=0)
        level = jnp.concatenate([level_b_ref[l]] * reps, axis=1)
        mixed = ((level * weights.astype(jnp.float32)) * cross).astype(jnp.bfloat16)
        put(cols, field + jnp.dot(gain, mixed, preferred_element_type=jnp.float32))
        return carry

    lax.fori_loop(0, slab_cols // width, step, 0)


def first_kernel(groups, width, lev_ref, key_ref, frac_ref, prior_ref, value_ref, var_ref, level_ref, ens_ref, *rest):
    shards = rest[:groups]
    cur_out, mean_ref, next_ref, cur_ref, dev_ref, gain_ref, level_b_ref, list_ref, sems = rest[groups:]
    lev_rows, members, slab_cols = cur_ref.shape
    copies = load_levels(ens_ref, cur_ref, sems)
    for copy in copies:
        copy.start()
    found = list_owned(key_ref, list_ref, key_ref.shape[1])
    observe(lev_ref[0], groups, prior_ref, value_ref, var_ref, level_ref, mean_ref, dev_ref, gain_ref, level_b_ref)
    for l in range(lev_rows):
        copies[l].wait()

        def put(cols, value, l=l):
            cur_out[l, :, cols] = value

        regress(lambda cols, l=l: cur_ref[l, :, cols], put, shards, dev_ref, gain_ref, level_b_ref, l, slab_cols, width)
    gather_priors(key_ref, frac_ref, list_ref, found, cur_out, next_ref)


def last_kernel(groups, width, lev_ref, prior_ref, value_ref, var_ref, level_ref, cur_ref, *rest):
    shards = rest[:groups]
    ens_out, mean_ref, buf_ref, dev_ref, gain_ref, level_b_ref, sems = rest[groups:]
    lev_rows, members, slab_cols = cur_ref.shape
    observe(lev_ref[0], groups, prior_ref, value_ref, var_ref, level_ref, mean_ref, dev_ref, gain_ref, level_b_ref)
    copies = []
    for l in range(lev_rows):

        def put(cols, value, l=l):
            buf_ref[l, :, cols] = value

        regress(lambda cols, l=l: cur_ref[l, :, cols], put, shards, dev_ref, gain_ref, level_b_ref, l, slab_cols, width)
        copies.append(pltpu.make_async_copy(buf_ref.at[l], ens_out.at[:, l, :], sems.at[l]))
        copies[l].start()
    for copy in copies:
        copy.wait()


def smem_row(b, n_obs):
    return pl.BlockSpec((1, n_obs), lambda *_: (b, 0), memory_space=pltpu.SMEM)


def on_device(ensemble, obs_cell, obs_value, obs_var, obs_frac, loc_column, loc_level):
    members, lev_rows, slab_cols = ensemble.shape
    n_blocks, n_obs = obs_cell.shape
    shard_rows = loc_column.shape[1]
    groups = lax.axis_size("lev")
    n_slabs = lax.axis_size("slab")
    total_cols = slab_cols * n_slabs
    width = 256 if slab_cols % 256 == 0 else LANES
    lev_index = lax.axis_index("lev")

    local_row = obs_cell // total_cols - lev_index * lev_rows
    local_col = (obs_cell % total_cols - lax.axis_index("slab") * slab_cols + 1) % total_cols
    owned = (local_row >= 0) & (local_row < lev_rows) & (local_col <= slab_cols)
    keys = jnp.where(owned, (local_row << CELL_BITS) + local_col, -1).reshape(n_blocks, 1, n_obs)
    fracs = obs_frac.reshape(n_blocks, 1, n_obs)
    values = obs_value.reshape(n_blocks, 1, n_obs)
    variances = obs_var.reshape(n_blocks, 1, n_obs)
    levels = loc_level.transpose(0, 2, 1)
    lev_scalar = lev_index.reshape(1).astype(jnp.int32)

    smem = pl.BlockSpec(memory_space=pltpu.SMEM)
    vmem = pl.BlockSpec(memory_space=pltpu.VMEM)
    hbm = pl.BlockSpec(memory_space=pl.ANY)
    f32 = jnp.float32
    field = jax.ShapeDtypeStruct((lev_rows, members, slab_cols), f32)
    row = jax.ShapeDtypeStruct((1, n_obs), f32)
    rows = jax.ShapeDtypeStruct((members, n_obs), f32)
    field_scratch = pltpu.VMEM((lev_rows, members, slab_cols), f32)
    work = [
        pltpu.VMEM((n_obs, members), jnp.bfloat16),
        pltpu.VMEM((members, n_obs), jnp.bfloat16),
        pltpu.VMEM((lev_rows, n_obs, LANES), f32),
    ]
    own_list = pltpu.SMEM((n_obs,), jnp.int32)
    dma = pltpu.SemaphoreType.DMA((lev_rows,))

    shards = [rows_over(loc_column[b], "lev") for b in range(n_blocks)]

    prior = pl.pallas_call(
        prior_kernel,
        out_shape=rows,
        in_specs=[smem, smem, hbm],
        out_specs=vmem,
        scratch_shapes=[field_scratch, own_list, dma],
        name="cells",
    )(keys[0], fracs[0], ensemble)
    prior = add_over(prior, ("slab", "lev"))

    current, mean_first, prior_next = pl.pallas_call(
        functools.partial(first_kernel, groups, width),
        out_shape=(field, row, rows),
        in_specs=[smem, smem, smem, vmem, vmem, vmem, vmem, hbm] + [vmem] * groups,
        out_specs=(vmem, vmem, vmem),
        scratch_shapes=[field_scratch] + work + [own_list, dma],
        name="block_first",
    )(lev_scalar, keys[1], fracs[1], prior, values[:1], variances[:1], levels[:1], ensemble, *shards[0])
    prior_next = add_over(prior_next, ("slab", "lev"))

    analysis, mean_last = pl.pallas_call(
        functools.partial(last_kernel, groups, width),
        out_shape=(jax.ShapeDtypeStruct(ensemble.shape, f32), row),
        in_specs=[smem, vmem, vmem, vmem, vmem, vmem] + [vmem] * groups,
        out_specs=(hbm, vmem),
        scratch_shapes=[field_scratch] + work + [dma],
        name="block_last",
    )(lev_scalar, prior_next, values[1:], variances[1:], levels[1:], current, *shards[1])
    return (analysis, jnp.concatenate([mean_first, mean_last], axis=0))


def solution(mesh):
    in_specs = (
        P(None, "lev", "slab"),
        P(),
        P(),
        P(),
        P(),
        P(None, "lev", "slab"),
        P(None, None, "lev"),
    )
    out_specs = (P(None, "lev", "slab"), P())
    return jax.shard_map(
        on_device, mesh=mesh, in_specs=in_specs, out_specs=out_specs, check_vma=False
    )
```

time: 249 us -> 114 us (0.46)
  waiting for transfers between devices: 155 us -> 47.4 us
  Pallas kernels: 0 us -> 42.3 us
  local copies, waits for them, and re-layouts: 36.3 us -> 5.85 us
  other arithmetic: 24.3 us -> 5.1 us
  matrix products: 16.2 us -> 0 us
  between operations: 16 us -> 0.92 us
  starting transfers between devices: 0.12 us -> 12 us
    psum x1 -> x0, waiting for transfers between devices: 154 us -> none  [on_device(): summed = lax.psum(tuple(pieces), ('slab', 'lev'))]
    ppermute x0 -> x16, waiting for transfers between devices: none -> 47.4 us  [swap(): return lax.ppermute(value, axis, [(i, i ^ bit) for i in range(size)])]
    pallas_call x0 -> x3, Pallas kernels: none -> 42.3 us  [the longest x1 19.4 us: on_device(): pl.pallas_call(functools.partial(first_kernel, groups, width), out_shape=...]
    dot_general x18 -> x0, matrix products: 16.2 us -> none  [the longest x8 7.72 us: regress_rows(): jnp.dot(gain_rows.T, mixed_rows, preferred_element_type=jnp.float32)]
    gather x10 -> x0, local copies, waits for them, and re-layouts: 15.3 us -> none  [the longest x4 12.3 us: cell_values(): picked = jnp.take(flattened, row_safe * slab_cols + col_safe, axis=1)]
    ppermute x0 -> x16, starting transfers between devices: none -> 12 us  [swap(): return lax.ppermute(value, axis, [(i, i ^ bit) for i in range(size)])]
    reshape x10 -> x0, local copies, waits for them, and re-layouts: 9.8 us -> none  [the longest x2 9.14 us: on_device(): current = current + increment.reshape(members, lev_rows, slab_cols)]
    reduce_sum x7 -> x0, other arithmetic: 6.89 us -> none  [the longest x2 3.28 us: on_device(): jnp.mean(current, axis=0)]
  transfers between devices with their start and end apart: 3 -> 16, of which waited for: 1 -> 10; matrix products, arithmetic and copies ran while one was open for 12% -> 6% of each run, Pallas kernels for 0% -> 23%
where the time goes in v1:
time: 114 us
  waiting for transfers between devices  47.4 us (42%)
  Pallas kernels  42.3 us (37%)
  starting transfers between devices  12 us (11%)
  local copies, waits for them, and re-layouts  5.85 us (5%)
  other arithmetic  5.1 us (4%)
    ppermute x16, waiting for transfers between devices, swap(): return lax.ppermute(value, axis, [(i, i ^ bit) for i in range(size)])  47.4 us
    pallas_call x1, Pallas kernels, on_device(): pl.pallas_call(functools.partial(first_kernel, groups, width), out_shape=...  19.4 us
    pallas_call x1, Pallas kernels, on_device(): pl.pallas_call(functools.partial(last_kernel, groups, width), out_shape=(...  16.7 us
    ppermute x16, starting transfers between devices, swap(): return lax.ppermute(value, axis, [(i, i ^ bit) for i in range(size)])  12 us
    pallas_call x1, Pallas kernels, on_device(): pl.pallas_call(prior_kernel, out_shape=rows, in_specs=[smem, smem, hbm],...  6.25 us
    add x10, other arithmetic, add_over(): value = value + swap(value, axis, bit)  3.14 us
  transfers between devices with their start and end apart: 16, of which 10 were waited for; matrix products, arithmetic and copies ran while one was open for 6% of the time, Pallas kernels for 23%

profile of v1, /device:TPU:0, one launch (start us, length us, event | category | flops | bytes accessed | tf_op | source)
XLA Modules:
  0.0 113.6 jit_solution(17780950619875089731)
XLA Ops:
  0.7 1.1 slice_bitcast_fusion
  1.8 4.1 %collective-permute-start.6 = (bf16[64,2304]{1,0:T(8,128)(2,1)S(1)}, bf16[64,2304]{1,0:T(8,128)(2,1)S(1)}, u32[]{:S(2)}, u32[]{:S(2)}) collective-permute-start(bf16[64,2304]{1,0:T(8,128)(2,1)S(1)} %get-tuple-element.13.rest_0_), channel_id=1, source_target_pairs={{0,2},{1,3},{2,0},{3,1},{4,6},{5,7},{6,4},{7,5},{8,10},{9,11},{10,... | collective-permute-start | bytes 884744 | tf_op jit(solution)/shard_map/ppermute | solution.py:16
  5.9 0.7 and_select_fusion
  6.6 0.6 fusion.3
  7.2 1.3 %fusion.2 = (f32[1,256]{1,0:T(1,128)}, f32[1,256]{1,0:T(1,128)}) fusion(f32[2,256]{1,0:T(2,128)} %param.11), kind=kLoop, calls=%fused_computation.13 | loop fusion | bytes 4096 | tf_op jit(solution)/shard_map/slice | solution.py:242
  8.5 6.2 %cells.1 = f32[80,256]{1,0:T(8,128)} custom-call(s32[1,256]{1,0:T(1,128)} %get-tuple-element.22.key_ref, f32[1,256]{1,0:T(1,128)} %get-tuple-element.20.frac_ref, f32[80,4,2304]{2,1,0:T(4,128)} %ens_ref.3), custom_call_target="tpu_custom_call" | custom-call | tf_op jit(solution)/shard_map/cells/pallas_call | solution.py:235
  14.9 1.5 %collective-permute-done = f32[80,256]{1,0:T(8,128)S(1)} collective-permute-done((f32[80,256]{1,0:T(8,128)}, f32[80,256]{1,0:T(8,128)S(1)}, u32[]{:S(2)}, u32[]{:S(2)}) %collective-permute-start) | collective-permute-done | bytes 81952 | tf_op jit(solution)/shard_map/ppermute | solution.py:16
  16.4 0.9 add.52
  17.3 4.5 %collective-permute-done.1 = f32[80,256]{1,0:T(8,128)S(1)} collective-permute-done((f32[80,256]{1,0:T(8,128)S(1)}, f32[80,256]{1,0:T(8,128)S(1)}, u32[]{:S(2)}, u32[]{:S(2)}) %collective-permute-start.1) | collective-permute-done | bytes 81952 | tf_op jit(solution)/shard_map/ppermute | solution.py:16
  21.9 1.5 %collective-permute-start.5 = (bf16[64,2304]{1,0:T(8,128)(2,1)S(1)}, bf16[64,2304]{1,0:T(8,128)(2,1)S(1)}, u32[]{:S(2)}, u32[]{:S(2)}) collective-permute-start(bf16[64,2304]{1,0:T(8,128)(2,1)S(1)} %get-tuple-element.13.rest_0_), channel_id=1, source_target_pairs={{0,1},{1,0},{2,3},{3,2},{4,5},{5,4},{6,7},{7,6},{8,9},{9,8},{10,11... | collective-permute-start | bytes 884744 | tf_op jit(solution)/shard_map/ppermute | solution.py:16
  23.5 2.9 %collective-permute-done.2 = f32[80,256]{1,0:T(8,128)S(1)} collective-permute-done((f32[80,256]{1,0:T(8,128)S(1)}, f32[80,256]{1,0:T(8,128)S(1)}, u32[]{:S(2)}, u32[]{:S(2)}) %collective-permute-start.2) | collective-permute-done | bytes 81952 | tf_op jit(solution)/shard_map/ppermute | solution.py:16
  26.4 1.5 %collective-permute-start.3 = (f32[80,256]{1,0:T(8,128)S(1)}, f32[80,256]{1,0:T(8,128)S(1)}, u32[]{:S(2)}, u32[]{:S(2)}) collective-permute-start(f32[80,256]{1,0:T(8,128)S(1)} %add.54), channel_id=1, source_target_pairs={{0,1},{1,0},{2,3},{3,2},{4,5},{5,4},{6,7},{7,6},{8,9},{9,8},{10,11... | collective-permute-start | bytes 245768 | tf_op jit(solution)/shard_map/ppermute | solution.py:16
  27.9 0.5 collective-permute-start.7
  28.5 0.6 fusion.1
  29.1 11.7 %collective-permute-done.3 = f32[80,256]{1,0:T(8,128)S(1)} collective-permute-done((f32[80,256]{1,0:T(8,128)S(1)}, f32[80,256]{1,0:T(8,128)S(1)}, u32[]{:S(2)}, u32[]{:S(2)}) %collective-permute-start.3) | collective-permute-done | bytes 81952 | tf_op jit(solution)/shard_map/ppermute | solution.py:16
  40.9 0.6 slice_bitcast_fusion.2
  41.5 5.6 %collective-permute-done.4 = f32[80,256]{1,0:T(8,128)S(1)} collective-permute-done((f32[80,256]{1,0:T(8,128)S(1)}, f32[80,256]{1,0:T(8,128)S(1)}, u32[]{:S(2)}, u32[]{:S(2)}) %collective-permute-start.4) | collective-permute-done | bytes 81952 | tf_op jit(solution)/shard_map/ppermute | solution.py:16
  47.1 0.6 add.56.prior_ref
  47.8 0.7 copy-done.4
  48.6 19.4 %block_first.1 = (f32[4,80,2304]{2,1,0:T(8,128)}, f32[1,256]{1,0:T(1,128)}, f32[80,256]{1,0:T(8,128)}) custom-call(s32[1]{0:T(128)} %bitcast.lev_ref, s32[1,256]{1,0:T(1,128)} %get-tuple-element.23.key_ref, f32[1,256]{1,0:T(1,128)} %get-tuple-element.21.frac_ref, f32[80,256]{1,0:T(8,128)} %add.56.prior_ref, f32[1,1,256]{2,1,0:T(1,128)} %get-tuple-element.24.value_ref, ...), custom_call_target="tpu_custom_call" | custom-call | tf_op jit(solution)/shard_map/block_first/pallas_call | solution.py:245
  68.0 1.5 %collective-permute-done.8 = f32[80,256]{1,0:T(8,128)S(1)} collective-permute-done((f32[80,256]{1,0:T(8,128)}, f32[80,256]{1,0:T(8,128)S(1)}, u32[]{:S(2)}, u32[]{:S(2)}) %collective-permute-start.8) | collective-permute-done | bytes 81952 | tf_op jit(solution)/shard_map/ppermute | solution.py:16
  69.5 0.9 add.57
  70.6 2.0 %collective-permute-start.15 = (bf16[64,2304]{1,0:T(8,128)(2,1)S(1)}, bf16[64,2304]{1,0:T(8,128)(2,1)S(1)}, u32[]{:S(2)}, u32[]{:S(2)}) collective-permute-start(bf16[64,2304]{1,0:T(8,128)(2,1)S(1)} %collective-permute-done.14.rest_2_), channel_id=1, source_target_pairs={{0,1},{1,0},{2,3},{3,2},{4,5},{5,4},{6,7},{7,6},{8,9},{9,8},{10,11... | collective-permute-start | bytes 884744 | tf_op jit(solution)/shard_map/ppermute | solution.py:16
  72.6 2.4 %collective-permute-done.9 = f32[80,256]{1,0:T(8,128)S(1)} collective-permute-done((f32[80,256]{1,0:T(8,128)S(1)}, f32[80,256]{1,0:T(8,128)S(1)}, u32[]{:S(2)}, u32[]{:S(2)}) %collective-permute-start.9) | collective-permute-done | bytes 81952 | tf_op jit(solution)/shard_map/ppermute | solution.py:16
  75.1 4.4 %collective-permute-done.10 = f32[80,256]{1,0:T(8,128)S(1)} collective-permute-done((f32[80,256]{1,0:T(8,128)S(1)}, f32[80,256]{1,0:T(8,128)S(1)}, u32[]{:S(2)}, u32[]{:S(2)}) %collective-permute-start.10) | collective-permute-done | bytes 81952 | tf_op jit(solution)/shard_map/ppermute | solution.py:16
  79.6 8.1 %collective-permute-done.11 = f32[80,256]{1,0:T(8,128)S(1)} collective-permute-done((f32[80,256]{1,0:T(8,128)S(1)}, f32[80,256]{1,0:T(8,128)S(1)}, u32[]{:S(2)}, u32[]{:S(2)}) %collective-permute-start.11) | collective-permute-done | bytes 81952 | tf_op jit(solution)/shard_map/ppermute | solution.py:16
  87.7 1.6 %collective-permute-start.12 = (f32[80,256]{1,0:T(8,128)S(1)}, f32[80,256]{1,0:T(8,128)S(1)}, u32[]{:S(2)}, u32[]{:S(2)}) collective-permute-start(f32[80,256]{1,0:T(8,128)S(1)} %add.60), channel_id=1, source_target_pairs={{0,2},{1,3},{2,0},{3,1},{4,6},{5,7},{6,4},{7,5},{8,10},{9,11},{10,... | collective-permute-start | bytes 245768 | tf_op jit(solution)/shard_map/ppermute | solution.py:16
  89.3 4.8 %collective-permute-done.12 = f32[80,256]{1,0:T(8,128)S(1)} collective-permute-done((f32[80,256]{1,0:T(8,128)S(1)}, f32[80,256]{1,0:T(8,128)S(1)}, u32[]{:S(2)}, u32[]{:S(2)}) %collective-permute-start.12) | collective-permute-done | bytes 81952 | tf_op jit(solution)/shard_map/ppermute | solution.py:16
  94.1 0.6 add.61.prior_ref
  94.8 0.7 copy-done.5
  95.6 16.7 %block_last.1 = (f32[80,4,2304]{2,1,0:T(4,128)}, f32[1,256]{1,0:T(1,128)}) custom-call(s32[1]{0:T(128)} %bitcast.lev_ref, f32[80,256]{1,0:T(8,128)} %add.61.prior_ref, f32[1,1,256]{2,1,0:T(1,128)} %get-tuple-element.25.value_ref, f32[1,1,256]{2,1,0:T(1,128)} %get-tuple-element.16.var_ref, f32[1,4,256]{2,1,0:T(4,128)} %get-tuple-element.14.level_ref, ...), custom_call_target="tpu_custom_call" | custom-call | tf_op jit(solution)/shard_map/block_last/pallas_call | solution.py:255
  112.3 1.3 %pad_maximum_fusion = f32[2,256]{1,0:T(2,128)} fusion(f32[1,256]{1,0:T(1,128)} %get-tuple-element.11, f32[1,256]{1,0:T(1,128)S(1)} %copy-done.11), kind=kLoop, calls=%fused_computation.7 | loop fusion | flops 512 | bytes 4096 | tf_op jit(solution)/shard_map/concatenate | solution.py:263
  (44 shorter events, 1.0 us)
Async XLA Ops:
  0.6 27.8 %copy-start.8 = (f32[2,256,4]{1,2,0:T(4,128)S(1)}, f32[2,256,4]{1,2,0:T(4,128)}, u32[]{:S(2)}) copy-start(f32[2,256,4]{1,2,0:T(4,128)} %param.13) | copy-start | bytes 24580
  0.6 40.3 %copy-start.9 = (f32[2,256]{1,0:T(2,128)S(1)}, f32[2,256]{1,0:T(2,128)}, u32[]{:S(2)}) copy-start(f32[2,256]{1,0:T(2,128)} %param.10) | copy-start | bytes 6148
  0.7 40.3 %copy-start.10 = (f32[2,256]{1,0:T(2,128)S(1)}, f32[2,256]{1,0:T(2,128)}, u32[]{:S(2)}) copy-start(f32[2,256]{1,0:T(2,128)} %param.9) | copy-start | bytes 6148
  1.8 46.0 %copy-start.1 = (bf16[64,2304]{1,0:T(8,128)(2,1)}, bf16[64,2304]{1,0:T(8,128)(2,1)S(1)}, u32[]{:S(2)}) copy-start(bf16[64,2304]{1,0:T(8,128)(2,1)S(1)} %get-tuple-element.13.rest_0_) | copy-start | bytes 884740
  1.8 68.7 %copy-start = (bf16[64,2304]{1,0:T(8,128)(2,1)}, bf16[64,2304]{1,0:T(8,128)(2,1)S(1)}, u32[]{:S(2)}) copy-start(bf16[64,2304]{1,0:T(8,128)(2,1)S(1)} %get-tuple-element.12.rest_0_) | copy-start | bytes 884740
  1.8 26.1 %collective-permute-start.6 = (bf16[64,2304]{1,0:T(8,128)(2,1)S(1)}, bf16[64,2304]{1,0:T(8,128)(2,1)S(1)}, u32[]{:S(2)}, u32[]{:S(2)}) collective-permute-start(bf16[64,2304]{1,0:T(8,128)(2,1)S(1)} %get-tuple-element.13.rest_0_), channel_id=1, source_target_pairs={{0,2},{1,3},{2,0},{3,1},{4,6},{5,7},{6,4},{7,5},{8,10},{9,11},{10,... | collective-permute-start | bytes 884744 | tf_op jit(solution)/shard_map/ppermute | solution.py:16
  14.8 1.6 %collective-permute-start = (f32[80,256]{1,0:T(8,128)}, f32[80,256]{1,0:T(8,128)S(1)}, u32[]{:S(2)}, u32[]{:S(2)}) collective-permute-start(f32[80,256]{1,0:T(8,128)} %cells.1), channel_id=1, source_target_pairs={{0,4},{4,0},{8,12},{12,8},{16,20},{20,16},{24,28},{28,24},{1,5},{5... | collective-permute-start | bytes 245768 | tf_op jit(solution)/shard_map/ppermute | solution.py:16
  17.3 4.6 %collective-permute-start.1 = (f32[80,256]{1,0:T(8,128)S(1)}, f32[80,256]{1,0:T(8,128)S(1)}, u32[]{:S(2)}, u32[]{:S(2)}) collective-permute-start(f32[80,256]{1,0:T(8,128)S(1)} %add.52), channel_id=1, source_target_pairs={{0,8},{4,12},{8,0},{12,4},{16,24},{20,28},{24,16},{28,20},{1,9},{5... | collective-permute-start | bytes 245768 | tf_op jit(solution)/shard_map/ppermute | solution.py:16
  21.8 4.5 %collective-permute-start.2 = (f32[80,256]{1,0:T(8,128)S(1)}, f32[80,256]{1,0:T(8,128)S(1)}, u32[]{:S(2)}, u32[]{:S(2)}) collective-permute-start(f32[80,256]{1,0:T(8,128)S(1)} %add.53), channel_id=1, source_target_pairs={{0,16},{4,20},{8,24},{12,28},{16,0},{20,4},{24,8},{28,12},{1,17},{... | collective-permute-start | bytes 245768 | tf_op jit(solution)/shard_map/ppermute | solution.py:16
  21.9 25.8 %collective-permute-start.5 = (bf16[64,2304]{1,0:T(8,128)(2,1)S(1)}, bf16[64,2304]{1,0:T(8,128)(2,1)S(1)}, u32[]{:S(2)}, u32[]{:S(2)}) collective-permute-start(bf16[64,2304]{1,0:T(8,128)(2,1)S(1)} %get-tuple-element.13.rest_0_), channel_id=1, source_target_pairs={{0,1},{1,0},{2,3},{3,2},{4,5},{5,4},{6,7},{7,6},{8,9},{9,8},{10,11... | collective-permute-start | bytes 884744 | tf_op jit(solution)/shard_map/ppermute | solution.py:16
  23.5 47.1 %collective-permute-start.14 = (bf16[64,2304]{1,0:T(8,128)(2,1)S(1)}, bf16[64,2304]{1,0:T(8,128)(2,1)S(1)}, u32[]{:S(2)}, u32[]{:S(2)}) collective-permute-start(bf16[64,2304]{1,0:T(8,128)(2,1)S(1)} %get-tuple-element.12.rest_0_), channel_id=1, source_target_pairs={{0,2},{1,3},{2,0},{3,1},{4,6},{5,7},{6,4},{7,5},{8,10},{9,11},{10,... | collective-permute-start | bytes 884744 | tf_op jit(solution)/shard_map/ppermute | solution.py:16
  26.4 14.5 %collective-permute-start.3 = (f32[80,256]{1,0:T(8,128)S(1)}, f32[80,256]{1,0:T(8,128)S(1)}, u32[]{:S(2)}, u32[]{:S(2)}) collective-permute-start(f32[80,256]{1,0:T(8,128)S(1)} %add.54), channel_id=1, source_target_pairs={{0,1},{1,0},{2,3},{3,2},{4,5},{5,4},{6,7},{7,6},{8,9},{9,8},{10,11... | collective-permute-start | bytes 245768 | tf_op jit(solution)/shard_map/ppermute | solution.py:16
  27.9 19.9 %copy-start.3 = (bf16[64,2304]{1,0:T(8,128)(2,1)}, bf16[64,2304]{1,0:T(8,128)(2,1)S(1)}, u32[]{:S(2)}) copy-start(bf16[64,2304]{1,0:T(8,128)(2,1)S(1)} %collective-permute-done.6.rest_2_) | copy-start | bytes 884740
  27.9 19.8 %collective-permute-start.7 = (bf16[64,2304]{1,0:T(8,128)(2,1)S(1)}, bf16[64,2304]{1,0:T(8,128)(2,1)S(1)}, u32[]{:S(2)}, u32[]{:S(2)}) collective-permute-start(bf16[64,2304]{1,0:T(8,128)(2,1)S(1)} %collective-permute-done.6.rest_2_), channel_id=1, source_target_pairs={{0,1},{1,0},{2,3},{3,2},{4,5},{5,4},{6,7},{7,6},{8,9},{9,8},{10,11... | collective-permute-start | bytes 884744 | tf_op jit(solution)/shard_map/ppermute | solution.py:16
  40.8 6.3 %collective-permute-start.4 = (f32[80,256]{1,0:T(8,128)S(1)}, f32[80,256]{1,0:T(8,128)S(1)}, u32[]{:S(2)}, u32[]{:S(2)}) collective-permute-start(f32[80,256]{1,0:T(8,128)S(1)} %add.55), channel_id=1, source_target_pairs={{0,2},{1,3},{2,0},{3,1},{4,6},{5,7},{6,4},{7,5},{8,10},{9,11},{10,... | collective-permute-start | bytes 245768 | tf_op jit(solution)/shard_map/ppermute | solution.py:16
  47.8 0.7 copy-start.4
  47.8 0.8 copy-start.7
  68.0 44.3 %copy-start.11 = (f32[1,256]{1,0:T(1,128)S(1)}, f32[1,256]{1,0:T(1,128)}, u32[]{:S(2)}) copy-start(f32[1,256]{1,0:T(1,128)} %get-tuple-element.10) | copy-start | bytes 3076
  68.0 1.6 %collective-permute-start.8 = (f32[80,256]{1,0:T(8,128)}, f32[80,256]{1,0:T(8,128)S(1)}, u32[]{:S(2)}, u32[]{:S(2)}) collective-permute-start(f32[80,256]{1,0:T(8,128)} %get-tuple-element.7), channel_id=1, source_target_pairs={{0,4},{4,0},{8,12},{12,8},{16,20},{20,16},{24,28},{28,24},{1,5},{5... | collective-permute-start | bytes 245768 | tf_op jit(solution)/shard_map/ppermute | solution.py:16
  70.4 4.6 %collective-permute-start.9 = (f32[80,256]{1,0:T(8,128)S(1)}, f32[80,256]{1,0:T(8,128)S(1)}, u32[]{:S(2)}, u32[]{:S(2)}) collective-permute-start(f32[80,256]{1,0:T(8,128)S(1)} %add.57), channel_id=1, source_target_pairs={{0,8},{4,12},{8,0},{12,4},{16,24},{20,28},{24,16},{28,20},{1,9},{5... | collective-permute-start | bytes 245768 | tf_op jit(solution)/shard_map/ppermute | solution.py:16
  70.5 24.2 %collective-permute-start.13 = (bf16[64,2304]{1,0:T(8,128)(2,1)S(1)}, bf16[64,2304]{1,0:T(8,128)(2,1)S(1)}, u32[]{:S(2)}, u32[]{:S(2)}) collective-permute-start(bf16[64,2304]{1,0:T(8,128)(2,1)S(1)} %get-tuple-element.12.rest_0_), channel_id=1, source_target_pairs={{0,1},{1,0},{2,3},{3,2},{4,5},{5,4},{6,7},{7,6},{8,9},{9,8},{10,11... | collective-permute-start | bytes 884744 | tf_op jit(solution)/shard_map/ppermute | solution.py:16
  70.6 24.2 %copy-start.2 = (bf16[64,2304]{1,0:T(8,128)(2,1)}, bf16[64,2304]{1,0:T(8,128)(2,1)S(1)}, u32[]{:S(2)}) copy-start(bf16[64,2304]{1,0:T(8,128)(2,1)S(1)} %collective-permute-done.14.rest_2_) | copy-start | bytes 884740
  70.6 24.1 %collective-permute-start.15 = (bf16[64,2304]{1,0:T(8,128)(2,1)S(1)}, bf16[64,2304]{1,0:T(8,128)(2,1)S(1)}, u32[]{:S(2)}, u32[]{:S(2)}) collective-permute-start(bf16[64,2304]{1,0:T(8,128)(2,1)S(1)} %collective-permute-done.14.rest_2_), channel_id=1, source_target_pairs={{0,1},{1,0},{2,3},{3,2},{4,5},{5,4},{6,7},{7,6},{8,9},{9,8},{10,11... | collective-permute-start | bytes 884744 | tf_op jit(solution)/shard_map/ppermute | solution.py:16
  75.0 4.5 %collective-permute-start.10 = (f32[80,256]{1,0:T(8,128)S(1)}, f32[80,256]{1,0:T(8,128)S(1)}, u32[]{:S(2)}, u32[]{:S(2)}) collective-permute-start(f32[80,256]{1,0:T(8,128)S(1)} %add.58), channel_id=1, source_target_pairs={{0,16},{4,20},{8,24},{12,28},{16,0},{20,4},{24,8},{28,12},{1,17},{... | collective-permute-start | bytes 245768 | tf_op jit(solution)/shard_map/ppermute | solution.py:16
  79.5 8.2 %collective-permute-start.11 = (f32[80,256]{1,0:T(8,128)S(1)}, f32[80,256]{1,0:T(8,128)S(1)}, u32[]{:S(2)}, u32[]{:S(2)}) collective-permute-start(f32[80,256]{1,0:T(8,128)S(1)} %add.59), channel_id=1, source_target_pairs={{0,1},{1,0},{2,3},{3,2},{4,5},{5,4},{6,7},{7,6},{8,9},{9,8},{10,11... | collective-permute-start | bytes 245768 | tf_op jit(solution)/shard_map/ppermute | solution.py:16
  87.7 6.4 %collective-permute-start.12 = (f32[80,256]{1,0:T(8,128)S(1)}, f32[80,256]{1,0:T(8,128)S(1)}, u32[]{:S(2)}, u32[]{:S(2)}) collective-permute-start(f32[80,256]{1,0:T(8,128)S(1)} %add.60), channel_id=1, source_target_pairs={{0,2},{1,3},{2,0},{3,1},{4,6},{5,7},{6,4},{7,5},{8,10},{9,11},{10,... | collective-permute-start | bytes 245768 | tf_op jit(solution)/shard_map/ppermute | solution.py:16
  94.7 0.7 copy-start.5
  94.8 0.8 copy-start.6

commit v2 on v1

v2 whole, which is shorter than its diff:
```python
import functools

import jax
import jax.numpy as jnp
from jax import lax
from jax.experimental import pallas as pl
from jax.experimental.pallas import tpu as pltpu
from jax.sharding import PartitionSpec as P


LANES = 128
CELL_BITS = 16


def swap(value, axis, bit):
    size = lax.axis_size(axis)
    return lax.ppermute(value, axis, [(i, i ^ bit) for i in range(size)])


def rounds_of(axis, first_bit):
    size = lax.axis_size(axis)
    if size & (size - 1):
        raise ValueError("axis size")
    bit = first_bit
    while bit < size:
        if bit * 2 < size:
            yield axis, (bit, bit * 2, bit * 3)
        else:
            yield axis, (bit,)
        bit *= 4


def add_over(keep, send):
    half = keep + swap(send, "slab", 1)
    rounds = list(rounds_of("slab", 2)) + list(rounds_of("lev", 1))
    for axis, distances in rounds:
        half = sum([swap(half, axis, d) for d in distances], half)
    return half, swap(half, "slab", 1)


def rows_over(own, axis):
    size = lax.axis_size(axis)
    shards = {0: own}
    order = sorted(range(1, size), key=lambda p: (bin(p).count("1"), -p))
    for p in order:
        low = p & -p
        shards[p] = swap(shards[p ^ low], axis, low)
    return [shards[p] for p in range(1, size)]


def list_owned(key_ref, list_ref, b):
    def step(o, found):
        list_ref[found] = o
        return found + (key_ref[b, o] >= 0).astype(jnp.int32)

    return lax.fori_loop(0, key_ref.shape[1], step, jnp.int32(0), unroll=8)


def gather_priors(key_ref, frac_ref, list_ref, b, found, source_ref, sum_ref):
    members = sum_ref.shape[0]
    slab_cols = source_ref.shape[2]
    lane = lax.broadcasted_iota(jnp.int32, (members, LANES), 1)
    sum_ref[...] = jnp.zeros(sum_ref.shape, jnp.float32)

    def step(i, carry):
        o = list_ref[i]
        key = key_ref[b, o]
        fraction = frac_ref[b, o]
        row = key >> CELL_BITS
        col = (key & ((1 << CELL_BITS) - 1)) - 1
        first = jnp.maximum(col, 0)
        second = jnp.minimum(col + 1, slab_cols - 1)
        weight_first = jnp.where(col >= 0, 1.0 - fraction, 0.0)
        weight_second = jnp.where(col + 1 < slab_cols, fraction, 0.0)
        slot = o & (LANES - 1)

        def picked(c):
            tile = source_ref[row, :, pl.ds(pl.multiple_of((c >> 7) * LANES, LANES), LANES)]
            return pltpu.roll(tile, (slot - c) & (LANES - 1), 1)

        value = weight_first * picked(first) + weight_second * picked(second)
        where_out = pl.ds(pl.multiple_of((o >> 7) * LANES, LANES), LANES)
        sum_ref[:, where_out] = jnp.where(lane == slot, value, sum_ref[:, where_out])
        return carry

    lax.fori_loop(0, found, step, 0)


def half_of(side, width):
    return pl.ds(pl.multiple_of(side * width, LANES), width)


def split_halves(side, sum_ref, keep_ref, send_ref):
    width = keep_ref.shape[1]
    keep_ref[...] = sum_ref[:, half_of(side, width)]
    send_ref[...] = sum_ref[:, half_of(1 - side, width)]


def load_levels(ens_ref, cur_ref, sems):
    return [
        pltpu.make_async_copy(ens_ref.at[:, l, :], cur_ref.at[l], sems.at[l])
        for l in range(cur_ref.shape[0])
    ]


def prior_kernel(place_ref, key_ref, frac_ref, ens_ref, keep_ref, send_ref, cur_ref, sum_ref, list_ref, sems):
    copies = load_levels(ens_ref, cur_ref, sems)
    for copy in copies:
        copy.start()
    found = list_owned(key_ref, list_ref, 0)
    for copy in copies:
        copy.wait()
    gather_priors(key_ref, frac_ref, list_ref, 0, found, cur_ref, sum_ref)
    split_halves(place_ref[1], sum_ref, keep_ref, send_ref)


def regroup(value, lev_index, groups):
    total = value.shape[1]
    lane = lax.broadcasted_iota(jnp.int32, value.shape, 1)
    bit = 1
    while bit < groups:
        span = (total // groups) * bit
        other = jnp.where(
            (lane & span) != 0, pltpu.roll(value, span, 1), pltpu.roll(value, total - span, 1)
        )
        value = jnp.where((lev_index & bit) != 0, other, value)
        bit *= 2
    return value


def observe(b, groups, place_ref, own_ref, other_ref, value_ref, var_ref, level_ref, mean_ref, work):
    sum_ref, dev_ref, gain_ref, level_b_ref = work
    lev_index, side = place_ref[0], place_ref[1]
    width = own_ref.shape[1]
    sum_ref[:, half_of(side, width)] = own_ref[...]
    sum_ref[:, half_of(1 - side, width)] = other_ref[...]
    prior = sum_ref[...]
    members, n_obs = prior.shape
    lev_rows = level_ref.shape[1]
    variance = var_ref[b : b + 1]
    obs_mean = jnp.sum(prior, axis=0, keepdims=True) / members
    mean_ref[...] = obs_mean
    deviation = prior - obs_mean
    spread = jnp.sum(deviation * deviation, axis=0, keepdims=True) / (members - 1.0)
    total_var = spread + variance
    shrink = 1.0 / (1.0 + jnp.sqrt(variance / total_var))
    gain = ((value_ref[b : b + 1] - obs_mean) - deviation * shrink) / (total_var * (members - 1.0))
    gain_ref[...] = regroup(gain, lev_index, groups).astype(jnp.bfloat16)
    pad = jnp.zeros((LANES - members, n_obs), jnp.float32)
    dev_all = jnp.concatenate([regroup(deviation, lev_index, groups), pad], axis=0)
    dev_ref[...] = dev_all.T[:, :members].astype(jnp.bfloat16)
    level_all = jnp.concatenate(
        [regroup(level_ref[b], lev_index, groups), jnp.zeros((LANES - lev_rows, n_obs), jnp.float32)], axis=0
    ).T
    for l in range(lev_rows):
        level_b_ref[l] = jnp.broadcast_to(level_all[:, l : l + 1], (n_obs, LANES))


def regress(field, shards, l, work):
    _, dev_ref, gain_ref, level_b_ref = work
    members, slab_cols = field.shape
    centred = (field - jnp.sum(field, axis=0, keepdims=True) / members).astype(jnp.bfloat16)
    cross = jnp.dot(dev_ref[...], centred, preferred_element_type=jnp.float32)
    weights = jnp.concatenate([s[...] for s in shards], axis=0)
    level = jnp.concatenate([level_b_ref[l]] * (slab_cols // LANES), axis=1)
    mixed = ((level * weights.astype(jnp.float32)) * cross).astype(jnp.bfloat16)
    return field + jnp.dot(gain_ref[...], mixed, preferred_element_type=jnp.float32)


def first_kernel(groups, place_ref, key_ref, frac_ref, own_ref, other_ref, value_ref, var_ref, level_ref, ens_ref, *rest):
    shards = [rest[0].at[0], *rest[1:groups]]
    cur_out, mean_ref, keep_ref, send_ref, cur_ref, sum_ref, dev_ref, gain_ref, level_b_ref, list_ref, sems = rest[groups:]
    work = (sum_ref, dev_ref, gain_ref, level_b_ref)
    lev_rows = cur_ref.shape[0]
    copies = load_levels(ens_ref, cur_ref, sems)
    for copy in copies:
        copy.start()
    found = list_owned(key_ref, list_ref, 1)
    observe(0, groups, place_ref, own_ref, other_ref, value_ref, var_ref, level_ref, mean_ref, work)
    for l in range(lev_rows):
        copies[l].wait()
        cur_out[l] = regress(cur_ref[l], shards, l, work)
    gather_priors(key_ref, frac_ref, list_ref, 1, found, cur_out, sum_ref)
    split_halves(place_ref[1], sum_ref, keep_ref, send_ref)


def last_kernel(groups, place_ref, own_ref, other_ref, value_ref, var_ref, level_ref, cur_ref, *rest):
    shards = [rest[0].at[1], *rest[1:groups]]
    ens_out, mean_ref, buf_ref, sum_ref, dev_ref, gain_ref, level_b_ref, sems = rest[groups:]
    work = (sum_ref, dev_ref, gain_ref, level_b_ref)
    lev_rows = cur_ref.shape[0]
    observe(1, groups, place_ref, own_ref, other_ref, value_ref, var_ref, level_ref, mean_ref, work)
    copies = []
    for l in range(lev_rows):
        buf_ref[l] = regress(cur_ref[l], shards, l, work)
        copies.append(pltpu.make_async_copy(buf_ref.at[l], ens_out.at[:, l, :], sems.at[l]))
        copies[l].start()
    for copy in copies:
        copy.wait()


def on_device(ensemble, obs_cell, obs_value, obs_var, obs_frac, loc_column, loc_level):
    members, lev_rows, slab_cols = ensemble.shape
    n_blocks, n_obs = obs_cell.shape
    groups = lax.axis_size("lev")
    total_cols = slab_cols * lax.axis_size("slab")
    lev_index = lax.axis_index("lev")
    slab_index = lax.axis_index("slab")

    local_row = obs_cell // total_cols - lev_index * lev_rows
    local_col = (obs_cell % total_cols - slab_index * slab_cols + 1) % total_cols
    owned = (local_row >= 0) & (local_row < lev_rows) & (local_col <= slab_cols)
    keys = jnp.where(owned, (local_row << CELL_BITS) + local_col, -1)
    levels = loc_level.transpose(0, 2, 1)
    place = jnp.stack([lev_index, slab_index & 1]).astype(jnp.int32)

    smem = pl.BlockSpec(memory_space=pltpu.SMEM)
    vmem = pl.BlockSpec(memory_space=pltpu.VMEM)
    hbm = pl.BlockSpec(memory_space=pl.ANY)
    f32 = jnp.float32
    field = jax.ShapeDtypeStruct((lev_rows, members, slab_cols), f32)
    row = jax.ShapeDtypeStruct((1, n_obs), f32)
    half = jax.ShapeDtypeStruct((members, n_obs // 2), f32)
    field_scratch = pltpu.VMEM((lev_rows, members, slab_cols), f32)
    sum_scratch = pltpu.VMEM((members, n_obs), f32)
    work = [
        sum_scratch,
        pltpu.VMEM((n_obs, members), jnp.bfloat16),
        pltpu.VMEM((members, n_obs), jnp.bfloat16),
        pltpu.VMEM((lev_rows, n_obs, LANES), f32),
    ]
    own_list = pltpu.SMEM((n_obs,), jnp.int32)
    dma = pltpu.SemaphoreType.DMA((lev_rows,))

    shards = [rows_over(loc_column[b], "lev") for b in range(n_blocks)]

    keep, send = pl.pallas_call(
        prior_kernel,
        out_shape=(half, half),
        in_specs=[smem, smem, smem, hbm],
        out_specs=(vmem, vmem),
        scratch_shapes=[field_scratch, sum_scratch, own_list, dma],
        name="cells",
    )(place, keys, obs_frac, ensemble)
    own, other = add_over(keep, send)

    current, mean_first, keep, send = pl.pallas_call(
        functools.partial(first_kernel, groups),
        out_shape=(field, row, half, half),
        in_specs=[smem, smem, smem, vmem, vmem, vmem, vmem, vmem, hbm, vmem] + [vmem] * (groups - 1),
        out_specs=(vmem, vmem, vmem, vmem),
        scratch_shapes=[field_scratch] + work + [own_list, dma],
        name="block_first",
    )(place, keys, obs_frac, own, other, obs_value, obs_var, levels, ensemble, loc_column, *shards[0])
    own, other = add_over(keep, send)

    analysis, mean_last = pl.pallas_call(
        functools.partial(last_kernel, groups),
        out_shape=(jax.ShapeDtypeStruct(ensemble.shape, f32), row),
        in_specs=[smem, vmem, vmem, vmem, vmem, vmem, vmem, vmem] + [vmem] * (groups - 1),
        out_specs=(hbm, vmem),
        scratch_shapes=[field_scratch] + work + [dma],
        name="block_last",
    )(place, own, other, obs_value, obs_var, levels, current, loc_column, *shards[1])
    return (analysis, jnp.concatenate([mean_first, mean_last], axis=0))


def solution(mesh):
    in_specs = (
        P(None, "lev", "slab"),
        P(),
        P(),
        P(),
        P(),
        P(None, "lev", "slab"),
        P(None, None, "lev"),
    )
    out_specs = (P(None, "lev", "slab"), P())
    return jax.shard_map(
        on_device, mesh=mesh, in_specs=in_specs, out_specs=out_specs, check_vma=False
    )
```

time: 114 us -> 94.4 us (0.83)
  Pallas kernels: 42.3 us -> 22.7 us
  starting transfers between devices: 12 us -> 25.5 us
  waiting for transfers between devices: 47.4 us -> 38.8 us
  local copies, waits for them, and re-layouts: 5.85 us -> 1.47 us
    pallas_call x3, Pallas kernels: 42.3 us -> 22.7 us  [the longest x1 9.67 us: on_device(): pl.pallas_call(functools.partial(first_kernel, groups), out_shape=(field,...]
    ppermute x16 -> x22, starting transfers between devices: 12 us -> 25.5 us  [swap(): return lax.ppermute(value, axis, [(i, i ^ bit) for i in range(size)])]
    ppermute x16 -> x22, waiting for transfers between devices: 47.4 us -> 38.8 us  [swap(): return lax.ppermute(value, axis, [(i, i ^ bit) for i in range(size)])]
    slice x4 -> x0, local copies, waits for them, and re-layouts: 3.1 us -> none  [the longest x1 1.31 us: on_device(): fracs[0]]
    add x10 -> x6, other arithmetic: 3.14 us -> 1.62 us  [the longest x2 1.57 us: add_over(): half = keep + swap(send, 'slab', 1)]
  transfers between devices with their start and end apart: 16 -> 22, of which waited for: 10 -> 13; matrix products, arithmetic and copies ran while one was open for 6% -> 2% of each run, Pallas kernels for 23% -> 0%
where the time goes in v2:
time: 94.4 us; the launch traced here: 94 us
  waiting for transfers between devices  38.8 us (41%)
  starting transfers between devices  25.5 us (27%)
  Pallas kernels  22.7 us (24%)
  other arithmetic  4.76 us (5%)
  local copies, waits for them, and re-layouts  1.47 us (2%)
    ppermute x22, waiting for transfers between devices, swap(): return lax.ppermute(value, axis, [(i, i ^ bit) for i in range(size)])  38.8 us
    ppermute x22, starting transfers between devices, swap(): return lax.ppermute(value, axis, [(i, i ^ bit) for i in range(size)])  25.5 us
    pallas_call x1, Pallas kernels, on_device(): pl.pallas_call(functools.partial(first_kernel, groups), out_shape=(field,...  9.67 us
    pallas_call x1, Pallas kernels, on_device(): pl.pallas_call(functools.partial(last_kernel, groups), out_shape=(jax.Sha...  6.88 us
    pallas_call x1, Pallas kernels, on_device(): pl.pallas_call(prior_kernel, out_shape=(half, half), in_specs=[smem, smem...  6.18 us
  transfers between devices with their start and end apart: 22, of which 13 were waited for; matrix products, arithmetic and copies ran while one was open for 2% of the time, Pallas kernels for 0%

profile of v2, /device:TPU:0, one launch (start us, length us, event | category | flops | bytes accessed | tf_op | source)
XLA Modules:
  0.0 94.0 jit_solution(7294735769134198592)
XLA Ops:
  1.2 1.3 %and_select_fusion.key_ref = s32[2,256]{1,0:T(2,128)} fusion(s32[2,256]{1,0:T(2,128)} %param.8, s32[]{:T(128)S(6)} %mul.7, s32[]{:T(128)S(6)} %mul.6), kind=kLoop, calls=%fused_computation.6 | loop fusion | flops 14848 | bytes 4104 | tf_op jit(solution)/shard_map/jit(_where)/select_n | solution.py:213
  2.5 6.2 %cells.1 = (f32[80,128]{1,0:T(8,128)}, f32[80,128]{1,0:T(8,128)}) custom-call(s32[2]{0:T(128)} %pad_add_fusion.place_ref, s32[2,256]{1,0:T(2,128)} %and_select_fusion.key_ref, f32[2,256]{1,0:T(2,128)} %frac_ref.3, f32[80,4,2304]{2,1,0:T(4,128)} %ens_ref.3), custom_call_target="tpu_custom_call" | custom-call | tf_op jit(solution)/shard_map/cells/pallas_call | solution.py:237
  8.8 3.9 %collective-permute-start.9 = (bf16[64,2304]{1,0:T(8,128)(2,1)S(1)}, bf16[64,2304]{1,0:T(8,128)(2,1)S(1)}, u32[]{:S(2)}, u32[]{:S(2)}) collective-permute-start(bf16[64,2304]{1,0:T(8,128)(2,1)S(1)} %get-tuple-element.19), channel_id=1, source_target_pairs={{0,2},{1,3},{2,0},{3,1},{4,6},{5,7},{6,4},{7,5},{8,10},{9,11},{10,... | collective-permute-start | bytes 884744 | tf_op jit(solution)/shard_map/ppermute | solution.py:17
  12.8 0.8 add.64
  13.6 1.3 %collective-permute-start.2 = (f32[80,128]{1,0:T(8,128)S(1)}, f32[80,128]{1,0:T(8,128)S(1)}, u32[]{:S(2)}, u32[]{:S(2)}) collective-permute-start(f32[80,128]{1,0:T(8,128)S(1)} %add.64), channel_id=1, source_target_pairs={{0,16},{4,20},{8,24},{12,28},{16,0},{20,4},{24,8},{28,12},{1,17},{... | collective-permute-start | bytes 122888 | tf_op jit(solution)/shard_map/ppermute | solution.py:17
  14.9 2.2 %collective-permute-start.1 = (f32[80,128]{1,0:T(8,128)S(1)}, f32[80,128]{1,0:T(8,128)S(1)}, u32[]{:S(2)}, u32[]{:S(2)}) collective-permute-start(f32[80,128]{1,0:T(8,128)S(1)} %add.64), channel_id=1, source_target_pairs={{0,8},{4,12},{8,0},{12,4},{16,24},{20,28},{24,16},{28,20},{1,9},{5... | collective-permute-start | bytes 122888 | tf_op jit(solution)/shard_map/ppermute | solution.py:17
  17.1 1.5 %collective-permute-done.3 = f32[80,128]{1,0:T(8,128)S(1)} collective-permute-done((f32[80,128]{1,0:T(8,128)S(1)}, f32[80,128]{1,0:T(8,128)S(1)}, u32[]{:S(2)}, u32[]{:S(2)}) %collective-permute-start.3) | collective-permute-done | bytes 40992 | tf_op jit(solution)/shard_map/ppermute | solution.py:17
  19.0 2.6 %collective-permute-start.6 = (f32[80,128]{1,0:T(8,128)S(1)}, f32[80,128]{1,0:T(8,128)S(1)}, u32[]{:S(2)}, u32[]{:S(2)}) collective-permute-start(f32[80,128]{1,0:T(8,128)S(1)} %add_add_fusion.3), channel_id=1, source_target_pairs={{0,3},{1,2},{2,1},{3,0},{4,7},{5,6},{6,5},{7,4},{8,11},{9,10},{10,... | collective-permute-start | bytes 122888 | tf_op jit(solution)/shard_map/ppermute | solution.py:17
  21.6 0.7 collective-permute-start.5
  22.3 1.2 %collective-permute-start.4 = (f32[80,128]{1,0:T(8,128)S(1)}, f32[80,128]{1,0:T(8,128)S(1)}, u32[]{:S(2)}, u32[]{:S(2)}) collective-permute-start(f32[80,128]{1,0:T(8,128)S(1)} %add_add_fusion.3), channel_id=1, source_target_pairs={{0,1},{1,0},{2,3},{3,2},{4,5},{5,4},{6,7},{7,6},{8,9},{9,8},{10,11... | collective-permute-start | bytes 122888 | tf_op jit(solution)/shard_map/ppermute | solution.py:17
  23.5 0.9 collective-permute-start.8
  24.4 4.4 %collective-permute-done.9.rest_2_ = bf16[64,2304]{1,0:T(8,128)(2,1)S(1)} collective-permute-done((bf16[64,2304]{1,0:T(8,128)(2,1)S(1)}, bf16[64,2304]{1,0:T(8,128)(2,1)S(1)}, u32[]{:S(2)}, u32[]{:S(2)}) %collective-permute-start.9) | collective-permute-done | bytes 294944 | tf_op jit(solution)/shard_map/ppermute | solution.py:17
  29.3 1.1 %collective-permute-done.5 = f32[80,128]{1,0:T(8,128)S(1)} collective-permute-done((f32[80,128]{1,0:T(8,128)S(1)}, f32[80,128]{1,0:T(8,128)S(1)}, u32[]{:S(2)}, u32[]{:S(2)}) %collective-permute-start.5) | collective-permute-done | bytes 40992 | tf_op jit(solution)/shard_map/ppermute | solution.py:17
  30.5 1.2 %collective-permute-done.7.other_ref = f32[80,128]{1,0:T(8,128)S(1)} collective-permute-done((f32[80,128]{1,0:T(8,128)S(1)}, f32[80,128]{1,0:T(8,128)S(1)}, u32[]{:S(2)}, u32[]{:S(2)}) %collective-permute-start.7) | collective-permute-done | bytes 40992 | tf_op jit(solution)/shard_map/ppermute | solution.py:17
  31.7 4.9 %collective-permute-done.8.rest_1_ = bf16[64,2304]{1,0:T(8,128)(2,1)S(1)} collective-permute-done((bf16[64,2304]{1,0:T(8,128)(2,1)S(1)}, bf16[64,2304]{1,0:T(8,128)(2,1)S(1)}, u32[]{:S(2)}, u32[]{:S(2)}) %collective-permute-start.8) | collective-permute-done | bytes 294944 | tf_op jit(solution)/shard_map/ppermute | solution.py:17
  36.6 5.7 %collective-permute-done.10.rest_3_ = bf16[64,2304]{1,0:T(8,128)(2,1)S(1)} collective-permute-done((bf16[64,2304]{1,0:T(8,128)(2,1)S(1)}, bf16[64,2304]{1,0:T(8,128)(2,1)S(1)}, u32[]{:S(2)}, u32[]{:S(2)}) %collective-permute-start.10) | collective-permute-done | bytes 294944 | tf_op jit(solution)/shard_map/ppermute | solution.py:17
  42.4 0.7 copy-done.3
  43.1 9.7 %block_first.1 = (f32[4,80,2304]{2,1,0:T(8,128)}, f32[1,256]{1,0:T(1,128)}, f32[80,128]{1,0:T(8,128)}, f32[80,128]{1,0:T(8,128)}) custom-call(s32[2]{0:T(128)} %pad_add_fusion.place_ref, s32[2,256]{1,0:T(2,128)} %and_select_fusion.key_ref, f32[2,256]{1,0:T(2,128)} %frac_ref.3, f32[80,128]{1,0:T(8,128)} %copy-done.7, f32[80,128]{1,0:T(8,128)} %copy-done.9, ...), custom_call_target="tpu_custom_call" | custom-call | tf_op jit(solution)/shard_map/block_first/pallas_call | solution.py:247
  52.9 1.9 %collective-permute-start.20 = (bf16[64,2304]{1,0:T(8,128)(2,1)S(1)}, bf16[64,2304]{1,0:T(8,128)(2,1)S(1)}, u32[]{:S(2)}, u32[]{:S(2)}) collective-permute-start(bf16[64,2304]{1,0:T(8,128)(2,1)S(1)} %get-tuple-element.18), channel_id=1, source_target_pairs={{0,2},{1,3},{2,0},{3,1},{4,6},{5,7},{6,4},{7,5},{8,10},{9,11},{10,... | collective-permute-start | bytes 884744 | tf_op jit(solution)/shard_map/ppermute | solution.py:17
  54.8 0.8 add.71
  55.7 3.4 %collective-permute-start.12 = (f32[80,128]{1,0:T(8,128)S(1)}, f32[80,128]{1,0:T(8,128)S(1)}, u32[]{:S(2)}, u32[]{:S(2)}) collective-permute-start(f32[80,128]{1,0:T(8,128)S(1)} %add.71), channel_id=1, source_target_pairs={{0,8},{4,12},{8,0},{12,4},{16,24},{20,28},{24,16},{28,20},{1,9},{5... | collective-permute-start | bytes 122888 | tf_op jit(solution)/shard_map/ppermute | solution.py:17
  59.1 1.5 %collective-permute-done.14 = f32[80,128]{1,0:T(8,128)S(1)} collective-permute-done((f32[80,128]{1,0:T(8,128)S(1)}, f32[80,128]{1,0:T(8,128)S(1)}, u32[]{:S(2)}, u32[]{:S(2)}) %collective-permute-start.14) | collective-permute-done | bytes 40992 | tf_op jit(solution)/shard_map/ppermute | solution.py:17
  61.1 3.8 %collective-permute-start.17 = (f32[80,128]{1,0:T(8,128)S(1)}, f32[80,128]{1,0:T(8,128)S(1)}, u32[]{:S(2)}, u32[]{:S(2)}) collective-permute-start(f32[80,128]{1,0:T(8,128)S(1)} %add_add_fusion.1), channel_id=1, source_target_pairs={{0,3},{1,2},{2,1},{3,0},{4,7},{5,6},{6,5},{7,4},{8,11},{9,10},{10,... | collective-permute-start | bytes 122888 | tf_op jit(solution)/shard_map/ppermute | solution.py:17
  64.9 0.7 collective-permute-start.16
  65.6 2.0 %collective-permute-start.19 = (bf16[64,2304]{1,0:T(8,128)(2,1)S(1)}, bf16[64,2304]{1,0:T(8,128)(2,1)S(1)}, u32[]{:S(2)}, u32[]{:S(2)}) collective-permute-start(bf16[64,2304]{1,0:T(8,128)(2,1)S(1)} %get-tuple-element.18), channel_id=1, source_target_pairs={{0,1},{1,0},{2,3},{3,2},{4,5},{5,4},{6,7},{7,6},{8,9},{9,8},{10,11... | collective-permute-start | bytes 884744 | tf_op jit(solution)/shard_map/ppermute | solution.py:17
  67.6 4.2 %collective-permute-done.20.rest_2_ = bf16[64,2304]{1,0:T(8,128)(2,1)S(1)} collective-permute-done((bf16[64,2304]{1,0:T(8,128)(2,1)S(1)}, bf16[64,2304]{1,0:T(8,128)(2,1)S(1)}, u32[]{:S(2)}, u32[]{:S(2)}) %collective-permute-start.20) | collective-permute-done | bytes 294944 | tf_op jit(solution)/shard_map/ppermute | solution.py:17
  71.8 1.2 %collective-permute-done.16 = f32[80,128]{1,0:T(8,128)S(1)} collective-permute-done((f32[80,128]{1,0:T(8,128)S(1)}, f32[80,128]{1,0:T(8,128)S(1)}, u32[]{:S(2)}, u32[]{:S(2)}) %collective-permute-start.16) | collective-permute-done | bytes 40992 | tf_op jit(solution)/shard_map/ppermute | solution.py:17
  73.2 6.2 %collective-permute-done.19.rest_1_ = bf16[64,2304]{1,0:T(8,128)(2,1)S(1)} collective-permute-done((bf16[64,2304]{1,0:T(8,128)(2,1)S(1)}, bf16[64,2304]{1,0:T(8,128)(2,1)S(1)}, u32[]{:S(2)}, u32[]{:S(2)}) %collective-permute-start.19) | collective-permute-done | bytes 294944 | tf_op jit(solution)/shard_map/ppermute | solution.py:17
  79.4 5.8 %collective-permute-done.21.rest_3_ = bf16[64,2304]{1,0:T(8,128)(2,1)S(1)} collective-permute-done((bf16[64,2304]{1,0:T(8,128)(2,1)S(1)}, bf16[64,2304]{1,0:T(8,128)(2,1)S(1)}, u32[]{:S(2)}, u32[]{:S(2)}) %collective-permute-start.21) | collective-permute-done | bytes 294944 | tf_op jit(solution)/shard_map/ppermute | solution.py:17
  85.2 0.7 copy-done.6
  85.9 6.9 %block_last.1 = (f32[80,4,2304]{2,1,0:T(4,128)}, f32[1,256]{1,0:T(1,128)}) custom-call(s32[2]{0:T(128)} %pad_add_fusion.place_ref, f32[80,128]{1,0:T(8,128)} %copy-done.8, f32[80,128]{1,0:T(8,128)} %copy-done.10, f32[2,256]{1,0:T(2,128)} %value_ref.3, f32[2,256]{1,0:T(2,128)} %var_ref.3, f32[2,4,256]{2,1,0:T(4,128)} %bitcast.8, ...), custom_call_target="tpu_custom_call" | custom-call | tf_op jit(solution)/shard_map/block_last/pallas_call | solution.py:257
  92.8 1.3 %pad_maximum_fusion = f32[2,256]{1,0:T(2,128)} fusion(f32[1,256]{1,0:T(1,128)} %get-tuple-element.17, f32[1,256]{1,0:T(1,128)S(1)} %copy-done.11), kind=kLoop, calls=%fused_computation.11 | loop fusion | flops 512 | bytes 4096 | tf_op jit(solution)/shard_map/concatenate | solution.py:265
  (49 shorter events, 2.6 us)
Async XLA Ops:
  0.6 8.2 %copy-start = (bf16[2,64,2304]{2,1,0:T(8,128)(2,1)S(1)}, bf16[2,64,2304]{2,1,0:T(8,128)(2,1)}, u32[]{:S(2)}) copy-start(bf16[2,64,2304]{2,1,0:T(8,128)(2,1)} %rest_0_.3) | copy-start | bytes 1769476
  8.7 4.1 %collective-permute-start = (f32[80,128]{1,0:T(8,128)}, f32[80,128]{1,0:T(8,128)S(1)}, u32[]{:S(2)}, u32[]{:S(2)}) collective-permute-start(f32[80,128]{1,0:T(8,128)} %get-tuple-element.11), channel_id=1, source_target_pairs={{0,4},{4,0},{8,12},{12,8},{16,20},{20,16},{24,28},{28,24},{1,5},{5... | collective-permute-start | bytes 122888 | tf_op jit(solution)/shard_map/ppermute | solution.py:17
  8.8 19.9 %collective-permute-start.9 = (bf16[64,2304]{1,0:T(8,128)(2,1)S(1)}, bf16[64,2304]{1,0:T(8,128)(2,1)S(1)}, u32[]{:S(2)}, u32[]{:S(2)}) collective-permute-start(bf16[64,2304]{1,0:T(8,128)(2,1)S(1)} %get-tuple-element.19), channel_id=1, source_target_pairs={{0,2},{1,3},{2,0},{3,1},{4,6},{5,7},{6,4},{7,5},{8,10},{9,11},{10,... | collective-permute-start | bytes 884744 | tf_op jit(solution)/shard_map/ppermute | solution.py:17
  13.6 5.0 %collective-permute-start.3 = (f32[80,128]{1,0:T(8,128)S(1)}, f32[80,128]{1,0:T(8,128)S(1)}, u32[]{:S(2)}, u32[]{:S(2)}) collective-permute-start(f32[80,128]{1,0:T(8,128)S(1)} %add.64), channel_id=1, source_target_pairs={{0,24},{4,28},{8,16},{12,20},{16,8},{20,12},{24,0},{28,4},{1,25},{... | collective-permute-start | bytes 122888 | tf_op jit(solution)/shard_map/ppermute | solution.py:17
  13.6 5.0 %collective-permute-start.2 = (f32[80,128]{1,0:T(8,128)S(1)}, f32[80,128]{1,0:T(8,128)S(1)}, u32[]{:S(2)}, u32[]{:S(2)}) collective-permute-start(f32[80,128]{1,0:T(8,128)S(1)} %add.64), channel_id=1, source_target_pairs={{0,16},{4,20},{8,24},{12,28},{16,0},{20,4},{24,8},{28,12},{1,17},{... | collective-permute-start | bytes 122888 | tf_op jit(solution)/shard_map/ppermute | solution.py:17
  14.9 4.2 %collective-permute-start.1 = (f32[80,128]{1,0:T(8,128)S(1)}, f32[80,128]{1,0:T(8,128)S(1)}, u32[]{:S(2)}, u32[]{:S(2)}) collective-permute-start(f32[80,128]{1,0:T(8,128)S(1)} %add.64), channel_id=1, source_target_pairs={{0,8},{4,12},{8,0},{12,4},{16,24},{20,28},{24,16},{28,20},{1,9},{5... | collective-permute-start | bytes 122888 | tf_op jit(solution)/shard_map/ppermute | solution.py:17
  19.0 10.2 %collective-permute-start.6 = (f32[80,128]{1,0:T(8,128)S(1)}, f32[80,128]{1,0:T(8,128)S(1)}, u32[]{:S(2)}, u32[]{:S(2)}) collective-permute-start(f32[80,128]{1,0:T(8,128)S(1)} %add_add_fusion.3), channel_id=1, source_target_pairs={{0,3},{1,2},{2,1},{3,0},{4,7},{5,6},{6,5},{7,4},{8,11},{9,10},{10,... | collective-permute-start | bytes 122888 | tf_op jit(solution)/shard_map/ppermute | solution.py:17
  21.6 8.8 %collective-permute-start.5 = (f32[80,128]{1,0:T(8,128)S(1)}, f32[80,128]{1,0:T(8,128)S(1)}, u32[]{:S(2)}, u32[]{:S(2)}) collective-permute-start(f32[80,128]{1,0:T(8,128)S(1)} %add_add_fusion.3), channel_id=1, source_target_pairs={{0,2},{1,3},{2,0},{3,1},{4,6},{5,7},{6,4},{7,5},{8,10},{9,11},{10,... | collective-permute-start | bytes 122888 | tf_op jit(solution)/shard_map/ppermute | solution.py:17
  22.3 8.1 %collective-permute-start.4 = (f32[80,128]{1,0:T(8,128)S(1)}, f32[80,128]{1,0:T(8,128)S(1)}, u32[]{:S(2)}, u32[]{:S(2)}) collective-permute-start(f32[80,128]{1,0:T(8,128)S(1)} %add_add_fusion.3), channel_id=1, source_target_pairs={{0,1},{1,0},{2,3},{3,2},{4,5},{5,4},{6,7},{7,6},{8,9},{9,8},{10,11... | collective-permute-start | bytes 122888 | tf_op jit(solution)/shard_map/ppermute | solution.py:17
  23.5 13.1 %collective-permute-start.8 = (bf16[64,2304]{1,0:T(8,128)(2,1)S(1)}, bf16[64,2304]{1,0:T(8,128)(2,1)S(1)}, u32[]{:S(2)}, u32[]{:S(2)}) collective-permute-start(bf16[64,2304]{1,0:T(8,128)(2,1)S(1)} %get-tuple-element.19), channel_id=1, source_target_pairs={{0,1},{1,0},{2,3},{3,2},{4,5},{5,4},{6,7},{7,6},{8,9},{9,8},{10,11... | collective-permute-start | bytes 884744 | tf_op jit(solution)/shard_map/ppermute | solution.py:17
  28.8 13.6 %copy-start.1 = (bf16[64,2304]{1,0:T(8,128)(2,1)}, bf16[64,2304]{1,0:T(8,128)(2,1)S(1)}, u32[]{:S(2)}) copy-start(bf16[64,2304]{1,0:T(8,128)(2,1)S(1)} %collective-permute-done.9.rest_2_) | copy-start | bytes 884740
  28.8 13.6 %collective-permute-start.10 = (bf16[64,2304]{1,0:T(8,128)(2,1)S(1)}, bf16[64,2304]{1,0:T(8,128)(2,1)S(1)}, u32[]{:S(2)}, u32[]{:S(2)}) collective-permute-start(bf16[64,2304]{1,0:T(8,128)(2,1)S(1)} %collective-permute-done.9.rest_2_), channel_id=1, source_target_pairs={{0,1},{1,0},{2,3},{3,2},{4,5},{5,4},{6,7},{7,6},{8,9},{9,8},{10,11... | collective-permute-start | bytes 884744 | tf_op jit(solution)/shard_map/ppermute | solution.py:17
  30.4 11.9 %copy-start.7 = (f32[80,128]{1,0:T(8,128)}, f32[80,128]{1,0:T(8,128)S(1)}, u32[]{:S(2)}) copy-start(f32[80,128]{1,0:T(8,128)S(1)} %add_add_fusion.2.own_ref) | copy-start | bytes 122884
  30.4 1.3 %collective-permute-start.7 = (f32[80,128]{1,0:T(8,128)S(1)}, f32[80,128]{1,0:T(8,128)S(1)}, u32[]{:S(2)}, u32[]{:S(2)}) collective-permute-start(f32[80,128]{1,0:T(8,128)S(1)} %add_add_fusion.2.own_ref), channel_id=1, source_target_pairs={{0,4},{4,0},{8,12},{12,8},{16,20},{20,16},{24,28},{28,24},{1,5},{5... | collective-permute-start | bytes 122888 | tf_op jit(solution)/shard_map/ppermute | solution.py:17
  31.7 10.6 %copy-start.9 = (f32[80,128]{1,0:T(8,128)}, f32[80,128]{1,0:T(8,128)S(1)}, u32[]{:S(2)}) copy-start(f32[80,128]{1,0:T(8,128)S(1)} %collective-permute-done.7.other_ref) | copy-start | bytes 122884
  36.6 5.7 %copy-start.2 = (bf16[64,2304]{1,0:T(8,128)(2,1)}, bf16[64,2304]{1,0:T(8,128)(2,1)S(1)}, u32[]{:S(2)}) copy-start(bf16[64,2304]{1,0:T(8,128)(2,1)S(1)} %collective-permute-done.8.rest_1_) | copy-start | bytes 884740
  42.4 0.7 copy-start.3
  52.8 40.0 %copy-start.11 = (f32[1,256]{1,0:T(1,128)S(1)}, f32[1,256]{1,0:T(1,128)}, u32[]{:S(2)}) copy-start(f32[1,256]{1,0:T(1,128)} %get-tuple-element.16) | copy-start | bytes 3076
  52.8 2.0 %collective-permute-start.11 = (f32[80,128]{1,0:T(8,128)}, f32[80,128]{1,0:T(8,128)S(1)}, u32[]{:S(2)}, u32[]{:S(2)}) collective-permute-start(f32[80,128]{1,0:T(8,128)} %get-tuple-element.13), channel_id=1, source_target_pairs={{0,4},{4,0},{8,12},{12,8},{16,20},{20,16},{24,28},{28,24},{1,5},{5... | collective-permute-start | bytes 122888 | tf_op jit(solution)/shard_map/ppermute | solution.py:17
  52.9 19.0 %collective-permute-start.20 = (bf16[64,2304]{1,0:T(8,128)(2,1)S(1)}, bf16[64,2304]{1,0:T(8,128)(2,1)S(1)}, u32[]{:S(2)}, u32[]{:S(2)}) collective-permute-start(bf16[64,2304]{1,0:T(8,128)(2,1)S(1)} %get-tuple-element.18), channel_id=1, source_target_pairs={{0,2},{1,3},{2,0},{3,1},{4,6},{5,7},{6,4},{7,5},{8,10},{9,11},{10,... | collective-permute-start | bytes 884744 | tf_op jit(solution)/shard_map/ppermute | solution.py:17
  55.6 5.0 %collective-permute-start.14 = (f32[80,128]{1,0:T(8,128)S(1)}, f32[80,128]{1,0:T(8,128)S(1)}, u32[]{:S(2)}, u32[]{:S(2)}) collective-permute-start(f32[80,128]{1,0:T(8,128)S(1)} %add.71), channel_id=1, source_target_pairs={{0,24},{4,28},{8,16},{12,20},{16,8},{20,12},{24,0},{28,4},{1,25},{... | collective-permute-start | bytes 122888 | tf_op jit(solution)/shard_map/ppermute | solution.py:17
  55.6 5.0 %collective-permute-start.13 = (f32[80,128]{1,0:T(8,128)S(1)}, f32[80,128]{1,0:T(8,128)S(1)}, u32[]{:S(2)}, u32[]{:S(2)}) collective-permute-start(f32[80,128]{1,0:T(8,128)S(1)} %add.71), channel_id=1, source_target_pairs={{0,16},{4,20},{8,24},{12,28},{16,0},{20,4},{24,8},{28,12},{1,17},{... | collective-permute-start | bytes 122888 | tf_op jit(solution)/shard_map/ppermute | solution.py:17
  55.7 5.4 %collective-permute-start.12 = (f32[80,128]{1,0:T(8,128)S(1)}, f32[80,128]{1,0:T(8,128)S(1)}, u32[]{:S(2)}, u32[]{:S(2)}) collective-permute-start(f32[80,128]{1,0:T(8,128)S(1)} %add.71), channel_id=1, source_target_pairs={{0,8},{4,12},{8,0},{12,4},{16,24},{20,28},{24,16},{28,20},{1,9},{5... | collective-permute-start | bytes 122888 | tf_op jit(solution)/shard_map/ppermute | solution.py:17
  61.1 10.8 %collective-permute-start.17 = (f32[80,128]{1,0:T(8,128)S(1)}, f32[80,128]{1,0:T(8,128)S(1)}, u32[]{:S(2)}, u32[]{:S(2)}) collective-permute-start(f32[80,128]{1,0:T(8,128)S(1)} %add_add_fusion.1), channel_id=1, source_target_pairs={{0,3},{1,2},{2,1},{3,0},{4,7},{5,6},{6,5},{7,4},{8,11},{9,10},{10,... | collective-permute-start | bytes 122888 | tf_op jit(solution)/shard_map/ppermute | solution.py:17
  64.9 8.2 %collective-permute-start.16 = (f32[80,128]{1,0:T(8,128)S(1)}, f32[80,128]{1,0:T(8,128)S(1)}, u32[]{:S(2)}, u32[]{:S(2)}) collective-permute-start(f32[80,128]{1,0:T(8,128)S(1)} %add_add_fusion.1), channel_id=1, source_target_pairs={{0,2},{1,3},{2,0},{3,1},{4,6},{5,7},{6,4},{7,5},{8,10},{9,11},{10,... | collective-permute-start | bytes 122888 | tf_op jit(solution)/shard_map/ppermute | solution.py:17
  65.6 7.5 %collective-permute-start.15 = (f32[80,128]{1,0:T(8,128)S(1)}, f32[80,128]{1,0:T(8,128)S(1)}, u32[]{:S(2)}, u32[]{:S(2)}) collective-permute-start(f32[80,128]{1,0:T(8,128)S(1)} %add_add_fusion.1), channel_id=1, source_target_pairs={{0,1},{1,0},{2,3},{3,2},{4,5},{5,4},{6,7},{7,6},{8,9},{9,8},{10,11... | collective-permute-start | bytes 122888 | tf_op jit(solution)/shard_map/ppermute | solution.py:17
  65.6 13.8 %collective-permute-start.19 = (bf16[64,2304]{1,0:T(8,128)(2,1)S(1)}, bf16[64,2304]{1,0:T(8,128)(2,1)S(1)}, u32[]{:S(2)}, u32[]{:S(2)}) collective-permute-start(bf16[64,2304]{1,0:T(8,128)(2,1)S(1)} %get-tuple-element.18), channel_id=1, source_target_pairs={{0,1},{1,0},{2,3},{3,2},{4,5},{5,4},{6,7},{7,6},{8,9},{9,8},{10,11... | collective-permute-start | bytes 884744 | tf_op jit(solution)/shard_map/ppermute | solution.py:17
  71.8 13.3 %copy-start.4 = (bf16[64,2304]{1,0:T(8,128)(2,1)}, bf16[64,2304]{1,0:T(8,128)(2,1)S(1)}, u32[]{:S(2)}) copy-start(bf16[64,2304]{1,0:T(8,128)(2,1)S(1)} %collective-permute-done.20.rest_2_) | copy-start | bytes 884740
  71.8 13.3 %collective-permute-start.21 = (bf16[64,2304]{1,0:T(8,128)(2,1)S(1)}, bf16[64,2304]{1,0:T(8,128)(2,1)S(1)}, u32[]{:S(2)}, u32[]{:S(2)}) collective-permute-start(bf16[64,2304]{1,0:T(8,128)(2,1)S(1)} %collective-permute-done.20.rest_2_), channel_id=1, source_target_pairs={{0,1},{1,0},{2,3},{3,2},{4,5},{5,4},{6,7},{7,6},{8,9},{9,8},{10,11... | collective-permute-start | bytes 884744 | tf_op jit(solution)/shard_map/ppermute | solution.py:17
  73.1 12.1 %copy-start.8 = (f32[80,128]{1,0:T(8,128)}, f32[80,128]{1,0:T(8,128)S(1)}, u32[]{:S(2)}) copy-start(f32[80,128]{1,0:T(8,128)S(1)} %add_add_fusion.own_ref) | copy-start | bytes 122884
  73.1 12.1 %collective-permute-start.18 = (f32[80,128]{1,0:T(8,128)S(1)}, f32[80,128]{1,0:T(8,128)S(1)}, u32[]{:S(2)}, u32[]{:S(2)}) collective-permute-start(f32[80,128]{1,0:T(8,128)S(1)} %add_add_fusion.own_ref), channel_id=1, source_target_pairs={{0,4},{4,0},{8,12},{12,8},{16,20},{20,16},{24,28},{28,24},{1,5},{5... | collective-permute-start | bytes 122888 | tf_op jit(solution)/shard_map/ppermute | solution.py:17
  79.4 5.8 %copy-start.5 = (bf16[64,2304]{1,0:T(8,128)(2,1)}, bf16[64,2304]{1,0:T(8,128)(2,1)S(1)}, u32[]{:S(2)}) copy-start(bf16[64,2304]{1,0:T(8,128)(2,1)S(1)} %collective-permute-done.19.rest_1_) | copy-start | bytes 884740
  (2 other events, 1.4 us)

commit v3 on v2

v3 whole, which is shorter than its diff:
```python
import functools

import jax
import jax.numpy as jnp
from jax import lax
from jax.experimental import pallas as pl
from jax.experimental.pallas import tpu as pltpu
from jax.sharding import PartitionSpec as P


LANES = 128
CELL_BITS = 16
BATCH = 4


def swap(value, axis, bit):
    size = lax.axis_size(axis)
    return lax.ppermute(value, axis, [(i, i ^ bit) for i in range(size)])


def rounds_of(axis, first_bit):
    size = lax.axis_size(axis)
    if size & (size - 1):
        raise ValueError("axis size")
    bit = first_bit
    while bit < size:
        if bit * 2 < size:
            yield axis, (bit, bit * 2, bit * 3)
        else:
            yield axis, (bit,)
        bit *= 4


def add_over(keep, send):
    half = keep + swap(send, "slab", 1)
    rounds = list(rounds_of("slab", 2)) + list(rounds_of("lev", 1))
    for axis, distances in rounds:
        half = sum([swap(half, axis, d) for d in distances], half)
    return half, swap(half, "slab", 1)


def rows_over(own, axis):
    size = lax.axis_size(axis)
    shards = {0: own}
    order = sorted(range(1, size), key=lambda p: (bin(p).count("1"), -p))
    for p in order:
        low = p & -p
        shards[p] = swap(shards[p ^ low], axis, low)
    return [shards[p] for p in range(1, size)]


def key_copy(place_ref, cell_ref, key_ref, key_smem, sem, sizes):
    lev_rows, slab_cols, total_cols = sizes
    lev_index, slab_index = place_ref[0], place_ref[1]
    cell = cell_ref[...]
    edge = slab_index == 0
    lowest = jnp.where(edge, 1, 0)
    key = jnp.full(cell.shape, -1, jnp.int32)
    for r in range(lev_rows):
        col = cell - ((lev_index * lev_rows + r) * total_cols + slab_index * slab_cols - 1)
        key = jnp.where((col >= lowest) & (col <= slab_cols), col + (r << CELL_BITS), key)
        key = jnp.where((col == total_cols) & edge, r << CELL_BITS, key)
    key_ref[...] = key
    return pltpu.make_async_copy(key_ref, key_smem, sem)


def list_owned(key_ref, list_ref, b):
    def step(o, found):
        list_ref[found] = o
        return found + (key_ref[b, o] >= 0).astype(jnp.int32)

    found = lax.fori_loop(0, key_ref.shape[1], step, jnp.int32(0), unroll=16)
    for extra in range(BATCH - 1):
        list_ref[found + extra] = 0
    return found


def gather_priors(key_ref, frac_ref, list_ref, b, found, source_ref, sum_ref):
    members = sum_ref.shape[0]
    slab_cols = source_ref.shape[2]
    lane = lax.broadcasted_iota(jnp.int32, (members, LANES), 1)
    sum_ref[...] = jnp.zeros(sum_ref.shape, jnp.float32)

    def value_of(i):
        o = list_ref[i]
        key = key_ref[b, o]
        fraction = frac_ref[b, o]
        row = jnp.maximum(key, 0) >> CELL_BITS
        col = (jnp.maximum(key, 0) & ((1 << CELL_BITS) - 1)) - 1
        first = jnp.maximum(col, 0)
        second = jnp.minimum(col + 1, slab_cols - 1)
        real = i < found
        weight_first = jnp.where(real & (col >= 0), 1.0 - fraction, 0.0)
        weight_second = jnp.where(real & (col + 1 < slab_cols), fraction, 0.0)
        slot = o & (LANES - 1)

        def picked(c):
            tile = source_ref[row, :, pl.ds(pl.multiple_of((c >> 7) * LANES, LANES), LANES)]
            return pltpu.roll(tile, (slot - c) & (LANES - 1), 1)

        value = weight_first * picked(first) + weight_second * picked(second)
        return (o >> 7) * LANES, jnp.where(lane == slot, value, 0.0)

    def step(i, carry):
        batch = [value_of(i * BATCH + k) for k in range(BATCH)]
        for start, value in batch:
            where_out = pl.ds(pl.multiple_of(start, LANES), LANES)
            sum_ref[:, where_out] = sum_ref[:, where_out] + value
        return carry

    lax.fori_loop(0, (found + BATCH - 1) // BATCH, step, 0)


def half_of(side, width):
    return pl.ds(pl.multiple_of(side * width, LANES), width)


def split_halves(side, sum_ref, keep_ref, send_ref):
    width = keep_ref.shape[1]
    keep_ref[...] = sum_ref[:, half_of(side, width)]
    send_ref[...] = sum_ref[:, half_of(1 - side, width)]


def load_levels(ens_ref, cur_ref, sems):
    return [
        pltpu.make_async_copy(ens_ref.at[:, l, :], cur_ref.at[l], sems.at[l])
        for l in range(cur_ref.shape[0])
    ]


def prior_kernel(sizes, place_ref, frac_ref, cell_ref, ens_ref, keep_ref, send_ref, cur_ref, sum_ref, key_ref, key_smem, list_ref, sems, key_sem):
    copies = load_levels(ens_ref, cur_ref, sems)
    for copy in copies:
        copy.start()
    keys = key_copy(place_ref, cell_ref, key_ref, key_smem, key_sem, sizes)
    keys.start()
    keys.wait()
    found = list_owned(key_smem, list_ref, 0)
    for copy in copies:
        copy.wait()
    gather_priors(key_smem, frac_ref, list_ref, 0, found, cur_ref, sum_ref)
    split_halves(place_ref[1] & 1, sum_ref, keep_ref, send_ref)


def regroup(value, lev_index, groups):
    total = value.shape[1]
    lane = lax.broadcasted_iota(jnp.int32, value.shape, 1)
    bit = 1
    while bit < groups:
        span = (total // groups) * bit
        other = jnp.where(
            (lane & span) != 0, pltpu.roll(value, span, 1), pltpu.roll(value, total - span, 1)
        )
        value = jnp.where((lev_index & bit) != 0, other, value)
        bit *= 2
    return value


def observe(b, groups, place_ref, own_ref, other_ref, value_ref, var_ref, level_ref, work):
    sum_ref, dev_ref, gain_ref, level_b_ref = work
    lev_index, side = place_ref[0], place_ref[1] & 1
    width = own_ref.shape[1]
    sum_ref[:, half_of(side, width)] = own_ref[...]
    sum_ref[:, half_of(1 - side, width)] = other_ref[...]
    prior = sum_ref[...]
    members, n_obs = prior.shape
    lev_rows = level_ref.shape[1]
    variance = var_ref[b : b + 1]
    obs_mean = jnp.sum(prior, axis=0, keepdims=True) / members
    deviation = prior - obs_mean
    spread = jnp.sum(deviation * deviation, axis=0, keepdims=True) / (members - 1.0)
    total_var = spread + variance
    shrink = 1.0 / (1.0 + jnp.sqrt(variance / total_var))
    gain = ((value_ref[b : b + 1] - obs_mean) - deviation * shrink) / (total_var * (members - 1.0))
    gain_ref[...] = regroup(gain, lev_index, groups).astype(jnp.bfloat16)
    pad = jnp.zeros((LANES - members, n_obs), jnp.float32)
    dev_all = jnp.concatenate([regroup(deviation, lev_index, groups), pad], axis=0)
    dev_ref[...] = dev_all.T[:, :members].astype(jnp.bfloat16)
    level_all = jnp.concatenate(
        [regroup(level_ref[b], lev_index, groups), jnp.zeros((LANES - lev_rows, n_obs), jnp.float32)], axis=0
    ).T
    for l in range(lev_rows):
        level_b_ref[l] = jnp.broadcast_to(level_all[:, l : l + 1], (n_obs, LANES))
    return obs_mean


def regress(field, rows_ref, l, work):
    _, dev_ref, gain_ref, level_b_ref = work
    members, slab_cols = field.shape
    centred = (field - jnp.sum(field, axis=0, keepdims=True) / members).astype(jnp.bfloat16)
    cross = jnp.dot(dev_ref[...], centred, preferred_element_type=jnp.float32)
    level = jnp.concatenate([level_b_ref[l]] * (slab_cols // LANES), axis=1)
    mixed = ((level * rows_ref[...].astype(jnp.float32)) * cross).astype(jnp.bfloat16)
    return field + jnp.dot(gain_ref[...], mixed, preferred_element_type=jnp.float32)


def load_rows(b, shards, rows_ref, sems):
    own, *rest = shards
    count = own.shape[1]
    return [
        pltpu.make_async_copy(own.at[b] if p == 0 else rest[p - 1], rows_ref.at[pl.ds(p * count, count)], sems.at[p])
        for p in range(len(shards))
    ]


def first_kernel(groups, sizes, place_ref, frac_ref, cell_ref, own_ref, other_ref, value_ref, var_ref, level_ref, ens_ref, *rest):
    shards = rest[:groups]
    cur_out, mean_ref, keep_ref, send_ref, cur_ref, rows_ref, *work, key_ref, key_smem, list_ref, sems, row_sems, key_sem = rest[groups:]
    lev_rows = cur_ref.shape[0]
    keys = key_copy(place_ref, cell_ref, key_ref, key_smem, key_sem, sizes)
    keys.start()
    copies = load_levels(ens_ref, cur_ref, sems)
    rows = load_rows(0, shards, rows_ref, row_sems)
    for copy in copies[:1] + rows + copies[1:]:
        copy.start()
    mean_ref[...] = observe(0, groups, place_ref, own_ref, other_ref, value_ref, var_ref, level_ref, work)
    keys.wait()
    found = list_owned(key_smem, list_ref, 1)
    for copy in rows:
        copy.wait()
    for l in range(lev_rows):
        copies[l].wait()
        cur_out[l] = regress(cur_ref[l], rows_ref, l, work)
    gather_priors(key_smem, frac_ref, list_ref, 1, found, cur_out, work[0])
    split_halves(place_ref[1] & 1, work[0], keep_ref, send_ref)


def last_kernel(groups, place_ref, own_ref, other_ref, value_ref, var_ref, level_ref, mean_in, cur_in, *rest):
    shards = rest[:groups]
    ens_out, mean_ref, cur_ref, rows_ref, buf_ref, *work, sems, row_sems = rest[groups:]
    lev_rows = cur_ref.shape[0]
    copies = [pltpu.make_async_copy(cur_in.at[l], cur_ref.at[l], sems.at[l]) for l in range(lev_rows)]
    rows = load_rows(1, shards, rows_ref, row_sems)
    for copy in copies[:1] + rows + copies[1:]:
        copy.start()
    mean_ref[0:1] = mean_in[...]
    mean_ref[1:2] = observe(1, groups, place_ref, own_ref, other_ref, value_ref, var_ref, level_ref, work)
    for copy in rows:
        copy.wait()
    stores = []
    for l in range(lev_rows):
        copies[l].wait()
        buf_ref[l] = regress(cur_ref[l], rows_ref, l, work)
        stores.append(pltpu.make_async_copy(buf_ref.at[l], ens_out.at[:, l, :], sems.at[l]))
        stores[l].start()
    for store in stores:
        store.wait()


def with_place(kernel):
    def run(lev_ref, slab_ref, *refs):
        kernel((lev_ref[0], slab_ref[0]), *refs)

    return run


def on_device(ensemble, obs_cell, obs_value, obs_var, obs_frac, loc_column, loc_level):
    members, lev_rows, slab_cols = ensemble.shape
    n_blocks, n_obs = obs_cell.shape
    groups = lax.axis_size("lev")
    sizes = (lev_rows, slab_cols, slab_cols * lax.axis_size("slab"))
    place = [lax.axis_index(axis).reshape(1).astype(jnp.int32) for axis in ("lev", "slab")]
    levels = loc_level.transpose(0, 2, 1)

    smem = pl.BlockSpec(memory_space=pltpu.SMEM)
    vmem = pl.BlockSpec(memory_space=pltpu.VMEM)
    hbm = pl.BlockSpec(memory_space=pl.ANY)
    f32 = jnp.float32
    field = jax.ShapeDtypeStruct((lev_rows, members, slab_cols), f32)
    row = jax.ShapeDtypeStruct((1, n_obs), f32)
    half = jax.ShapeDtypeStruct((members, n_obs // 2), f32)
    field_scratch = pltpu.VMEM((lev_rows, members, slab_cols), f32)
    rows_scratch = pltpu.VMEM((n_obs, slab_cols), jnp.bfloat16)
    sum_scratch = pltpu.VMEM((members, n_obs), f32)
    work = [
        sum_scratch,
        pltpu.VMEM((n_obs, members), jnp.bfloat16),
        pltpu.VMEM((members, n_obs), jnp.bfloat16),
        pltpu.VMEM((lev_rows, n_obs, LANES), f32),
    ]
    own = [
        pltpu.VMEM((n_blocks, n_obs), jnp.int32),
        pltpu.SMEM((n_blocks, n_obs), jnp.int32),
        pltpu.SMEM((n_obs + BATCH,), jnp.int32),
    ]
    dma = pltpu.SemaphoreType.DMA((lev_rows,))
    row_dma = pltpu.SemaphoreType.DMA((groups,))
    one_dma = pltpu.SemaphoreType.DMA

    shards = [rows_over(loc_column[0], "lev")]

    keep, send = pl.pallas_call(
        with_place(functools.partial(prior_kernel, sizes)),
        out_shape=(half, half),
        in_specs=[smem, smem, smem, vmem, hbm],
        out_specs=(vmem, vmem),
        scratch_shapes=[field_scratch, sum_scratch] + own + [dma, one_dma],
        name="cells",
    )(*place, obs_frac, obs_cell, ensemble)
    later_rows, keep = lax.optimization_barrier((loc_column, keep))
    shards.append(rows_over(later_rows[1], "lev"))
    ours, theirs = add_over(keep, send)

    current, mean_first, keep, send = pl.pallas_call(
        with_place(functools.partial(first_kernel, groups, sizes)),
        out_shape=(field, row, half, half),
        in_specs=[smem, smem, smem] + [vmem] * 6 + [hbm] * (1 + groups),
        out_specs=(vmem, vmem, vmem, vmem),
        scratch_shapes=[field_scratch, rows_scratch] + work + own + [dma, row_dma, one_dma],
        name="block_first",
    )(*place, obs_frac, obs_cell, ours, theirs, obs_value, obs_var, levels, ensemble, loc_column, *shards[0])
    ours, theirs = add_over(keep, send)

    analysis, mean = pl.pallas_call(
        with_place(functools.partial(last_kernel, groups)),
        out_shape=(jax.ShapeDtypeStruct(ensemble.shape, f32), jax.ShapeDtypeStruct((n_blocks, n_obs), f32)),
        in_specs=[smem, smem] + [vmem] * 6 + [hbm] * (1 + groups),
        out_specs=(hbm, vmem),
        scratch_shapes=[field_scratch, rows_scratch, field_scratch] + work + [dma, row_dma],
        name="block_last",
    )(*place, ours, theirs, obs_value, obs_var, levels, mean_first, current, loc_column, *shards[1])
    return (analysis, mean)


def solution(mesh):
    in_specs = (
        P(None, "lev", "slab"),
        P(),
        P(),
        P(),
        P(),
        P(None, "lev", "slab"),
        P(None, None, "lev"),
    )
    out_specs = (P(None, "lev", "slab"), P())
    return jax.shard_map(
        on_device, mesh=mesh, in_specs=in_specs, out_specs=out_specs, check_vma=False
    )
```

time: 94.4 us -> 88.2 us (0.934)
  Pallas kernels: 22.7 us -> 19.4 us
  other arithmetic: 4.76 us -> 1.62 us
    pallas_call x3, Pallas kernels: 22.7 us -> 19.4 us  [the longest x1 7.77 us: on_device(): pl.pallas_call(with_place(functools.partial(first_kernel, groups, sizes))...]
    select_n x1 -> x0, other arithmetic: 1.29 us -> none  [on_device(): keys = jnp.where(owned, (local_row << CELL_BITS) + local_col, -1)]
    concatenate x1 -> x0, other arithmetic: 1.27 us -> none  [on_device(): return (analysis, jnp.concatenate([mean_first, mean_last], axis=0))]
    ppermute x22, waiting for transfers between devices: 38.8 us -> 39.7 us  [swap(): return lax.ppermute(value, axis, [(i, i ^ bit) for i in range(size)])]
  transfers between devices with their start and end apart: 22 -> 22, of which waited for: 13 -> 14; matrix products, arithmetic and copies ran while one was open for 2% -> 2% of each run, Pallas kernels for 0% -> 0%
where the time goes in v3:
time: 88.2 us; the launch traced here: 87.7 us
  waiting for transfers between devices  39.7 us (45%)
  starting transfers between devices  24.7 us (28%)
  Pallas kernels  19.4 us (22%)
  other arithmetic  1.62 us (2%)
  local copies, waits for them, and re-layouts  1.47 us (2%)
    ppermute x22, waiting for transfers between devices, swap(): return lax.ppermute(value, axis, [(i, i ^ bit) for i in range(size)])  39.7 us
    ppermute x22, starting transfers between devices, swap(): return lax.ppermute(value, axis, [(i, i ^ bit) for i in range(size)])  24.7 us
    pallas_call x1, Pallas kernels, on_device(): pl.pallas_call(with_place(functools.partial(first_kernel, groups, sizes))...  7.77 us
    pallas_call x1, Pallas kernels, on_device(): pl.pallas_call(with_place(functools.partial(last_kernel, groups)), out_sh...  6.95 us
    pallas_call x1, Pallas kernels, on_device(): pl.pallas_call(with_place(functools.partial(prior_kernel, sizes)), out_sh...  4.7 us
  transfers between devices with their start and end apart: 22, of which 14 were waited for; matrix products, arithmetic and copies ran while one was open for 2% of the time, Pallas kernels for 0%

profile of v3, /device:TPU:0, one launch (start us, length us, event | category | flops | bytes accessed | tf_op | source)
XLA Modules:
  0.0 87.7 jit_solution(15986935683107307166)
XLA Ops:
  0.6 4.7 %cells.1 = (f32[80,128]{1,0:T(8,128)}, f32[80,128]{1,0:T(8,128)}) custom-call(s32[1]{0:T(128)} %bitcast.lev_ref, s32[1]{0:T(128)} %bitcast.1.slab_ref, f32[2,256]{1,0:T(2,128)} %refs_0_.3, s32[2,256]{1,0:T(2,128)} %refs_1_.3, f32[80,4,2304]{2,1,0:T(4,128)} %refs_7_.2), custom_call_target="tpu_custom_call" | custom-call | tf_op jit(solution)/shard_map/cells/pallas_call | solution.py:292
  5.5 4.0 %collective-permute-start.9 = (bf16[64,2304]{1,0:T(8,128)(2,1)S(1)}, bf16[64,2304]{1,0:T(8,128)(2,1)S(1)}, u32[]{:S(2)}, u32[]{:S(2)}) collective-permute-start(bf16[64,2304]{1,0:T(8,128)(2,1)S(1)} %slice_bitcast_fusion.1), channel_id=1, source_target_pairs={{0,2},{1,3},{2,0},{3,1},{4,6},{5,7},{6,4},{7,5},{8,10},{9,11},{10,... | collective-permute-start | bytes 884744 | tf_op jit(solution)/shard_map/ppermute | solution.py:18
  9.4 0.8 add.42
  10.2 1.4 %collective-permute-start.3 = (f32[80,128]{1,0:T(8,128)S(1)}, f32[80,128]{1,0:T(8,128)S(1)}, u32[]{:S(2)}, u32[]{:S(2)}) collective-permute-start(f32[80,128]{1,0:T(8,128)S(1)} %add.42), channel_id=1, source_target_pairs={{0,24},{4,28},{8,16},{12,20},{16,8},{20,12},{24,0},{28,4},{1,25},{... | collective-permute-start | bytes 122888 | tf_op jit(solution)/shard_map/ppermute | solution.py:18
  11.7 0.8 collective-permute-start.2
  12.5 1.2 %collective-permute-start.1 = (f32[80,128]{1,0:T(8,128)S(1)}, f32[80,128]{1,0:T(8,128)S(1)}, u32[]{:S(2)}, u32[]{:S(2)}) collective-permute-start(f32[80,128]{1,0:T(8,128)S(1)} %add.42), channel_id=1, source_target_pairs={{0,8},{4,12},{8,0},{12,4},{16,24},{20,28},{24,16},{28,20},{1,9},{5... | collective-permute-start | bytes 122888 | tf_op jit(solution)/shard_map/ppermute | solution.py:18
  13.7 1.4 %collective-permute-done.3 = f32[80,128]{1,0:T(8,128)S(1)} collective-permute-done((f32[80,128]{1,0:T(8,128)S(1)}, f32[80,128]{1,0:T(8,128)S(1)}, u32[]{:S(2)}, u32[]{:S(2)}) %collective-permute-start.3) | collective-permute-done | bytes 40992 | tf_op jit(solution)/shard_map/ppermute | solution.py:18
  15.7 0.8 collective-permute-done.1
  16.5 2.4 %collective-permute-start.6 = (f32[80,128]{1,0:T(8,128)S(1)}, f32[80,128]{1,0:T(8,128)S(1)}, u32[]{:S(2)}, u32[]{:S(2)}) collective-permute-start(f32[80,128]{1,0:T(8,128)S(1)} %add_add_fusion.3), channel_id=1, source_target_pairs={{0,3},{1,2},{2,1},{3,0},{4,7},{5,6},{6,5},{7,4},{8,11},{9,10},{10,... | collective-permute-start | bytes 122888 | tf_op jit(solution)/shard_map/ppermute | solution.py:18
  18.9 0.7 collective-permute-start.5
  19.6 1.3 %collective-permute-start.4 = (f32[80,128]{1,0:T(8,128)S(1)}, f32[80,128]{1,0:T(8,128)S(1)}, u32[]{:S(2)}, u32[]{:S(2)}) collective-permute-start(f32[80,128]{1,0:T(8,128)S(1)} %add_add_fusion.3), channel_id=1, source_target_pairs={{0,1},{1,0},{2,3},{3,2},{4,5},{5,4},{6,7},{7,6},{8,9},{9,8},{10,11... | collective-permute-start | bytes 122888 | tf_op jit(solution)/shard_map/ppermute | solution.py:18
  21.0 0.7 collective-permute-start.8
  21.7 3.8 %collective-permute-done.9.refs_10_ = bf16[64,2304]{1,0:T(8,128)(2,1)S(1)} collective-permute-done((bf16[64,2304]{1,0:T(8,128)(2,1)S(1)}, bf16[64,2304]{1,0:T(8,128)(2,1)S(1)}, u32[]{:S(2)}, u32[]{:S(2)}) %collective-permute-start.9) | collective-permute-done | bytes 294944 | tf_op jit(solution)/shard_map/ppermute | solution.py:18
  25.9 1.1 %collective-permute-done.5 = f32[80,128]{1,0:T(8,128)S(1)} collective-permute-done((f32[80,128]{1,0:T(8,128)S(1)}, f32[80,128]{1,0:T(8,128)S(1)}, u32[]{:S(2)}, u32[]{:S(2)}) %collective-permute-start.5) | collective-permute-done | bytes 40992 | tf_op jit(solution)/shard_map/ppermute | solution.py:18
  27.2 1.2 %collective-permute-done.7.refs_3_ = f32[80,128]{1,0:T(8,128)S(1)} collective-permute-done((f32[80,128]{1,0:T(8,128)S(1)}, f32[80,128]{1,0:T(8,128)S(1)}, u32[]{:S(2)}, u32[]{:S(2)}) %collective-permute-start.7) | collective-permute-done | bytes 40992 | tf_op jit(solution)/shard_map/ppermute | solution.py:18
  28.4 4.8 %collective-permute-done.8.refs_9_ = bf16[64,2304]{1,0:T(8,128)(2,1)S(1)} collective-permute-done((bf16[64,2304]{1,0:T(8,128)(2,1)S(1)}, bf16[64,2304]{1,0:T(8,128)(2,1)S(1)}, u32[]{:S(2)}, u32[]{:S(2)}) %collective-permute-start.8) | collective-permute-done | bytes 294944 | tf_op jit(solution)/shard_map/ppermute | solution.py:18
  33.2 5.9 %collective-permute-done.10.refs_11_ = bf16[64,2304]{1,0:T(8,128)(2,1)S(1)} collective-permute-done((bf16[64,2304]{1,0:T(8,128)(2,1)S(1)}, bf16[64,2304]{1,0:T(8,128)(2,1)S(1)}, u32[]{:S(2)}, u32[]{:S(2)}) %collective-permute-start.10) | collective-permute-done | bytes 294944 | tf_op jit(solution)/shard_map/ppermute | solution.py:18
  39.1 0.7 copy-done.7
  39.8 7.8 %block_first.1 = (f32[4,80,2304]{2,1,0:T(8,128)}, f32[1,256]{1,0:T(1,128)}, f32[80,128]{1,0:T(8,128)}, f32[80,128]{1,0:T(8,128)}) custom-call(s32[1]{0:T(128)} %bitcast.lev_ref, s32[1]{0:T(128)} %bitcast.1.slab_ref, f32[2,256]{1,0:T(2,128)} %refs_0_.3, s32[2,256]{1,0:T(2,128)} %refs_1_.3, f32[80,128]{1,0:T(8,128)} %copy-done.9, f32[80,128]{1,0:T(8,128)} %copy-done.11, ...), custom_call_target="tpu_custom_call" | custom-call | tf_op jit(solution)/shard_map/block_first/pallas_call | solution.py:304
  47.7 1.6 %collective-permute-start.20 = (bf16[64,2304]{1,0:T(8,128)(2,1)S(1)}, bf16[64,2304]{1,0:T(8,128)(2,1)S(1)}, u32[]{:S(2)}, u32[]{:S(2)}) collective-permute-start(bf16[64,2304]{1,0:T(8,128)(2,1)S(1)} %slice_bitcast_fusion), channel_id=1, source_target_pairs={{0,2},{1,3},{2,0},{3,1},{4,6},{5,7},{6,4},{7,5},{8,10},{9,11},{10,... | collective-permute-start | bytes 884744 | tf_op jit(solution)/shard_map/ppermute | solution.py:18
  49.3 0.8 add.49
  50.4 1.2 %collective-permute-start.13 = (f32[80,128]{1,0:T(8,128)S(1)}, f32[80,128]{1,0:T(8,128)S(1)}, u32[]{:S(2)}, u32[]{:S(2)}) collective-permute-start(f32[80,128]{1,0:T(8,128)S(1)} %add.49), channel_id=1, source_target_pairs={{0,16},{4,20},{8,24},{12,28},{16,0},{20,4},{24,8},{28,12},{1,17},{... | collective-permute-start | bytes 122888 | tf_op jit(solution)/shard_map/ppermute | solution.py:18
  51.6 2.0 %collective-permute-start.12 = (f32[80,128]{1,0:T(8,128)S(1)}, f32[80,128]{1,0:T(8,128)S(1)}, u32[]{:S(2)}, u32[]{:S(2)}) collective-permute-start(f32[80,128]{1,0:T(8,128)S(1)} %add.49), channel_id=1, source_target_pairs={{0,8},{4,12},{8,0},{12,4},{16,24},{20,28},{24,16},{28,20},{1,9},{5... | collective-permute-start | bytes 122888 | tf_op jit(solution)/shard_map/ppermute | solution.py:18
  53.6 1.5 %collective-permute-done.14 = f32[80,128]{1,0:T(8,128)S(1)} collective-permute-done((f32[80,128]{1,0:T(8,128)S(1)}, f32[80,128]{1,0:T(8,128)S(1)}, u32[]{:S(2)}, u32[]{:S(2)}) %collective-permute-start.14) | collective-permute-done | bytes 40992 | tf_op jit(solution)/shard_map/ppermute | solution.py:18
  55.6 3.5 %collective-permute-start.17 = (f32[80,128]{1,0:T(8,128)S(1)}, f32[80,128]{1,0:T(8,128)S(1)}, u32[]{:S(2)}, u32[]{:S(2)}) collective-permute-start(f32[80,128]{1,0:T(8,128)S(1)} %add_add_fusion.1), channel_id=1, source_target_pairs={{0,3},{1,2},{2,1},{3,0},{4,7},{5,6},{6,5},{7,4},{8,11},{9,10},{10,... | collective-permute-start | bytes 122888 | tf_op jit(solution)/shard_map/ppermute | solution.py:18
  59.1 0.7 collective-permute-start.16
  60.1 1.7 %collective-permute-start.19 = (bf16[64,2304]{1,0:T(8,128)(2,1)S(1)}, bf16[64,2304]{1,0:T(8,128)(2,1)S(1)}, u32[]{:S(2)}, u32[]{:S(2)}) collective-permute-start(bf16[64,2304]{1,0:T(8,128)(2,1)S(1)} %slice_bitcast_fusion), channel_id=1, source_target_pairs={{0,1},{1,0},{2,3},{3,2},{4,5},{5,4},{6,7},{7,6},{8,9},{9,8},{10,11... | collective-permute-start | bytes 884744 | tf_op jit(solution)/shard_map/ppermute | solution.py:18
  61.8 4.9 %collective-permute-done.20.refs_9_ = bf16[64,2304]{1,0:T(8,128)(2,1)S(1)} collective-permute-done((bf16[64,2304]{1,0:T(8,128)(2,1)S(1)}, bf16[64,2304]{1,0:T(8,128)(2,1)S(1)}, u32[]{:S(2)}, u32[]{:S(2)}) %collective-permute-start.20) | collective-permute-done | bytes 294944 | tf_op jit(solution)/shard_map/ppermute | solution.py:18
  66.7 1.3 %collective-permute-done.16 = f32[80,128]{1,0:T(8,128)S(1)} collective-permute-done((f32[80,128]{1,0:T(8,128)S(1)}, f32[80,128]{1,0:T(8,128)S(1)}, u32[]{:S(2)}, u32[]{:S(2)}) %collective-permute-start.16) | collective-permute-done | bytes 40992 | tf_op jit(solution)/shard_map/ppermute | solution.py:18
  68.1 6.2 %collective-permute-done.19.refs_8_ = bf16[64,2304]{1,0:T(8,128)(2,1)S(1)} collective-permute-done((bf16[64,2304]{1,0:T(8,128)(2,1)S(1)}, bf16[64,2304]{1,0:T(8,128)(2,1)S(1)}, u32[]{:S(2)}, u32[]{:S(2)}) %collective-permute-start.19) | collective-permute-done | bytes 294944 | tf_op jit(solution)/shard_map/ppermute | solution.py:18
  74.3 5.8 %collective-permute-done.21.refs_10_ = bf16[64,2304]{1,0:T(8,128)(2,1)S(1)} collective-permute-done((bf16[64,2304]{1,0:T(8,128)(2,1)S(1)}, bf16[64,2304]{1,0:T(8,128)(2,1)S(1)}, u32[]{:S(2)}, u32[]{:S(2)}) %collective-permute-start.21) | collective-permute-done | bytes 294944 | tf_op jit(solution)/shard_map/ppermute | solution.py:18
  80.8 7.0 %block_last.1 = (f32[80,4,2304]{2,1,0:T(4,128)}, f32[2,256]{1,0:T(2,128)}) custom-call(s32[1]{0:T(128)} %bitcast.lev_ref, s32[1]{0:T(128)} %bitcast.1.slab_ref, f32[80,128]{1,0:T(8,128)} %copy-done.8, f32[80,128]{1,0:T(8,128)} %copy-done.10, f32[2,256]{1,0:T(2,128)} %refs_2_.3, f32[2,256]{1,0:T(2,128)} %refs_3_.1, f32[2,4,256]{2,1,0:T(4,128)} %bitcast.8, ...), custom_call_target="tpu_custom_call" | custom-call | tf_op jit(solution)/shard_map/block_last/pallas_call | solution.py:314
  (47 shorter events, 3.2 us)
Async XLA Ops:
  0.6 4.8 %copy-start = (bf16[2,64,2304]{2,1,0:T(8,128)(2,1)S(1)}, bf16[2,64,2304]{2,1,0:T(8,128)(2,1)}, u32[]{:S(2)}) copy-start(bf16[2,64,2304]{2,1,0:T(8,128)(2,1)} %refs_7_.3) | copy-start | bytes 1769476
  5.3 42.3 %copy-start.1 = (bf16[2,64,2304]{2,1,0:T(8,128)(2,1)S(1)}, bf16[2,64,2304]{2,1,0:T(8,128)(2,1)}, u32[]{:S(2)}) copy-start(bf16[2,64,2304]{2,1,0:T(8,128)(2,1)} %refs_7_.3) | copy-start | bytes 1769476
  5.4 4.1 %collective-permute-start = (f32[80,128]{1,0:T(8,128)}, f32[80,128]{1,0:T(8,128)S(1)}, u32[]{:S(2)}, u32[]{:S(2)}) collective-permute-start(f32[80,128]{1,0:T(8,128)} %get-tuple-element.12), channel_id=1, source_target_pairs={{0,4},{4,0},{8,12},{12,8},{16,20},{20,16},{24,28},{28,24},{1,5},{5... | collective-permute-start | bytes 122888 | tf_op jit(solution)/shard_map/ppermute | solution.py:18
  5.5 19.9 %collective-permute-start.9 = (bf16[64,2304]{1,0:T(8,128)(2,1)S(1)}, bf16[64,2304]{1,0:T(8,128)(2,1)S(1)}, u32[]{:S(2)}, u32[]{:S(2)}) collective-permute-start(bf16[64,2304]{1,0:T(8,128)(2,1)S(1)} %slice_bitcast_fusion.1), channel_id=1, source_target_pairs={{0,2},{1,3},{2,0},{3,1},{4,6},{5,7},{6,4},{7,5},{8,10},{9,11},{10,... | collective-permute-start | bytes 884744 | tf_op jit(solution)/shard_map/ppermute | solution.py:18
  10.2 4.9 %collective-permute-start.3 = (f32[80,128]{1,0:T(8,128)S(1)}, f32[80,128]{1,0:T(8,128)S(1)}, u32[]{:S(2)}, u32[]{:S(2)}) collective-permute-start(f32[80,128]{1,0:T(8,128)S(1)} %add.42), channel_id=1, source_target_pairs={{0,24},{4,28},{8,16},{12,20},{16,8},{20,12},{24,0},{28,4},{1,25},{... | collective-permute-start | bytes 122888 | tf_op jit(solution)/shard_map/ppermute | solution.py:18
  11.7 4.0 %collective-permute-start.2 = (f32[80,128]{1,0:T(8,128)S(1)}, f32[80,128]{1,0:T(8,128)S(1)}, u32[]{:S(2)}, u32[]{:S(2)}) collective-permute-start(f32[80,128]{1,0:T(8,128)S(1)} %add.42), channel_id=1, source_target_pairs={{0,16},{4,20},{8,24},{12,28},{16,0},{20,4},{24,8},{28,12},{1,17},{... | collective-permute-start | bytes 122888 | tf_op jit(solution)/shard_map/ppermute | solution.py:18
  12.5 4.0 %collective-permute-start.1 = (f32[80,128]{1,0:T(8,128)S(1)}, f32[80,128]{1,0:T(8,128)S(1)}, u32[]{:S(2)}, u32[]{:S(2)}) collective-permute-start(f32[80,128]{1,0:T(8,128)S(1)} %add.42), channel_id=1, source_target_pairs={{0,8},{4,12},{8,0},{12,4},{16,24},{20,28},{24,16},{28,20},{1,9},{5... | collective-permute-start | bytes 122888 | tf_op jit(solution)/shard_map/ppermute | solution.py:18
  16.5 9.4 %collective-permute-start.6 = (f32[80,128]{1,0:T(8,128)S(1)}, f32[80,128]{1,0:T(8,128)S(1)}, u32[]{:S(2)}, u32[]{:S(2)}) collective-permute-start(f32[80,128]{1,0:T(8,128)S(1)} %add_add_fusion.3), channel_id=1, source_target_pairs={{0,3},{1,2},{2,1},{3,0},{4,7},{5,6},{6,5},{7,4},{8,11},{9,10},{10,... | collective-permute-start | bytes 122888 | tf_op jit(solution)/shard_map/ppermute | solution.py:18
  18.9 8.2 %collective-permute-start.5 = (f32[80,128]{1,0:T(8,128)S(1)}, f32[80,128]{1,0:T(8,128)S(1)}, u32[]{:S(2)}, u32[]{:S(2)}) collective-permute-start(f32[80,128]{1,0:T(8,128)S(1)} %add_add_fusion.3), channel_id=1, source_target_pairs={{0,2},{1,3},{2,0},{3,1},{4,6},{5,7},{6,4},{7,5},{8,10},{9,11},{10,... | collective-permute-start | bytes 122888 | tf_op jit(solution)/shard_map/ppermute | solution.py:18
  19.6 7.4 %collective-permute-start.4 = (f32[80,128]{1,0:T(8,128)S(1)}, f32[80,128]{1,0:T(8,128)S(1)}, u32[]{:S(2)}, u32[]{:S(2)}) collective-permute-start(f32[80,128]{1,0:T(8,128)S(1)} %add_add_fusion.3), channel_id=1, source_target_pairs={{0,1},{1,0},{2,3},{3,2},{4,5},{5,4},{6,7},{7,6},{8,9},{9,8},{10,11... | collective-permute-start | bytes 122888 | tf_op jit(solution)/shard_map/ppermute | solution.py:18
  21.0 12.2 %collective-permute-start.8 = (bf16[64,2304]{1,0:T(8,128)(2,1)S(1)}, bf16[64,2304]{1,0:T(8,128)(2,1)S(1)}, u32[]{:S(2)}, u32[]{:S(2)}) collective-permute-start(bf16[64,2304]{1,0:T(8,128)(2,1)S(1)} %slice_bitcast_fusion.1), channel_id=1, source_target_pairs={{0,1},{1,0},{2,3},{3,2},{4,5},{5,4},{6,7},{7,6},{8,9},{9,8},{10,11... | collective-permute-start | bytes 884744 | tf_op jit(solution)/shard_map/ppermute | solution.py:18
  25.4 13.7 %copy-start.3 = (bf16[64,2304]{1,0:T(8,128)(2,1)}, bf16[64,2304]{1,0:T(8,128)(2,1)S(1)}, u32[]{:S(2)}) copy-start(bf16[64,2304]{1,0:T(8,128)(2,1)S(1)} %collective-permute-done.9.refs_10_) | copy-start | bytes 884740
  25.4 13.7 %collective-permute-start.10 = (bf16[64,2304]{1,0:T(8,128)(2,1)S(1)}, bf16[64,2304]{1,0:T(8,128)(2,1)S(1)}, u32[]{:S(2)}, u32[]{:S(2)}) collective-permute-start(bf16[64,2304]{1,0:T(8,128)(2,1)S(1)} %collective-permute-done.9.refs_10_), channel_id=1, source_target_pairs={{0,1},{1,0},{2,3},{3,2},{4,5},{5,4},{6,7},{7,6},{8,9},{9,8},{10,11... | collective-permute-start | bytes 884744 | tf_op jit(solution)/shard_map/ppermute | solution.py:18
  27.1 12.0 %copy-start.9 = (f32[80,128]{1,0:T(8,128)}, f32[80,128]{1,0:T(8,128)S(1)}, u32[]{:S(2)}) copy-start(f32[80,128]{1,0:T(8,128)S(1)} %add_add_fusion.2.refs_2_) | copy-start | bytes 122884
  27.1 1.3 %collective-permute-start.7 = (f32[80,128]{1,0:T(8,128)S(1)}, f32[80,128]{1,0:T(8,128)S(1)}, u32[]{:S(2)}, u32[]{:S(2)}) collective-permute-start(f32[80,128]{1,0:T(8,128)S(1)} %add_add_fusion.2.refs_2_), channel_id=1, source_target_pairs={{0,4},{4,0},{8,12},{12,8},{16,20},{20,16},{24,28},{28,24},{1,5},{5... | collective-permute-start | bytes 122888 | tf_op jit(solution)/shard_map/ppermute | solution.py:18
  28.4 10.7 %copy-start.11 = (f32[80,128]{1,0:T(8,128)}, f32[80,128]{1,0:T(8,128)S(1)}, u32[]{:S(2)}) copy-start(f32[80,128]{1,0:T(8,128)S(1)} %collective-permute-done.7.refs_3_) | copy-start | bytes 122884
  33.2 5.9 %copy-start.5 = (bf16[64,2304]{1,0:T(8,128)(2,1)}, bf16[64,2304]{1,0:T(8,128)(2,1)S(1)}, u32[]{:S(2)}) copy-start(bf16[64,2304]{1,0:T(8,128)(2,1)S(1)} %collective-permute-done.8.refs_9_) | copy-start | bytes 884740
  39.1 0.7 copy-start.7
  47.6 1.7 %collective-permute-start.11 = (f32[80,128]{1,0:T(8,128)}, f32[80,128]{1,0:T(8,128)S(1)}, u32[]{:S(2)}, u32[]{:S(2)}) collective-permute-start(f32[80,128]{1,0:T(8,128)} %get-tuple-element.14), channel_id=1, source_target_pairs={{0,4},{4,0},{8,12},{12,8},{16,20},{20,16},{24,28},{28,24},{1,5},{5... | collective-permute-start | bytes 122888 | tf_op jit(solution)/shard_map/ppermute | solution.py:18
  47.7 19.0 %collective-permute-start.20 = (bf16[64,2304]{1,0:T(8,128)(2,1)S(1)}, bf16[64,2304]{1,0:T(8,128)(2,1)S(1)}, u32[]{:S(2)}, u32[]{:S(2)}) collective-permute-start(bf16[64,2304]{1,0:T(8,128)(2,1)S(1)} %slice_bitcast_fusion), channel_id=1, source_target_pairs={{0,2},{1,3},{2,0},{3,1},{4,6},{5,7},{6,4},{7,5},{8,10},{9,11},{10,... | collective-permute-start | bytes 884744 | tf_op jit(solution)/shard_map/ppermute | solution.py:18
  50.1 5.0 %collective-permute-start.14 = (f32[80,128]{1,0:T(8,128)S(1)}, f32[80,128]{1,0:T(8,128)S(1)}, u32[]{:S(2)}, u32[]{:S(2)}) collective-permute-start(f32[80,128]{1,0:T(8,128)S(1)} %add.49), channel_id=1, source_target_pairs={{0,24},{4,28},{8,16},{12,20},{16,8},{20,12},{24,0},{28,4},{1,25},{... | collective-permute-start | bytes 122888 | tf_op jit(solution)/shard_map/ppermute | solution.py:18
  50.4 4.7 %collective-permute-start.13 = (f32[80,128]{1,0:T(8,128)S(1)}, f32[80,128]{1,0:T(8,128)S(1)}, u32[]{:S(2)}, u32[]{:S(2)}) collective-permute-start(f32[80,128]{1,0:T(8,128)S(1)} %add.49), channel_id=1, source_target_pairs={{0,16},{4,20},{8,24},{12,28},{16,0},{20,4},{24,8},{28,12},{1,17},{... | collective-permute-start | bytes 122888 | tf_op jit(solution)/shard_map/ppermute | solution.py:18
  51.6 4.0 %collective-permute-start.12 = (f32[80,128]{1,0:T(8,128)S(1)}, f32[80,128]{1,0:T(8,128)S(1)}, u32[]{:S(2)}, u32[]{:S(2)}) collective-permute-start(f32[80,128]{1,0:T(8,128)S(1)} %add.49), channel_id=1, source_target_pairs={{0,8},{4,12},{8,0},{12,4},{16,24},{20,28},{24,16},{28,20},{1,9},{5... | collective-permute-start | bytes 122888 | tf_op jit(solution)/shard_map/ppermute | solution.py:18
  55.6 11.1 %collective-permute-start.17 = (f32[80,128]{1,0:T(8,128)S(1)}, f32[80,128]{1,0:T(8,128)S(1)}, u32[]{:S(2)}, u32[]{:S(2)}) collective-permute-start(f32[80,128]{1,0:T(8,128)S(1)} %add_add_fusion.1), channel_id=1, source_target_pairs={{0,3},{1,2},{2,1},{3,0},{4,7},{5,6},{6,5},{7,4},{8,11},{9,10},{10,... | collective-permute-start | bytes 122888 | tf_op jit(solution)/shard_map/ppermute | solution.py:18
  59.1 8.9 %collective-permute-start.16 = (f32[80,128]{1,0:T(8,128)S(1)}, f32[80,128]{1,0:T(8,128)S(1)}, u32[]{:S(2)}, u32[]{:S(2)}) collective-permute-start(f32[80,128]{1,0:T(8,128)S(1)} %add_add_fusion.1), channel_id=1, source_target_pairs={{0,2},{1,3},{2,0},{3,1},{4,6},{5,7},{6,4},{7,5},{8,10},{9,11},{10,... | collective-permute-start | bytes 122888 | tf_op jit(solution)/shard_map/ppermute | solution.py:18
  59.8 8.2 %collective-permute-start.15 = (f32[80,128]{1,0:T(8,128)S(1)}, f32[80,128]{1,0:T(8,128)S(1)}, u32[]{:S(2)}, u32[]{:S(2)}) collective-permute-start(f32[80,128]{1,0:T(8,128)S(1)} %add_add_fusion.1), channel_id=1, source_target_pairs={{0,1},{1,0},{2,3},{3,2},{4,5},{5,4},{6,7},{7,6},{8,9},{9,8},{10,11... | collective-permute-start | bytes 122888 | tf_op jit(solution)/shard_map/ppermute | solution.py:18
  60.1 14.2 %collective-permute-start.19 = (bf16[64,2304]{1,0:T(8,128)(2,1)S(1)}, bf16[64,2304]{1,0:T(8,128)(2,1)S(1)}, u32[]{:S(2)}, u32[]{:S(2)}) collective-permute-start(bf16[64,2304]{1,0:T(8,128)(2,1)S(1)} %slice_bitcast_fusion), channel_id=1, source_target_pairs={{0,1},{1,0},{2,3},{3,2},{4,5},{5,4},{6,7},{7,6},{8,9},{9,8},{10,11... | collective-permute-start | bytes 884744 | tf_op jit(solution)/shard_map/ppermute | solution.py:18
  66.7 13.4 %copy-start.2 = (bf16[64,2304]{1,0:T(8,128)(2,1)}, bf16[64,2304]{1,0:T(8,128)(2,1)S(1)}, u32[]{:S(2)}) copy-start(bf16[64,2304]{1,0:T(8,128)(2,1)S(1)} %collective-permute-done.20.refs_9_) | copy-start | bytes 884740
  66.7 13.4 %collective-permute-start.21 = (bf16[64,2304]{1,0:T(8,128)(2,1)S(1)}, bf16[64,2304]{1,0:T(8,128)(2,1)S(1)}, u32[]{:S(2)}, u32[]{:S(2)}) collective-permute-start(bf16[64,2304]{1,0:T(8,128)(2,1)S(1)} %collective-permute-done.20.refs_9_), channel_id=1, source_target_pairs={{0,1},{1,0},{2,3},{3,2},{4,5},{5,4},{6,7},{7,6},{8,9},{9,8},{10,11... | collective-permute-start | bytes 884744 | tf_op jit(solution)/shard_map/ppermute | solution.py:18
  68.0 12.1 %copy-start.8 = (f32[80,128]{1,0:T(8,128)}, f32[80,128]{1,0:T(8,128)S(1)}, u32[]{:S(2)}) copy-start(f32[80,128]{1,0:T(8,128)S(1)} %add_add_fusion.refs_0_) | copy-start | bytes 122884
  68.0 12.1 %collective-permute-start.18 = (f32[80,128]{1,0:T(8,128)S(1)}, f32[80,128]{1,0:T(8,128)S(1)}, u32[]{:S(2)}, u32[]{:S(2)}) collective-permute-start(f32[80,128]{1,0:T(8,128)S(1)} %add_add_fusion.refs_0_), channel_id=1, source_target_pairs={{0,4},{4,0},{8,12},{12,8},{16,20},{20,16},{24,28},{28,24},{1,5},{5... | collective-permute-start | bytes 122888 | tf_op jit(solution)/shard_map/ppermute | solution.py:18
  74.3 5.8 %copy-start.4 = (bf16[64,2304]{1,0:T(8,128)(2,1)}, bf16[64,2304]{1,0:T(8,128)(2,1)S(1)}, u32[]{:S(2)}) copy-start(bf16[64,2304]{1,0:T(8,128)(2,1)S(1)} %collective-permute-done.19.refs_8_) | copy-start | bytes 884740
  (2 other events, 1.4 us)

commit v4 on v3

--- a/solution.py
+++ b/solution.py
@@ -11,6 +11,7 @@
 LANES = 128
 CELL_BITS = 16
 BATCH = 4
+KERNEL_VMEM = 32 * 1024 * 1024
 
 
 def swap(value, axis, bit):
@@ -33,7 +34,7 @@
 
 def add_over(keep, send):
     half = keep + swap(send, "slab", 1)
-    rounds = list(rounds_of("slab", 2)) + list(rounds_of("lev", 1))
+    rounds = list(rounds_of("lev", 1)) + list(rounds_of("slab", 2))
     for axis, distances in rounds:
         half = sum([swap(half, axis, d) for d in distances], half)
     return half, swap(half, "slab", 1)
@@ -184,63 +185,51 @@
     return obs_mean
 
 
-def regress(field, rows_ref, l, work):
+def regress(field, shards, l, work):
     _, dev_ref, gain_ref, level_b_ref = work
     members, slab_cols = field.shape
     centred = (field - jnp.sum(field, axis=0, keepdims=True) / members).astype(jnp.bfloat16)
     cross = jnp.dot(dev_ref[...], centred, preferred_element_type=jnp.float32)
     level = jnp.concatenate([level_b_ref[l]] * (slab_cols // LANES), axis=1)
-    mixed = ((level * rows_ref[...].astype(jnp.float32)) * cross).astype(jnp.bfloat16)
+    rows = jnp.concatenate([r[...] for r in shards], axis=0)
+    mixed = ((level * rows.astype(jnp.float32)) * cross).astype(jnp.bfloat16)
     return field + jnp.dot(gain_ref[...], mixed, preferred_element_type=jnp.float32)
 
 
-def load_rows(b, shards, rows_ref, sems):
-    own, *rest = shards
-    count = own.shape[1]
-    return [
-        pltpu.make_async_copy(own.at[b] if p == 0 else rest[p - 1], rows_ref.at[pl.ds(p * count, count)], sems.at[p])
-        for p in range(len(shards))
-    ]
-
-
 def first_kernel(groups, sizes, place_ref, frac_ref, cell_ref, own_ref, other_ref, value_ref, var_ref, level_ref, ens_ref, *rest):
-    shards = rest[:groups]
-    cur_out, mean_ref, keep_ref, send_ref, cur_ref, rows_ref, *work, key_ref, key_smem, list_ref, sems, row_sems, key_sem = rest[groups:]
+    cur_out, mean_ref, keep_ref, send_ref, cur_ref, rows_ref, *work, key_ref, key_smem, list_ref, sems, row_sem, key_sem = rest[groups:]
+    shards = [rows_ref, *rest[1:groups]]
     lev_rows = cur_ref.shape[0]
     keys = key_copy(place_ref, cell_ref, key_ref, key_smem, key_sem, sizes)
     keys.start()
     copies = load_levels(ens_ref, cur_ref, sems)
-    rows = load_rows(0, shards, rows_ref, row_sems)
-    for copy in copies[:1] + rows + copies[1:]:
+    rows = pltpu.make_async_copy(rest[0].at[0], rows_ref, row_sem)
+    rows.start()
+    for copy in copies:
         copy.start()
     mean_ref[...] = observe(0, groups, place_ref, own_ref, other_ref, value_ref, var_ref, level_ref, work)
     keys.wait()
     found = list_owned(key_smem, list_ref, 1)
-    for copy in rows:
-        copy.wait()
+    rows.wait()
     for l in range(lev_rows):
         copies[l].wait()
-        cur_out[l] = regress(cur_ref[l], rows_ref, l, work)
+        cur_out[l] = regress(cur_ref[l], shards, l, work)
     gather_priors(key_smem, frac_ref, list_ref, 1, found, cur_out, work[0])
     split_halves(place_ref[1] & 1, work[0], keep_ref, send_ref)
 
 
-def last_kernel(groups, place_ref, own_ref, other_ref, value_ref, var_ref, level_ref, mean_in, cur_in, *rest):
-    shards = rest[:groups]
-    ens_out, mean_ref, cur_ref, rows_ref, buf_ref, *work, sems, row_sems = rest[groups:]
+def last_kernel(groups, place_ref, own_ref, other_ref, value_ref, var_ref, level_ref, mean_in, cur_ref, *rest):
+    ens_out, mean_ref, rows_ref, buf_ref, *work, sems, row_sem = rest[groups:]
+    shards = [rows_ref, *rest[1:groups]]
     lev_rows = cur_ref.shape[0]
-    copies = [pltpu.make_async_copy(cur_in.at[l], cur_ref.at[l], sems.at[l]) for l in range(lev_rows)]
-    rows = load_rows(1, shards, rows_ref, row_sems)
-    for copy in copies[:1] + rows + copies[1:]:
-        copy.start()
+    rows = pltpu.make_async_copy(rest[0].at[1], rows_ref, row_sem)
+    rows.start()
     mean_ref[0:1] = mean_in[...]
     mean_ref[1:2] = observe(1, groups, place_ref, own_ref, other_ref, value_ref, var_ref, level_ref, work)
-    for copy in rows:
-        copy.wait()
+    rows.wait()
     stores = []
     for l in range(lev_rows):
-        copies[l].wait()
-        buf_ref[l] = regress(cur_ref[l], rows_ref, l, work)
+        buf_ref[l] = regress(cur_ref[l], shards, l, work)
         stores.append(pltpu.make_async_copy(buf_ref.at[l], ens_out.at[:, l, :], sems.at[l]))
         stores[l].start()
     for store in stores:
@@ -252,6 +241,14 @@
         kernel((lev_ref[0], slab_ref[0]), *refs)
 
     return run
+
+
+def near(*arrays):
+    return [pltpu.with_memory_space_constraint(a, pltpu.VMEM) for a in arrays]
+
+
+def far(*arrays):
+    return [pltpu.with_memory_space_constraint(a, pltpu.HBM) for a in arrays]
 
 
 def on_device(ensemble, obs_cell, obs_value, obs_var, obs_frac, loc_column, loc_level):
@@ -266,11 +263,11 @@
     vmem = pl.BlockSpec(memory_space=pltpu.VMEM)
     hbm = pl.BlockSpec(memory_space=pl.ANY)
     f32 = jnp.float32
-    field = jax.ShapeDtypeStruct((lev_rows, members, slab_cols), f32)
-    row = jax.ShapeDtypeStruct((1, n_obs), f32)
-    half = jax.ShapeDtypeStruct((members, n_obs // 2), f32)
+    field = pltpu.VMEM((lev_rows, members, slab_cols), f32)
+    row = pltpu.VMEM((1, n_obs), f32)
+    half = pltpu.VMEM((members, n_obs // 2), f32)
     field_scratch = pltpu.VMEM((lev_rows, members, slab_cols), f32)
-    rows_scratch = pltpu.VMEM((n_obs, slab_cols), jnp.bfloat16)
+    rows_scratch = pltpu.VMEM(loc_column.shape[1:], jnp.bfloat16)
     sum_scratch = pltpu.VMEM((members, n_obs), f32)
     work = [
         sum_scratch,
@@ -284,7 +281,6 @@
         pltpu.SMEM((n_obs + BATCH,), jnp.int32),
     ]
     dma = pltpu.SemaphoreType.DMA((lev_rows,))
-    row_dma = pltpu.SemaphoreType.DMA((groups,))
     one_dma = pltpu.SemaphoreType.DMA
 
     shards = [rows_over(loc_column[0], "lev")]
@@ -295,8 +291,9 @@
         in_specs=[smem, smem, smem, vmem, hbm],
         out_specs=(vmem, vmem),
         scratch_shapes=[field_scratch, sum_scratch] + own + [dma, one_dma],
+        compiler_params=pltpu.CompilerParams(vmem_limit_bytes=KERNEL_VMEM),
         name="cells",
-    )(*place, obs_frac, obs_cell, ensemble)
+    )(*place, *far(obs_frac, obs_cell, ensemble))
     later_rows, keep = lax.optimization_barrier((loc_column, keep))
     shards.append(rows_over(later_rows[1], "lev"))
     ours, theirs = add_over(keep, send)
@@ -304,21 +301,23 @@
     current, mean_first, keep, send = pl.pallas_call(
         with_place(functools.partial(first_kernel, groups, sizes)),
         out_shape=(field, row, half, half),
-        in_specs=[smem, smem, smem] + [vmem] * 6 + [hbm] * (1 + groups),
+        in_specs=[smem, smem, smem] + [vmem] * 6 + [hbm] * 2 + [vmem] * (groups - 1),
         out_specs=(vmem, vmem, vmem, vmem),
-        scratch_shapes=[field_scratch, rows_scratch] + work + own + [dma, row_dma, one_dma],
+        scratch_shapes=[field_scratch, rows_scratch] + work + own + [dma, one_dma, one_dma],
+        compiler_params=pltpu.CompilerParams(vmem_limit_bytes=KERNEL_VMEM),
         name="block_first",
-    )(*place, obs_frac, obs_cell, ours, theirs, obs_value, obs_var, levels, ensemble, loc_column, *shards[0])
+    )(*place, obs_frac, obs_cell, *near(ours, theirs), obs_value, obs_var, levels, *far(ensemble, loc_column), *near(*shards[0]))
     ours, theirs = add_over(keep, send)
 
     analysis, mean = pl.pallas_call(
         with_place(functools.partial(last_kernel, groups)),
         out_shape=(jax.ShapeDtypeStruct(ensemble.shape, f32), jax.ShapeDtypeStruct((n_blocks, n_obs), f32)),
-        in_specs=[smem, smem] + [vmem] * 6 + [hbm] * (1 + groups),
+        in_specs=[smem, smem] + [vmem] * 7 + [hbm] + [vmem] * (groups - 1),
         out_specs=(hbm, vmem),
-        scratch_shapes=[field_scratch, rows_scratch, field_scratch] + work + [dma, row_dma],
+        scratch_shapes=[rows_scratch, field_scratch] + work + [dma, one_dma],
+        compiler_params=pltpu.CompilerParams(vmem_limit_bytes=KERNEL_VMEM),
         name="block_last",
-    )(*place, ours, theirs, obs_value, obs_var, levels, mean_first, current, loc_column, *shards[1])
+    )(*place, *near(ours, theirs), obs_value, obs_var, levels, *near(mean_first, current), *far(loc_column), *near(*shards[1]))
     return (analysis, mean)
 
 

time: 88.2 us -> 94.1 us (1.067)
  waiting for transfers between devices: 39.7 us -> 50.3 us
  Pallas kernels: 19.4 us -> 15.4 us
  starting transfers between devices: 24.7 us -> 27.2 us
  other arithmetic: 1.62 us -> 0.07 us
  local copies, waits for them, and re-layouts: 1.47 us -> 0.08 us
    ppermute x22, waiting for transfers between devices: 39.7 us -> 50.3 us  [swap(): return lax.ppermute(value, axis, [(i, i ^ bit) for i in range(size)])]
    ppermute x22, starting transfers between devices: 24.7 us -> 27.2 us  [swap(): return lax.ppermute(value, axis, [(i, i ^ bit) for i in range(size)])]
    pallas_call x1, Pallas kernels: 7.77 us -> 5.89 us  [on_device(): pl.pallas_call(with_place(functools.partial(first_kernel, groups, sizes))...]
    add x2, other arithmetic: 1.57 us -> 0.01 us  [add_over(): half = keep + swap(send, 'slab', 1)]
    pallas_call x1, Pallas kernels: 6.95 us -> 5.4 us  [on_device(): pl.pallas_call(with_place(functools.partial(last_kernel, groups)), out_sh...]
    unnamed x24 -> x14, local copies, waits for them, and re-layouts: 1.43 us -> 0.03 us
  transfers between devices with their start and end apart: 22 -> 22, of which waited for: 14 -> 11; matrix products, arithmetic and copies ran while one was open for 2% -> 0% of each run, Pallas kernels for 0% -> 0%
where the time goes in v4:
time: 94.1 us; the launch traced here: 93.9 us
  waiting for transfers between devices  50.3 us (53%)
  starting transfers between devices  27.2 us (29%)
  Pallas kernels  15.4 us (16%)
    ppermute x22, waiting for transfers between devices, swap(): return lax.ppermute(value, axis, [(i, i ^ bit) for i in range(size)])  50.3 us
    ppermute x22, starting transfers between devices, swap(): return lax.ppermute(value, axis, [(i, i ^ bit) for i in range(size)])  27.2 us
    pallas_call x1, Pallas kernels, on_device(): pl.pallas_call(with_place(functools.partial(first_kernel, groups, sizes))...  5.89 us
    pallas_call x1, Pallas kernels, on_device(): pl.pallas_call(with_place(functools.partial(last_kernel, groups)), out_sh...  5.4 us
    pallas_call x1, Pallas kernels, on_device(): pl.pallas_call(with_place(functools.partial(prior_kernel, sizes)), out_sh...  4.07 us
  transfers between devices with their start and end apart: 22, of which 11 were waited for; matrix products, arithmetic and copies ran while one was open for 0% of the time, Pallas kernels for 0%

profile of v4, /device:TPU:0, one launch (start us, length us, event | category | flops | bytes accessed | tf_op | source)
XLA Modules:
  0.0 93.9 jit_solution(7167831081354749161)
XLA Ops:
  0.7 4.1 %cells.1 = (f32[80,128]{1,0:T(8,128)S(1)}, f32[80,128]{1,0:T(8,128)S(1)}) custom-call(s32[1]{0:T(128)} %bitcast.lev_ref, s32[1]{0:T(128)} %bitcast.1.slab_ref, f32[2,256]{1,0:T(2,128)} %refs_0_.3, s32[2,256]{1,0:T(2,128)} %refs_1_.3, f32[80,4,2304]{2,1,0:T(4,128)} %refs_7_.2), custom_call_target="tpu_custom_call" | custom-call | tf_op jit(solution)/shard_map/cells/pallas_call | solution.py:288
  4.9 4.0 %collective-permute-start.9 = (bf16[64,2304]{1,0:T(8,128)(2,1)S(1)}, bf16[64,2304]{1,0:T(8,128)(2,1)S(1)}, u32[]{:S(2)}, u32[]{:S(2)}) collective-permute-start(bf16[64,2304]{1,0:T(8,128)(2,1)S(1)} %slice_bitcast_fusion.1), channel_id=1, source_target_pairs={{0,2},{1,3},{2,0},{3,1},{4,6},{5,7},{6,4},{7,5},{8,10},{9,11},{10,... | collective-permute-start | bytes 884744 | tf_op jit(solution)/shard_map/ppermute | solution.py:19
  8.9 2.3 %collective-permute-start.3 = (f32[80,128]{1,0:T(8,128)S(1)}, f32[80,128]{1,0:T(8,128)S(1)}, u32[]{:S(2)}, u32[]{:S(2)}) collective-permute-start(f32[80,128]{1,0:T(8,128)S(1)} %add.42), channel_id=1, source_target_pairs={{0,3},{1,2},{2,1},{3,0},{4,7},{5,6},{6,5},{7,4},{8,11},{9,10},{10,... | collective-permute-start | bytes 122888 | tf_op jit(solution)/shard_map/ppermute | solution.py:19
  11.2 1.0 %collective-permute-start.2 = (f32[80,128]{1,0:T(8,128)S(1)}, f32[80,128]{1,0:T(8,128)S(1)}, u32[]{:S(2)}, u32[]{:S(2)}) collective-permute-start(f32[80,128]{1,0:T(8,128)S(1)} %add.42), channel_id=1, source_target_pairs={{0,2},{1,3},{2,0},{3,1},{4,6},{5,7},{6,4},{7,5},{8,10},{9,11},{10,... | collective-permute-start | bytes 122888 | tf_op jit(solution)/shard_map/ppermute | solution.py:19
  12.2 1.2 %collective-permute-start.1 = (f32[80,128]{1,0:T(8,128)S(1)}, f32[80,128]{1,0:T(8,128)S(1)}, u32[]{:S(2)}, u32[]{:S(2)}) collective-permute-start(f32[80,128]{1,0:T(8,128)S(1)} %add.42), channel_id=1, source_target_pairs={{0,1},{1,0},{2,3},{3,2},{4,5},{5,4},{6,7},{7,6},{8,9},{9,8},{10,11... | collective-permute-start | bytes 122888 | tf_op jit(solution)/shard_map/ppermute | solution.py:19
  13.3 5.8 %collective-permute-done.3 = f32[80,128]{1,0:T(8,128)S(1)} collective-permute-done((f32[80,128]{1,0:T(8,128)S(1)}, f32[80,128]{1,0:T(8,128)S(1)}, u32[]{:S(2)}, u32[]{:S(2)}) %collective-permute-start.3) | collective-permute-done | bytes 40992 | tf_op jit(solution)/shard_map/ppermute | solution.py:19
  19.2 7.2 %collective-permute-done.2 = f32[80,128]{1,0:T(8,128)S(1)} collective-permute-done((f32[80,128]{1,0:T(8,128)S(1)}, f32[80,128]{1,0:T(8,128)S(1)}, u32[]{:S(2)}, u32[]{:S(2)}) %collective-permute-start.2) | collective-permute-done | bytes 40992 | tf_op jit(solution)/shard_map/ppermute | solution.py:19
  26.4 1.6 %collective-permute-start.6 = (f32[80,128]{1,0:T(8,128)S(1)}, f32[80,128]{1,0:T(8,128)S(1)}, u32[]{:S(2)}, u32[]{:S(2)}) collective-permute-start(f32[80,128]{1,0:T(8,128)S(1)} %add_add_fusion.3), channel_id=1, source_target_pairs={{0,24},{4,28},{8,16},{12,20},{16,8},{20,12},{24,0},{28,4},{1,25},{... | collective-permute-start | bytes 122888 | tf_op jit(solution)/shard_map/ppermute | solution.py:19
  27.9 0.8 collective-permute-start.5
  28.7 1.2 %collective-permute-start.4 = (f32[80,128]{1,0:T(8,128)S(1)}, f32[80,128]{1,0:T(8,128)S(1)}, u32[]{:S(2)}, u32[]{:S(2)}) collective-permute-start(f32[80,128]{1,0:T(8,128)S(1)} %add_add_fusion.3), channel_id=1, source_target_pairs={{0,8},{4,12},{8,0},{12,4},{16,24},{20,28},{24,16},{28,20},{1,9},{5... | collective-permute-start | bytes 122888 | tf_op jit(solution)/shard_map/ppermute | solution.py:19
  29.9 0.7 collective-permute-start.8
  30.7 1.3 %collective-permute-start.10 = (bf16[64,2304]{1,0:T(8,128)(2,1)S(1)}, bf16[64,2304]{1,0:T(8,128)(2,1)S(1)}, u32[]{:S(2)}, u32[]{:S(2)}) collective-permute-start(bf16[64,2304]{1,0:T(8,128)(2,1)S(1)} %collective-permute-done.9.refs_10_), channel_id=1, source_target_pairs={{0,1},{1,0},{2,3},{3,2},{4,5},{5,4},{6,7},{7,6},{8,9},{9,8},{10,11... | collective-permute-start | bytes 884744 | tf_op jit(solution)/shard_map/ppermute | solution.py:19
  32.0 0.1 collective-permute-done.5
  32.1 0.7 collective-permute-done.4
  32.8 1.2 %collective-permute-done.7.refs_3_ = f32[80,128]{1,0:T(8,128)S(1)} collective-permute-done((f32[80,128]{1,0:T(8,128)S(1)}, f32[80,128]{1,0:T(8,128)S(1)}, u32[]{:S(2)}, u32[]{:S(2)}) %collective-permute-start.7) | collective-permute-done | bytes 40992 | tf_op jit(solution)/shard_map/ppermute | solution.py:19
  34.0 5.8 %collective-permute-done.8.refs_9_ = bf16[64,2304]{1,0:T(8,128)(2,1)S(1)} collective-permute-done((bf16[64,2304]{1,0:T(8,128)(2,1)S(1)}, bf16[64,2304]{1,0:T(8,128)(2,1)S(1)}, u32[]{:S(2)}, u32[]{:S(2)}) %collective-permute-start.8) | collective-permute-done | bytes 294944 | tf_op jit(solution)/shard_map/ppermute | solution.py:19
  39.8 4.4 %collective-permute-done.10.refs_11_ = bf16[64,2304]{1,0:T(8,128)(2,1)S(1)} collective-permute-done((bf16[64,2304]{1,0:T(8,128)(2,1)S(1)}, bf16[64,2304]{1,0:T(8,128)(2,1)S(1)}, u32[]{:S(2)}, u32[]{:S(2)}) %collective-permute-start.10) | collective-permute-done | bytes 294944 | tf_op jit(solution)/shard_map/ppermute | solution.py:19
  44.3 5.9 %block_first.1 = (f32[4,80,2304]{2,1,0:T(8,128)S(1)}, f32[1,256]{1,0:T(1,128)S(1)}, f32[80,128]{1,0:T(8,128)S(1)}, f32[80,128]{1,0:T(8,128)S(1)}) custom-call(s32[1]{0:T(128)} %bitcast.lev_ref, s32[1]{0:T(128)} %bitcast.1.slab_ref, f32[2,256]{1,0:T(2,128)S(1)} %copy-done.3, s32[2,256]{1,0:T(2,128)S(1)} %copy-done.4, f32[80,128]{1,0:T(8,128)S(1)} %add_add_fusion.2.refs_2_, ...), custom_call_target="tpu_custom_call" | custom-call | tf_op jit(solution)/shard_map/block_first/pallas_call | solution.py:301
  50.3 2.9 %collective-permute-start.20 = (bf16[64,2304]{1,0:T(8,128)(2,1)S(1)}, bf16[64,2304]{1,0:T(8,128)(2,1)S(1)}, u32[]{:S(2)}, u32[]{:S(2)}) collective-permute-start(bf16[64,2304]{1,0:T(8,128)(2,1)S(1)} %slice_bitcast_fusion), channel_id=1, source_target_pairs={{0,2},{1,3},{2,0},{3,1},{4,6},{5,7},{6,4},{7,5},{8,10},{9,11},{10,... | collective-permute-start | bytes 884744 | tf_op jit(solution)/shard_map/ppermute | solution.py:19
  53.2 2.5 %collective-permute-start.14 = (f32[80,128]{1,0:T(8,128)S(1)}, f32[80,128]{1,0:T(8,128)S(1)}, u32[]{:S(2)}, u32[]{:S(2)}) collective-permute-start(f32[80,128]{1,0:T(8,128)S(1)} %add.49), channel_id=1, source_target_pairs={{0,3},{1,2},{2,1},{3,0},{4,7},{5,6},{6,5},{7,4},{8,11},{9,10},{10,... | collective-permute-start | bytes 122888 | tf_op jit(solution)/shard_map/ppermute | solution.py:19
  55.7 1.0 %collective-permute-start.13 = (f32[80,128]{1,0:T(8,128)S(1)}, f32[80,128]{1,0:T(8,128)S(1)}, u32[]{:S(2)}, u32[]{:S(2)}) collective-permute-start(f32[80,128]{1,0:T(8,128)S(1)} %add.49), channel_id=1, source_target_pairs={{0,2},{1,3},{2,0},{3,1},{4,6},{5,7},{6,4},{7,5},{8,10},{9,11},{10,... | collective-permute-start | bytes 122888 | tf_op jit(solution)/shard_map/ppermute | solution.py:19
  56.7 1.0 %collective-permute-start.12 = (f32[80,128]{1,0:T(8,128)S(1)}, f32[80,128]{1,0:T(8,128)S(1)}, u32[]{:S(2)}, u32[]{:S(2)}) collective-permute-start(f32[80,128]{1,0:T(8,128)S(1)} %add.49), channel_id=1, source_target_pairs={{0,1},{1,0},{2,3},{3,2},{4,5},{5,4},{6,7},{7,6},{8,9},{9,8},{10,11... | collective-permute-start | bytes 122888 | tf_op jit(solution)/shard_map/ppermute | solution.py:19
  57.7 5.7 %collective-permute-done.14 = f32[80,128]{1,0:T(8,128)S(1)} collective-permute-done((f32[80,128]{1,0:T(8,128)S(1)}, f32[80,128]{1,0:T(8,128)S(1)}, u32[]{:S(2)}, u32[]{:S(2)}) %collective-permute-start.14) | collective-permute-done | bytes 40992 | tf_op jit(solution)/shard_map/ppermute | solution.py:19
  63.4 7.3 %collective-permute-done.13 = f32[80,128]{1,0:T(8,128)S(1)} collective-permute-done((f32[80,128]{1,0:T(8,128)S(1)}, f32[80,128]{1,0:T(8,128)S(1)}, u32[]{:S(2)}, u32[]{:S(2)}) %collective-permute-start.13) | collective-permute-done | bytes 40992 | tf_op jit(solution)/shard_map/ppermute | solution.py:19
  70.7 0.3 collective-permute-start.17
  71.0 1.2 %collective-permute-start.16 = (f32[80,128]{1,0:T(8,128)S(1)}, f32[80,128]{1,0:T(8,128)S(1)}, u32[]{:S(2)}, u32[]{:S(2)}) collective-permute-start(f32[80,128]{1,0:T(8,128)S(1)} %add_add_fusion.1), channel_id=1, source_target_pairs={{0,16},{4,20},{8,24},{12,28},{16,0},{20,4},{24,8},{28,12},{1,17},{... | collective-permute-start | bytes 122888 | tf_op jit(solution)/shard_map/ppermute | solution.py:19
  72.2 2.1 %collective-permute-start.15 = (f32[80,128]{1,0:T(8,128)S(1)}, f32[80,128]{1,0:T(8,128)S(1)}, u32[]{:S(2)}, u32[]{:S(2)}) collective-permute-start(f32[80,128]{1,0:T(8,128)S(1)} %add_add_fusion.1), channel_id=1, source_target_pairs={{0,8},{4,12},{8,0},{12,4},{16,24},{20,28},{24,16},{28,20},{1,9},{5... | collective-permute-start | bytes 122888 | tf_op jit(solution)/shard_map/ppermute | solution.py:19
  74.3 0.7 collective-permute-start.19
  75.0 1.3 %collective-permute-start.21 = (bf16[64,2304]{1,0:T(8,128)(2,1)S(1)}, bf16[64,2304]{1,0:T(8,128)(2,1)S(1)}, u32[]{:S(2)}, u32[]{:S(2)}) collective-permute-start(bf16[64,2304]{1,0:T(8,128)(2,1)S(1)} %collective-permute-done.20.refs_9_), channel_id=1, source_target_pairs={{0,1},{1,0},{2,3},{3,2},{4,5},{5,4},{6,7},{7,6},{8,9},{9,8},{10,11... | collective-permute-start | bytes 884744 | tf_op jit(solution)/shard_map/ppermute | solution.py:19
  76.4 7.7 %collective-permute-done.19.refs_8_ = bf16[64,2304]{1,0:T(8,128)(2,1)S(1)} collective-permute-done((bf16[64,2304]{1,0:T(8,128)(2,1)S(1)}, bf16[64,2304]{1,0:T(8,128)(2,1)S(1)}, u32[]{:S(2)}, u32[]{:S(2)}) %collective-permute-start.19) | collective-permute-done | bytes 294944 | tf_op jit(solution)/shard_map/ppermute | solution.py:19
  84.2 4.4 %collective-permute-done.21.refs_10_ = bf16[64,2304]{1,0:T(8,128)(2,1)S(1)} collective-permute-done((bf16[64,2304]{1,0:T(8,128)(2,1)S(1)}, bf16[64,2304]{1,0:T(8,128)(2,1)S(1)}, u32[]{:S(2)}, u32[]{:S(2)}) %collective-permute-start.21) | collective-permute-done | bytes 294944 | tf_op jit(solution)/shard_map/ppermute | solution.py:19
  88.5 5.4 %block_last.1 = (f32[80,4,2304]{2,1,0:T(4,128)}, f32[2,256]{1,0:T(2,128)}) custom-call(s32[1]{0:T(128)} %bitcast.lev_ref, s32[1]{0:T(128)} %bitcast.1.slab_ref, f32[80,128]{1,0:T(8,128)S(1)} %add_add_fusion.refs_0_, f32[80,128]{1,0:T(8,128)S(1)} %collective-permute-done.18.refs_1_, f32[2,256]{1,0:T(2,128)S(1)} %copy-done.1, f32[2,256]{1,0:T(2,128)S(1)} %copy-done.2, ...), custom_call_target="tpu_custom_call" | custom-call | tf_op jit(solution)/shard_map/block_last/pallas_call | solution.py:312
  (37 shorter events, 0.5 us)
Async XLA Ops:
  0.6 43.6 %copy-start.3 = (f32[2,256]{1,0:T(2,128)S(1)}, f32[2,256]{1,0:T(2,128)}, u32[]{:S(2)}) copy-start(f32[2,256]{1,0:T(2,128)} %refs_0_.3) | copy-start | bytes 6148
  0.6 43.6 %copy-start.4 = (s32[2,256]{1,0:T(2,128)S(1)}, s32[2,256]{1,0:T(2,128)}, u32[]{:S(2)}) copy-start(s32[2,256]{1,0:T(2,128)} %refs_1_.3) | copy-start | bytes 6148
  0.7 4.2 %copy-start.5 = (bf16[2,64,2304]{2,1,0:T(8,128)(2,1)S(1)}, bf16[2,64,2304]{2,1,0:T(8,128)(2,1)}, u32[]{:S(2)}) copy-start(bf16[2,64,2304]{2,1,0:T(8,128)(2,1)} %refs_7_.3) | copy-start | bytes 1769476
  0.7 43.6 %copy-start.2 = (f32[2,256]{1,0:T(2,128)S(1)}, f32[2,256]{1,0:T(2,128)}, u32[]{:S(2)}) copy-start(f32[2,256]{1,0:T(2,128)} %refs_3_.1) | copy-start | bytes 6148
  0.7 43.6 %copy-start.1 = (f32[2,256]{1,0:T(2,128)S(1)}, f32[2,256]{1,0:T(2,128)}, u32[]{:S(2)}) copy-start(f32[2,256]{1,0:T(2,128)} %refs_2_.3) | copy-start | bytes 6148
  0.7 43.6 %copy-start = (f32[2,256,4]{1,2,0:T(4,128)S(1)}, f32[2,256,4]{1,2,0:T(4,128)}, u32[]{:S(2)}) copy-start(f32[2,256,4]{1,2,0:T(4,128)} %param.13) | copy-start | bytes 24580
  4.8 45.5 %copy-start.6 = (bf16[2,64,2304]{2,1,0:T(8,128)(2,1)S(1)}, bf16[2,64,2304]{2,1,0:T(8,128)(2,1)}, u32[]{:S(2)}) copy-start(bf16[2,64,2304]{2,1,0:T(8,128)(2,1)} %refs_7_.3) | copy-start | bytes 1769476
  4.8 4.1 %collective-permute-start = (f32[80,128]{1,0:T(8,128)S(1)}, f32[80,128]{1,0:T(8,128)S(1)}, u32[]{:S(2)}, u32[]{:S(2)}) collective-permute-start(f32[80,128]{1,0:T(8,128)S(1)} %get-tuple-element.12), channel_id=1, source_target_pairs={{0,4},{4,0},{8,12},{12,8},{16,20},{20,16},{24,28},{28,24},{1,5},{5... | collective-permute-start | bytes 122888 | tf_op jit(solution)/shard_map/ppermute | solution.py:19
  4.9 25.8 %collective-permute-start.9 = (bf16[64,2304]{1,0:T(8,128)(2,1)S(1)}, bf16[64,2304]{1,0:T(8,128)(2,1)S(1)}, u32[]{:S(2)}, u32[]{:S(2)}) collective-permute-start(bf16[64,2304]{1,0:T(8,128)(2,1)S(1)} %slice_bitcast_fusion.1), channel_id=1, source_target_pairs={{0,2},{1,3},{2,0},{3,1},{4,6},{5,7},{6,4},{7,5},{8,10},{9,11},{10,... | collective-permute-start | bytes 884744 | tf_op jit(solution)/shard_map/ppermute | solution.py:19
  8.9 10.3 %collective-permute-start.3 = (f32[80,128]{1,0:T(8,128)S(1)}, f32[80,128]{1,0:T(8,128)S(1)}, u32[]{:S(2)}, u32[]{:S(2)}) collective-permute-start(f32[80,128]{1,0:T(8,128)S(1)} %add.42), channel_id=1, source_target_pairs={{0,3},{1,2},{2,1},{3,0},{4,7},{5,6},{6,5},{7,4},{8,11},{9,10},{10,... | collective-permute-start | bytes 122888 | tf_op jit(solution)/shard_map/ppermute | solution.py:19
  11.2 15.2 %collective-permute-start.2 = (f32[80,128]{1,0:T(8,128)S(1)}, f32[80,128]{1,0:T(8,128)S(1)}, u32[]{:S(2)}, u32[]{:S(2)}) collective-permute-start(f32[80,128]{1,0:T(8,128)S(1)} %add.42), channel_id=1, source_target_pairs={{0,2},{1,3},{2,0},{3,1},{4,6},{5,7},{6,4},{7,5},{8,10},{9,11},{10,... | collective-permute-start | bytes 122888 | tf_op jit(solution)/shard_map/ppermute | solution.py:19
  12.2 14.2 %collective-permute-start.1 = (f32[80,128]{1,0:T(8,128)S(1)}, f32[80,128]{1,0:T(8,128)S(1)}, u32[]{:S(2)}, u32[]{:S(2)}) collective-permute-start(f32[80,128]{1,0:T(8,128)S(1)} %add.42), channel_id=1, source_target_pairs={{0,1},{1,0},{2,3},{3,2},{4,5},{5,4},{6,7},{7,6},{8,9},{9,8},{10,11... | collective-permute-start | bytes 122888 | tf_op jit(solution)/shard_map/ppermute | solution.py:19
  26.4 5.6 %collective-permute-start.6 = (f32[80,128]{1,0:T(8,128)S(1)}, f32[80,128]{1,0:T(8,128)S(1)}, u32[]{:S(2)}, u32[]{:S(2)}) collective-permute-start(f32[80,128]{1,0:T(8,128)S(1)} %add_add_fusion.3), channel_id=1, source_target_pairs={{0,24},{4,28},{8,16},{12,20},{16,8},{20,12},{24,0},{28,4},{1,25},{... | collective-permute-start | bytes 122888 | tf_op jit(solution)/shard_map/ppermute | solution.py:19
  27.9 4.1 %collective-permute-start.5 = (f32[80,128]{1,0:T(8,128)S(1)}, f32[80,128]{1,0:T(8,128)S(1)}, u32[]{:S(2)}, u32[]{:S(2)}) collective-permute-start(f32[80,128]{1,0:T(8,128)S(1)} %add_add_fusion.3), channel_id=1, source_target_pairs={{0,16},{4,20},{8,24},{12,28},{16,0},{20,4},{24,8},{28,12},{1,17},{... | collective-permute-start | bytes 122888 | tf_op jit(solution)/shard_map/ppermute | solution.py:19
  28.7 4.0 %collective-permute-start.4 = (f32[80,128]{1,0:T(8,128)S(1)}, f32[80,128]{1,0:T(8,128)S(1)}, u32[]{:S(2)}, u32[]{:S(2)}) collective-permute-start(f32[80,128]{1,0:T(8,128)S(1)} %add_add_fusion.3), channel_id=1, source_target_pairs={{0,8},{4,12},{8,0},{12,4},{16,24},{20,28},{24,16},{28,20},{1,9},{5... | collective-permute-start | bytes 122888 | tf_op jit(solution)/shard_map/ppermute | solution.py:19
  29.9 9.9 %collective-permute-start.8 = (bf16[64,2304]{1,0:T(8,128)(2,1)S(1)}, bf16[64,2304]{1,0:T(8,128)(2,1)S(1)}, u32[]{:S(2)}, u32[]{:S(2)}) collective-permute-start(bf16[64,2304]{1,0:T(8,128)(2,1)S(1)} %slice_bitcast_fusion.1), channel_id=1, source_target_pairs={{0,1},{1,0},{2,3},{3,2},{4,5},{5,4},{6,7},{7,6},{8,9},{9,8},{10,11... | collective-permute-start | bytes 884744 | tf_op jit(solution)/shard_map/ppermute | solution.py:19
  30.7 13.6 %collective-permute-start.10 = (bf16[64,2304]{1,0:T(8,128)(2,1)S(1)}, bf16[64,2304]{1,0:T(8,128)(2,1)S(1)}, u32[]{:S(2)}, u32[]{:S(2)}) collective-permute-start(bf16[64,2304]{1,0:T(8,128)(2,1)S(1)} %collective-permute-done.9.refs_10_), channel_id=1, source_target_pairs={{0,1},{1,0},{2,3},{3,2},{4,5},{5,4},{6,7},{7,6},{8,9},{9,8},{10,11... | collective-permute-start | bytes 884744 | tf_op jit(solution)/shard_map/ppermute | solution.py:19
  32.8 1.3 %collective-permute-start.7 = (f32[80,128]{1,0:T(8,128)S(1)}, f32[80,128]{1,0:T(8,128)S(1)}, u32[]{:S(2)}, u32[]{:S(2)}) collective-permute-start(f32[80,128]{1,0:T(8,128)S(1)} %add_add_fusion.2.refs_2_), channel_id=1, source_target_pairs={{0,4},{4,0},{8,12},{12,8},{16,20},{20,16},{24,28},{28,24},{1,5},{5... | collective-permute-start | bytes 122888 | tf_op jit(solution)/shard_map/ppermute | solution.py:19
  50.2 3.1 %collective-permute-start.11 = (f32[80,128]{1,0:T(8,128)S(1)}, f32[80,128]{1,0:T(8,128)S(1)}, u32[]{:S(2)}, u32[]{:S(2)}) collective-permute-start(f32[80,128]{1,0:T(8,128)S(1)} %get-tuple-element.14), channel_id=1, source_target_pairs={{0,4},{4,0},{8,12},{12,8},{16,20},{20,16},{24,28},{28,24},{1,5},{5... | collective-permute-start | bytes 122888 | tf_op jit(solution)/shard_map/ppermute | solution.py:19
  50.3 24.7 %collective-permute-start.20 = (bf16[64,2304]{1,0:T(8,128)(2,1)S(1)}, bf16[64,2304]{1,0:T(8,128)(2,1)S(1)}, u32[]{:S(2)}, u32[]{:S(2)}) collective-permute-start(bf16[64,2304]{1,0:T(8,128)(2,1)S(1)} %slice_bitcast_fusion), channel_id=1, source_target_pairs={{0,2},{1,3},{2,0},{3,1},{4,6},{5,7},{6,4},{7,5},{8,10},{9,11},{10,... | collective-permute-start | bytes 884744 | tf_op jit(solution)/shard_map/ppermute | solution.py:19
  53.2 10.2 %collective-permute-start.14 = (f32[80,128]{1,0:T(8,128)S(1)}, f32[80,128]{1,0:T(8,128)S(1)}, u32[]{:S(2)}, u32[]{:S(2)}) collective-permute-start(f32[80,128]{1,0:T(8,128)S(1)} %add.49), channel_id=1, source_target_pairs={{0,3},{1,2},{2,1},{3,0},{4,7},{5,6},{6,5},{7,4},{8,11},{9,10},{10,... | collective-permute-start | bytes 122888 | tf_op jit(solution)/shard_map/ppermute | solution.py:19
  55.7 15.0 %collective-permute-start.13 = (f32[80,128]{1,0:T(8,128)S(1)}, f32[80,128]{1,0:T(8,128)S(1)}, u32[]{:S(2)}, u32[]{:S(2)}) collective-permute-start(f32[80,128]{1,0:T(8,128)S(1)} %add.49), channel_id=1, source_target_pairs={{0,2},{1,3},{2,0},{3,1},{4,6},{5,7},{6,4},{7,5},{8,10},{9,11},{10,... | collective-permute-start | bytes 122888 | tf_op jit(solution)/shard_map/ppermute | solution.py:19
  56.7 14.0 %collective-permute-start.12 = (f32[80,128]{1,0:T(8,128)S(1)}, f32[80,128]{1,0:T(8,128)S(1)}, u32[]{:S(2)}, u32[]{:S(2)}) collective-permute-start(f32[80,128]{1,0:T(8,128)S(1)} %add.49), channel_id=1, source_target_pairs={{0,1},{1,0},{2,3},{3,2},{4,5},{5,4},{6,7},{7,6},{8,9},{9,8},{10,11... | collective-permute-start | bytes 122888 | tf_op jit(solution)/shard_map/ppermute | solution.py:19
  70.7 5.6 %collective-permute-start.17 = (f32[80,128]{1,0:T(8,128)S(1)}, f32[80,128]{1,0:T(8,128)S(1)}, u32[]{:S(2)}, u32[]{:S(2)}) collective-permute-start(f32[80,128]{1,0:T(8,128)S(1)} %add_add_fusion.1), channel_id=1, source_target_pairs={{0,24},{4,28},{8,16},{12,20},{16,8},{20,12},{24,0},{28,4},{1,25},{... | collective-permute-start | bytes 122888 | tf_op jit(solution)/shard_map/ppermute | solution.py:19
  71.0 5.3 %collective-permute-start.16 = (f32[80,128]{1,0:T(8,128)S(1)}, f32[80,128]{1,0:T(8,128)S(1)}, u32[]{:S(2)}, u32[]{:S(2)}) collective-permute-start(f32[80,128]{1,0:T(8,128)S(1)} %add_add_fusion.1), channel_id=1, source_target_pairs={{0,16},{4,20},{8,24},{12,28},{16,0},{20,4},{24,8},{28,12},{1,17},{... | collective-permute-start | bytes 122888 | tf_op jit(solution)/shard_map/ppermute | solution.py:19
  72.2 4.1 %collective-permute-start.15 = (f32[80,128]{1,0:T(8,128)S(1)}, f32[80,128]{1,0:T(8,128)S(1)}, u32[]{:S(2)}, u32[]{:S(2)}) collective-permute-start(f32[80,128]{1,0:T(8,128)S(1)} %add_add_fusion.1), channel_id=1, source_target_pairs={{0,8},{4,12},{8,0},{12,4},{16,24},{20,28},{24,16},{28,20},{1,9},{5... | collective-permute-start | bytes 122888 | tf_op jit(solution)/shard_map/ppermute | solution.py:19
  74.3 9.9 %collective-permute-start.19 = (bf16[64,2304]{1,0:T(8,128)(2,1)S(1)}, bf16[64,2304]{1,0:T(8,128)(2,1)S(1)}, u32[]{:S(2)}, u32[]{:S(2)}) collective-permute-start(bf16[64,2304]{1,0:T(8,128)(2,1)S(1)} %slice_bitcast_fusion), channel_id=1, source_target_pairs={{0,1},{1,0},{2,3},{3,2},{4,5},{5,4},{6,7},{7,6},{8,9},{9,8},{10,11... | collective-permute-start | bytes 884744 | tf_op jit(solution)/shard_map/ppermute | solution.py:19
  75.0 13.5 %collective-permute-start.21 = (bf16[64,2304]{1,0:T(8,128)(2,1)S(1)}, bf16[64,2304]{1,0:T(8,128)(2,1)S(1)}, u32[]{:S(2)}, u32[]{:S(2)}) collective-permute-start(bf16[64,2304]{1,0:T(8,128)(2,1)S(1)} %collective-permute-done.20.refs_9_), channel_id=1, source_target_pairs={{0,1},{1,0},{2,3},{3,2},{4,5},{5,4},{6,7},{7,6},{8,9},{9,8},{10,11... | collective-permute-start | bytes 884744 | tf_op jit(solution)/shard_map/ppermute | solution.py:19
  76.3 12.2 %collective-permute-start.18 = (f32[80,128]{1,0:T(8,128)S(1)}, f32[80,128]{1,0:T(8,128)S(1)}, u32[]{:S(2)}, u32[]{:S(2)}) collective-permute-start(f32[80,128]{1,0:T(8,128)S(1)} %add_add_fusion.refs_0_), channel_id=1, source_target_pairs={{0,4},{4,0},{8,12},{12,8},{16,20},{20,16},{24,28},{28,24},{1,5},{5... | collective-permute-start | bytes 122888 | tf_op jit(solution)/shard_map/ppermute | solution.py:19

commit v5 on v4

--- a/solution.py
+++ b/solution.py
@@ -32,22 +32,45 @@
         bit *= 4
 
 
-def add_over(keep, send):
+def add_over(keep, send, lev_first):
     half = keep + swap(send, "slab", 1)
-    rounds = list(rounds_of("lev", 1)) + list(rounds_of("slab", 2))
+    rounds = [list(rounds_of("lev", 1)), list(rounds_of("slab", 2))]
+    rounds = sum(rounds if lev_first else rounds[::-1], [])
     for axis, distances in rounds:
         half = sum([swap(half, axis, d) for d in distances], half)
     return half, swap(half, "slab", 1)
 
 
-def rows_over(own, axis):
-    size = lax.axis_size(axis)
+def paired_rows(groups):
+    return groups == 4
+
+
+def swap_either(value, even_bit, odd_bit):
+    slabs, groups = lax.axis_size("slab"), lax.axis_size("lev")
+    pairs = [
+        (s * groups + l, s * groups + (l ^ (odd_bit if s & 1 else even_bit)))
+        for s in range(slabs)
+        for l in range(groups)
+    ]
+    return lax.ppermute(value, ("slab", "lev"), pairs)
+
+
+def rows_over(own):
+    size = lax.axis_size("lev")
+    if paired_rows(size):
+        far_even = swap_either(own, 2, 1)
+        far_odd = swap_either(own, 1, 2)
+        passed = jnp.where((lax.axis_index("slab") & 1) == 0, far_even, far_odd)
+        return [far_odd, far_even, swap(passed, "lev", 1)]
     shards = {0: own}
-    order = sorted(range(1, size), key=lambda p: (bin(p).count("1"), -p))
-    for p in order:
+    for p in row_order(size):
         low = p & -p
-        shards[p] = swap(shards[p ^ low], axis, low)
+        shards[p] = swap(shards[p ^ low], "lev", low)
     return [shards[p] for p in range(1, size)]
+
+
+def row_order(size):
+    return sorted(range(1, size), key=lambda p: (bin(p).count("1"), -p))
 
 
 def key_copy(place_ref, cell_ref, key_ref, key_smem, sem, sizes):
@@ -143,17 +166,23 @@
     split_halves(place_ref[1] & 1, sum_ref, keep_ref, send_ref)
 
 
-def regroup(value, lev_index, groups):
+def regroup(value, lev_index, side, groups):
     total = value.shape[1]
+    block = total // groups
     lane = lax.broadcasted_iota(jnp.int32, value.shape, 1)
     bit = 1
     while bit < groups:
-        span = (total // groups) * bit
+        span = block * bit
         other = jnp.where(
             (lane & span) != 0, pltpu.roll(value, span, 1), pltpu.roll(value, total - span, 1)
         )
         value = jnp.where((lev_index & bit) != 0, other, value)
         bit *= 2
+    if paired_rows(groups):
+        low, high = pltpu.roll(value, total - block, 1), pltpu.roll(value, block, 1)
+        inner = jnp.where(lane < 2 * block, low, high)
+        crossed = (side == 1) & (lane >= block) & (lane < 3 * block)
+        value = jnp.where(crossed, inner, value)
     return value
 
 
@@ -173,12 +202,12 @@
     total_var = spread + variance
     shrink = 1.0 / (1.0 + jnp.sqrt(variance / total_var))
     gain = ((value_ref[b : b + 1] - obs_mean) - deviation * shrink) / (total_var * (members - 1.0))
-    gain_ref[...] = regroup(gain, lev_index, groups).astype(jnp.bfloat16)
+    gain_ref[...] = regroup(gain, lev_index, side, groups).astype(jnp.bfloat16)
     pad = jnp.zeros((LANES - members, n_obs), jnp.float32)
-    dev_all = jnp.concatenate([regroup(deviation, lev_index, groups), pad], axis=0)
+    dev_all = jnp.concatenate([regroup(deviation, lev_index, side, groups), pad], axis=0)
     dev_ref[...] = dev_all.T[:, :members].astype(jnp.bfloat16)
     level_all = jnp.concatenate(
-        [regroup(level_ref[b], lev_index, groups), jnp.zeros((LANES - lev_rows, n_obs), jnp.float32)], axis=0
+        [regroup(level_ref[b], lev_index, side, groups), jnp.zeros((LANES - lev_rows, n_obs), jnp.float32)], axis=0
     ).T
     for l in range(lev_rows):
         level_b_ref[l] = jnp.broadcast_to(level_all[:, l : l + 1], (n_obs, LANES))
@@ -283,7 +312,7 @@
     dma = pltpu.SemaphoreType.DMA((lev_rows,))
     one_dma = pltpu.SemaphoreType.DMA
 
-    shards = [rows_over(loc_column[0], "lev")]
+    shards = [rows_over(loc_column[0])]
 
     keep, send = pl.pallas_call(
         with_place(functools.partial(prior_kernel, sizes)),
@@ -295,8 +324,8 @@
         name="cells",
     )(*place, *far(obs_frac, obs_cell, ensemble))
     later_rows, keep = lax.optimization_barrier((loc_column, keep))
-    shards.append(rows_over(later_rows[1], "lev"))
-    ours, theirs = add_over(keep, send)
+    shards.append(rows_over(later_rows[1]))
+    ours, theirs = add_over(keep, send, True)
 
     current, mean_first, keep, send = pl.pallas_call(
         with_place(functools.partial(first_kernel, groups, sizes)),
@@ -307,7 +336,7 @@
         compiler_params=pltpu.CompilerParams(vmem_limit_bytes=KERNEL_VMEM),
         name="block_first",
     )(*place, obs_frac, obs_cell, *near(ours, theirs), obs_value, obs_var, levels, *far(ensemble, loc_column), *near(*shards[0]))
-    ours, theirs = add_over(keep, send)
+    ours, theirs = add_over(keep, send, False)
 
     analysis, mean = pl.pallas_call(
         with_place(functools.partial(last_kernel, groups)),

time: 94.1 us -> 77 us (0.82)
  waiting for transfers between devices: 50.3 us -> 26.9 us
  starting transfers between devices: 27.2 us -> 33.5 us
    ppermute x22 -> x18, waiting for transfers between devices: 50.3 us -> 25.8 us  [swap(): return lax.ppermute(value, axis, [(i, i ^ bit) for i in range(size)])]
    ppermute x0 -> x4, starting transfers between devices: none -> 10.5 us  [swap_either(): return lax.ppermute(value, ('slab', 'lev'), pairs)]
    ppermute x22 -> x18, starting transfers between devices: 27.2 us -> 22.9 us  [swap(): return lax.ppermute(value, axis, [(i, i ^ bit) for i in range(size)])]
    ppermute x0 -> x4, waiting for transfers between devices: none -> 1.04 us  [swap_either(): return lax.ppermute(value, ('slab', 'lev'), pairs)]
  transfers between devices with their start and end apart: 22 -> 22, of which waited for: 11 -> 9; matrix products, arithmetic and copies ran while one was open for 0% -> 0% of each run, Pallas kernels for 0% -> 0%
where the time goes in v5:
time: 77 us; the launch traced here: 76.8 us
  starting transfers between devices  33.5 us (44%)
  waiting for transfers between devices  26.9 us (35%)
  Pallas kernels  15.4 us (20%)
  between operations  0.82 us (1%)
    ppermute x18, waiting for transfers between devices, swap(): return lax.ppermute(value, axis, [(i, i ^ bit) for i in range(size)])  25.8 us
    ppermute x18, starting transfers between devices, swap(): return lax.ppermute(value, axis, [(i, i ^ bit) for i in range(size)])  22.9 us
    ppermute x4, starting transfers between devices, swap_either(): return lax.ppermute(value, ('slab', 'lev'), pairs)  10.5 us
    pallas_call x1, Pallas kernels, on_device(): pl.pallas_call(with_place(functools.partial(first_kernel, groups, sizes))...  5.93 us
    pallas_call x1, Pallas kernels, on_device(): pl.pallas_call(with_place(functools.partial(last_kernel, groups)), out_sh...  5.4 us
    pallas_call x1, Pallas kernels, on_device(): pl.pallas_call(with_place(functools.partial(prior_kernel, sizes)), out_sh...  4.07 us
  transfers between devices with their start and end apart: 22, of which 9 were waited for; matrix products, arithmetic and copies ran while one was open for 0% of the time, Pallas kernels for 0%

profile of v5, /device:TPU:0, one launch (start us, length us, event | category | flops | bytes accessed | tf_op | source)
XLA Modules:
  0.0 76.8 jit_solution(12829580412242449)
XLA Ops:
  0.7 4.1 %cells.1 = (f32[80,128]{1,0:T(8,128)S(1)}, f32[80,128]{1,0:T(8,128)S(1)}) custom-call(s32[1]{0:T(128)} %bitcast.lev_ref, s32[1]{0:T(128)} %bitcast.1.slab_ref, f32[2,256]{1,0:T(2,128)} %refs_0_.3, s32[2,256]{1,0:T(2,128)} %refs_1_.3, f32[80,4,2304]{2,1,0:T(4,128)} %refs_7_.2), custom_call_target="tpu_custom_call" | custom-call | tf_op jit(solution)/shard_map/cells/pallas_call | solution.py:317
  4.8 0.1 collective-permute-start
  4.9 4.0 %collective-permute-start.9 = (bf16[64,2304]{1,0:T(8,128)(2,1)S(1)}, bf16[64,2304]{1,0:T(8,128)(2,1)S(1)}, u32[]{:S(2)}, u32[]{:S(2)}) collective-permute-start(bf16[64,2304]{1,0:T(8,128)(2,1)S(1)} %slice_bitcast_fusion.1), channel_id=1, source_target_pairs={{0,2},{1,3},{2,0},{3,1},{4,5},{5,4},{6,7},{7,6},{8,10},{9,11},{10,... | collective-permute-start | bytes 884744 | tf_op jit(solution)/shard_map/ppermute | solution.py:55
  8.9 1.7 %collective-permute-start.8 = (bf16[64,2304]{1,0:T(8,128)(2,1)S(1)}, bf16[64,2304]{1,0:T(8,128)(2,1)S(1)}, u32[]{:S(2)}, u32[]{:S(2)}) collective-permute-start(bf16[64,2304]{1,0:T(8,128)(2,1)S(1)} %slice_bitcast_fusion.1), channel_id=1, source_target_pairs={{0,1},{1,0},{2,3},{3,2},{4,6},{5,7},{6,4},{7,5},{8,9},{9,8},{10,11... | collective-permute-start | bytes 884744 | tf_op jit(solution)/shard_map/ppermute | solution.py:55
  10.6 0.5 collective-permute-start.3
  11.2 1.3 %collective-permute-start.2 = (f32[80,128]{1,0:T(8,128)S(1)}, f32[80,128]{1,0:T(8,128)S(1)}, u32[]{:S(2)}, u32[]{:S(2)}) collective-permute-start(f32[80,128]{1,0:T(8,128)S(1)} %add.42), channel_id=1, source_target_pairs={{0,2},{1,3},{2,0},{3,1},{4,6},{5,7},{6,4},{7,5},{8,10},{9,11},{10,... | collective-permute-start | bytes 122888 | tf_op jit(solution)/shard_map/ppermute | solution.py:19
  12.4 2.6 %collective-permute-start.1 = (f32[80,128]{1,0:T(8,128)S(1)}, f32[80,128]{1,0:T(8,128)S(1)}, u32[]{:S(2)}, u32[]{:S(2)}) collective-permute-start(f32[80,128]{1,0:T(8,128)S(1)} %add.42), channel_id=1, source_target_pairs={{0,1},{1,0},{2,3},{3,2},{4,5},{5,4},{6,7},{7,6},{8,9},{9,8},{10,11... | collective-permute-start | bytes 122888 | tf_op jit(solution)/shard_map/ppermute | solution.py:19
  15.1 10.4 %collective-permute-done.3 = f32[80,128]{1,0:T(8,128)S(1)} collective-permute-done((f32[80,128]{1,0:T(8,128)S(1)}, f32[80,128]{1,0:T(8,128)S(1)}, u32[]{:S(2)}, u32[]{:S(2)}) %collective-permute-start.3) | collective-permute-done | bytes 40992 | tf_op jit(solution)/shard_map/ppermute | solution.py:19
  25.5 2.1 %collective-permute-start.6 = (f32[80,128]{1,0:T(8,128)S(1)}, f32[80,128]{1,0:T(8,128)S(1)}, u32[]{:S(2)}, u32[]{:S(2)}) collective-permute-start(f32[80,128]{1,0:T(8,128)S(1)} %add_add_fusion.3), channel_id=1, source_target_pairs={{0,24},{4,28},{8,16},{12,20},{16,8},{20,12},{24,0},{28,4},{1,25},{... | collective-permute-start | bytes 122888 | tf_op jit(solution)/shard_map/ppermute | solution.py:19
  27.6 0.4 collective-permute-start.5
  28.1 1.0 %collective-permute-start.4 = (f32[80,128]{1,0:T(8,128)S(1)}, f32[80,128]{1,0:T(8,128)S(1)}, u32[]{:S(2)}, u32[]{:S(2)}) collective-permute-start(f32[80,128]{1,0:T(8,128)S(1)} %add_add_fusion.3), channel_id=1, source_target_pairs={{0,8},{4,12},{8,0},{12,4},{16,24},{20,28},{24,16},{28,20},{1,9},{5... | collective-permute-start | bytes 122888 | tf_op jit(solution)/shard_map/ppermute | solution.py:19
  29.1 2.0 %collective-permute-start.10 = (bf16[64,2304]{1,0:T(8,128)(2,1)S(1)}, bf16[64,2304]{1,0:T(8,128)(2,1)S(1)}, u32[]{:S(2)}, u32[]{:S(2)}) collective-permute-start(bf16[64,2304]{1,0:T(8,128)(2,1)S(1)} %broadcast_select_fusion.1), channel_id=1, source_target_pairs={{0,1},{1,0},{2,3},{3,2},{4,5},{5,4},{6,7},{7,6},{8,9},{9,8},{10,11... | collective-permute-start | bytes 884744 | tf_op jit(solution)/shard_map/ppermute | solution.py:19
  31.1 0.6 collective-permute-done.5
  31.8 0.3 collective-permute-done.4
  32.2 1.2 %collective-permute-done.7.refs_3_ = f32[80,128]{1,0:T(8,128)S(1)} collective-permute-done((f32[80,128]{1,0:T(8,128)S(1)}, f32[80,128]{1,0:T(8,128)S(1)}, u32[]{:S(2)}, u32[]{:S(2)}) %collective-permute-start.7) | collective-permute-done | bytes 40992 | tf_op jit(solution)/shard_map/ppermute | solution.py:19
  33.4 4.8 %collective-permute-done.10.refs_11_ = bf16[64,2304]{1,0:T(8,128)(2,1)S(1)} collective-permute-done((bf16[64,2304]{1,0:T(8,128)(2,1)S(1)}, bf16[64,2304]{1,0:T(8,128)(2,1)S(1)}, u32[]{:S(2)}, u32[]{:S(2)}) %collective-permute-start.10) | collective-permute-done | bytes 294944 | tf_op jit(solution)/shard_map/ppermute | solution.py:19
  38.2 5.9 %block_first.1 = (f32[4,80,2304]{2,1,0:T(8,128)S(1)}, f32[1,256]{1,0:T(1,128)S(1)}, f32[80,128]{1,0:T(8,128)S(1)}, f32[80,128]{1,0:T(8,128)S(1)}) custom-call(s32[1]{0:T(128)} %bitcast.lev_ref, s32[1]{0:T(128)} %bitcast.1.slab_ref, f32[2,256]{1,0:T(2,128)S(1)} %copy-done.3, s32[2,256]{1,0:T(2,128)S(1)} %copy-done.4, f32[80,128]{1,0:T(8,128)S(1)} %add_add_fusion.2.refs_2_, ...), custom_call_target="tpu_custom_call" | custom-call | tf_op jit(solution)/shard_map/block_first/pallas_call | solution.py:330
  44.3 2.9 %collective-permute-start.20 = (bf16[64,2304]{1,0:T(8,128)(2,1)S(1)}, bf16[64,2304]{1,0:T(8,128)(2,1)S(1)}, u32[]{:S(2)}, u32[]{:S(2)}) collective-permute-start(bf16[64,2304]{1,0:T(8,128)(2,1)S(1)} %slice_bitcast_fusion), channel_id=1, source_target_pairs={{0,2},{1,3},{2,0},{3,1},{4,5},{5,4},{6,7},{7,6},{8,10},{9,11},{10,... | collective-permute-start | bytes 884744 | tf_op jit(solution)/shard_map/ppermute | solution.py:55
  47.2 1.9 %collective-permute-start.19 = (bf16[64,2304]{1,0:T(8,128)(2,1)S(1)}, bf16[64,2304]{1,0:T(8,128)(2,1)S(1)}, u32[]{:S(2)}, u32[]{:S(2)}) collective-permute-start(bf16[64,2304]{1,0:T(8,128)(2,1)S(1)} %slice_bitcast_fusion), channel_id=1, source_target_pairs={{0,1},{1,0},{2,3},{3,2},{4,6},{5,7},{6,4},{7,5},{8,9},{9,8},{10,11... | collective-permute-start | bytes 884744 | tf_op jit(solution)/shard_map/ppermute | solution.py:55
  49.1 0.1 collective-permute-start.14
  49.2 1.0 %collective-permute-start.13 = (f32[80,128]{1,0:T(8,128)S(1)}, f32[80,128]{1,0:T(8,128)S(1)}, u32[]{:S(2)}, u32[]{:S(2)}) collective-permute-start(f32[80,128]{1,0:T(8,128)S(1)} %add.49), channel_id=1, source_target_pairs={{0,16},{4,20},{8,24},{12,28},{16,0},{20,4},{24,8},{28,12},{1,17},{... | collective-permute-start | bytes 122888 | tf_op jit(solution)/shard_map/ppermute | solution.py:19
  50.2 2.5 %collective-permute-start.12 = (f32[80,128]{1,0:T(8,128)S(1)}, f32[80,128]{1,0:T(8,128)S(1)}, u32[]{:S(2)}, u32[]{:S(2)}) collective-permute-start(f32[80,128]{1,0:T(8,128)S(1)} %add.49), channel_id=1, source_target_pairs={{0,8},{4,12},{8,0},{12,4},{16,24},{20,28},{24,16},{28,20},{1,9},{5... | collective-permute-start | bytes 122888 | tf_op jit(solution)/shard_map/ppermute | solution.py:19
  52.6 1.4 %collective-permute-done.14 = f32[80,128]{1,0:T(8,128)S(1)} collective-permute-done((f32[80,128]{1,0:T(8,128)S(1)}, f32[80,128]{1,0:T(8,128)S(1)}, u32[]{:S(2)}, u32[]{:S(2)}) %collective-permute-start.14) | collective-permute-done | bytes 40992 | tf_op jit(solution)/shard_map/ppermute | solution.py:19
  54.1 0.6 collective-permute-done.12
  54.6 0.5 collective-permute-start.17
  55.2 1.1 %collective-permute-start.16 = (f32[80,128]{1,0:T(8,128)S(1)}, f32[80,128]{1,0:T(8,128)S(1)}, u32[]{:S(2)}, u32[]{:S(2)}) collective-permute-start(f32[80,128]{1,0:T(8,128)S(1)} %add_add_fusion.1), channel_id=1, source_target_pairs={{0,2},{1,3},{2,0},{3,1},{4,6},{5,7},{6,4},{7,5},{8,10},{9,11},{10,... | collective-permute-start | bytes 122888 | tf_op jit(solution)/shard_map/ppermute | solution.py:19
  56.3 2.8 %collective-permute-start.15 = (f32[80,128]{1,0:T(8,128)S(1)}, f32[80,128]{1,0:T(8,128)S(1)}, u32[]{:S(2)}, u32[]{:S(2)}) collective-permute-start(f32[80,128]{1,0:T(8,128)S(1)} %add_add_fusion.1), channel_id=1, source_target_pairs={{0,1},{1,0},{2,3},{3,2},{4,5},{5,4},{6,7},{7,6},{8,9},{9,8},{10,11... | collective-permute-start | bytes 122888 | tf_op jit(solution)/shard_map/ppermute | solution.py:19
  59.1 1.0 %collective-permute-done.19.refs_8_ = bf16[64,2304]{1,0:T(8,128)(2,1)S(1)} collective-permute-done((bf16[64,2304]{1,0:T(8,128)(2,1)S(1)}, bf16[64,2304]{1,0:T(8,128)(2,1)S(1)}, u32[]{:S(2)}, u32[]{:S(2)}) %collective-permute-start.19) | collective-permute-done | bytes 294944 | tf_op jit(solution)/shard_map/ppermute | solution.py:55
  60.2 4.3 %collective-permute-start.21 = (bf16[64,2304]{1,0:T(8,128)(2,1)S(1)}, bf16[64,2304]{1,0:T(8,128)(2,1)S(1)}, u32[]{:S(2)}, u32[]{:S(2)}) collective-permute-start(bf16[64,2304]{1,0:T(8,128)(2,1)S(1)} %broadcast_select_fusion), channel_id=1, source_target_pairs={{0,1},{1,0},{2,3},{3,2},{4,5},{5,4},{6,7},{7,6},{8,9},{9,8},{10,11... | collective-permute-start | bytes 884744 | tf_op jit(solution)/shard_map/ppermute | solution.py:19
  64.5 0.4 collective-permute-start.18
  64.9 6.5 %collective-permute-done.21.refs_10_ = bf16[64,2304]{1,0:T(8,128)(2,1)S(1)} collective-permute-done((bf16[64,2304]{1,0:T(8,128)(2,1)S(1)}, bf16[64,2304]{1,0:T(8,128)(2,1)S(1)}, u32[]{:S(2)}, u32[]{:S(2)}) %collective-permute-start.21) | collective-permute-done | bytes 294944 | tf_op jit(solution)/shard_map/ppermute | solution.py:19
  71.4 5.4 %block_last.1 = (f32[80,4,2304]{2,1,0:T(4,128)}, f32[2,256]{1,0:T(2,128)}) custom-call(s32[1]{0:T(128)} %bitcast.lev_ref, s32[1]{0:T(128)} %bitcast.1.slab_ref, f32[80,128]{1,0:T(8,128)S(1)} %add_add_fusion.refs_0_, f32[80,128]{1,0:T(8,128)S(1)} %collective-permute-done.18.refs_1_, f32[2,256]{1,0:T(2,128)S(1)} %copy-done.1, f32[2,256]{1,0:T(2,128)S(1)} %copy-done.2, ...), custom_call_target="tpu_custom_call" | custom-call | tf_op jit(solution)/shard_map/block_last/pallas_call | solution.py:341
  (39 shorter events, 0.4 us)
Async XLA Ops:
  0.6 37.5 %copy-start.3 = (f32[2,256]{1,0:T(2,128)S(1)}, f32[2,256]{1,0:T(2,128)}, u32[]{:S(2)}) copy-start(f32[2,256]{1,0:T(2,128)} %refs_0_.3) | copy-start | bytes 6148
  0.6 37.5 %copy-start.4 = (s32[2,256]{1,0:T(2,128)S(1)}, s32[2,256]{1,0:T(2,128)}, u32[]{:S(2)}) copy-start(s32[2,256]{1,0:T(2,128)} %refs_1_.3) | copy-start | bytes 6148
  0.7 4.2 %copy-start.5 = (bf16[2,64,2304]{2,1,0:T(8,128)(2,1)S(1)}, bf16[2,64,2304]{2,1,0:T(8,128)(2,1)}, u32[]{:S(2)}) copy-start(bf16[2,64,2304]{2,1,0:T(8,128)(2,1)} %refs_7_.3) | copy-start | bytes 1769476
  0.7 37.5 %copy-start.2 = (f32[2,256]{1,0:T(2,128)S(1)}, f32[2,256]{1,0:T(2,128)}, u32[]{:S(2)}) copy-start(f32[2,256]{1,0:T(2,128)} %refs_3_.1) | copy-start | bytes 6148
  0.7 37.5 %copy-start.1 = (f32[2,256]{1,0:T(2,128)S(1)}, f32[2,256]{1,0:T(2,128)}, u32[]{:S(2)}) copy-start(f32[2,256]{1,0:T(2,128)} %refs_2_.3) | copy-start | bytes 6148
  0.7 37.5 %copy-start = (f32[2,256,4]{1,2,0:T(4,128)S(1)}, f32[2,256,4]{1,2,0:T(4,128)}, u32[]{:S(2)}) copy-start(f32[2,256,4]{1,2,0:T(4,128)} %param.13) | copy-start | bytes 24580
  4.8 5.8 %collective-permute-start = (f32[80,128]{1,0:T(8,128)S(1)}, f32[80,128]{1,0:T(8,128)S(1)}, u32[]{:S(2)}, u32[]{:S(2)}) collective-permute-start(f32[80,128]{1,0:T(8,128)S(1)} %get-tuple-element.12), channel_id=1, source_target_pairs={{0,4},{4,0},{8,12},{12,8},{16,20},{20,16},{24,28},{28,24},{1,5},{5... | collective-permute-start | bytes 122888 | tf_op jit(solution)/shard_map/ppermute | solution.py:19
  4.9 24.2 %collective-permute-start.9 = (bf16[64,2304]{1,0:T(8,128)(2,1)S(1)}, bf16[64,2304]{1,0:T(8,128)(2,1)S(1)}, u32[]{:S(2)}, u32[]{:S(2)}) collective-permute-start(bf16[64,2304]{1,0:T(8,128)(2,1)S(1)} %slice_bitcast_fusion.1), channel_id=1, source_target_pairs={{0,2},{1,3},{2,0},{3,1},{4,5},{5,4},{6,7},{7,6},{8,10},{9,11},{10,... | collective-permute-start | bytes 884744 | tf_op jit(solution)/shard_map/ppermute | solution.py:55
  8.9 20.2 %collective-permute-start.8 = (bf16[64,2304]{1,0:T(8,128)(2,1)S(1)}, bf16[64,2304]{1,0:T(8,128)(2,1)S(1)}, u32[]{:S(2)}, u32[]{:S(2)}) collective-permute-start(bf16[64,2304]{1,0:T(8,128)(2,1)S(1)} %slice_bitcast_fusion.1), channel_id=1, source_target_pairs={{0,1},{1,0},{2,3},{3,2},{4,6},{5,7},{6,4},{7,5},{8,9},{9,8},{10,11... | collective-permute-start | bytes 884744 | tf_op jit(solution)/shard_map/ppermute | solution.py:55
  10.6 33.6 %copy-start.6 = (bf16[2,64,2304]{2,1,0:T(8,128)(2,1)S(1)}, bf16[2,64,2304]{2,1,0:T(8,128)(2,1)}, u32[]{:S(2)}) copy-start(bf16[2,64,2304]{2,1,0:T(8,128)(2,1)} %refs_7_.3) | copy-start | bytes 1769476
  10.6 14.9 %collective-permute-start.3 = (f32[80,128]{1,0:T(8,128)S(1)}, f32[80,128]{1,0:T(8,128)S(1)}, u32[]{:S(2)}, u32[]{:S(2)}) collective-permute-start(f32[80,128]{1,0:T(8,128)S(1)} %add.42), channel_id=1, source_target_pairs={{0,3},{1,2},{2,1},{3,0},{4,7},{5,6},{6,5},{7,4},{8,11},{9,10},{10,... | collective-permute-start | bytes 122888 | tf_op jit(solution)/shard_map/ppermute | solution.py:19
  11.2 14.3 %collective-permute-start.2 = (f32[80,128]{1,0:T(8,128)S(1)}, f32[80,128]{1,0:T(8,128)S(1)}, u32[]{:S(2)}, u32[]{:S(2)}) collective-permute-start(f32[80,128]{1,0:T(8,128)S(1)} %add.42), channel_id=1, source_target_pairs={{0,2},{1,3},{2,0},{3,1},{4,6},{5,7},{6,4},{7,5},{8,10},{9,11},{10,... | collective-permute-start | bytes 122888 | tf_op jit(solution)/shard_map/ppermute | solution.py:19
  12.4 13.1 %collective-permute-start.1 = (f32[80,128]{1,0:T(8,128)S(1)}, f32[80,128]{1,0:T(8,128)S(1)}, u32[]{:S(2)}, u32[]{:S(2)}) collective-permute-start(f32[80,128]{1,0:T(8,128)S(1)} %add.42), channel_id=1, source_target_pairs={{0,1},{1,0},{2,3},{3,2},{4,5},{5,4},{6,7},{7,6},{8,9},{9,8},{10,11... | collective-permute-start | bytes 122888 | tf_op jit(solution)/shard_map/ppermute | solution.py:19
  25.5 5.6 %collective-permute-start.6 = (f32[80,128]{1,0:T(8,128)S(1)}, f32[80,128]{1,0:T(8,128)S(1)}, u32[]{:S(2)}, u32[]{:S(2)}) collective-permute-start(f32[80,128]{1,0:T(8,128)S(1)} %add_add_fusion.3), channel_id=1, source_target_pairs={{0,24},{4,28},{8,16},{12,20},{16,8},{20,12},{24,0},{28,4},{1,25},{... | collective-permute-start | bytes 122888 | tf_op jit(solution)/shard_map/ppermute | solution.py:19
  27.6 4.1 %collective-permute-start.5 = (f32[80,128]{1,0:T(8,128)S(1)}, f32[80,128]{1,0:T(8,128)S(1)}, u32[]{:S(2)}, u32[]{:S(2)}) collective-permute-start(f32[80,128]{1,0:T(8,128)S(1)} %add_add_fusion.3), channel_id=1, source_target_pairs={{0,16},{4,20},{8,24},{12,28},{16,0},{20,4},{24,8},{28,12},{1,17},{... | collective-permute-start | bytes 122888 | tf_op jit(solution)/shard_map/ppermute | solution.py:19
  28.1 4.0 %collective-permute-start.4 = (f32[80,128]{1,0:T(8,128)S(1)}, f32[80,128]{1,0:T(8,128)S(1)}, u32[]{:S(2)}, u32[]{:S(2)}) collective-permute-start(f32[80,128]{1,0:T(8,128)S(1)} %add_add_fusion.3), channel_id=1, source_target_pairs={{0,8},{4,12},{8,0},{12,4},{16,24},{20,28},{24,16},{28,20},{1,9},{5... | collective-permute-start | bytes 122888 | tf_op jit(solution)/shard_map/ppermute | solution.py:19
  29.1 9.1 %collective-permute-start.10 = (bf16[64,2304]{1,0:T(8,128)(2,1)S(1)}, bf16[64,2304]{1,0:T(8,128)(2,1)S(1)}, u32[]{:S(2)}, u32[]{:S(2)}) collective-permute-start(bf16[64,2304]{1,0:T(8,128)(2,1)S(1)} %broadcast_select_fusion.1), channel_id=1, source_target_pairs={{0,1},{1,0},{2,3},{3,2},{4,5},{5,4},{6,7},{7,6},{8,9},{9,8},{10,11... | collective-permute-start | bytes 884744 | tf_op jit(solution)/shard_map/ppermute | solution.py:19
  32.1 1.3 %collective-permute-start.7 = (f32[80,128]{1,0:T(8,128)S(1)}, f32[80,128]{1,0:T(8,128)S(1)}, u32[]{:S(2)}, u32[]{:S(2)}) collective-permute-start(f32[80,128]{1,0:T(8,128)S(1)} %add_add_fusion.2.refs_2_), channel_id=1, source_target_pairs={{0,4},{4,0},{8,12},{12,8},{16,20},{20,16},{24,28},{28,24},{1,5},{5... | collective-permute-start | bytes 122888 | tf_op jit(solution)/shard_map/ppermute | solution.py:19
  44.1 4.9 %collective-permute-start.11 = (f32[80,128]{1,0:T(8,128)S(1)}, f32[80,128]{1,0:T(8,128)S(1)}, u32[]{:S(2)}, u32[]{:S(2)}) collective-permute-start(f32[80,128]{1,0:T(8,128)S(1)} %get-tuple-element.14), channel_id=1, source_target_pairs={{0,4},{4,0},{8,12},{12,8},{16,20},{20,16},{24,28},{28,24},{1,5},{5... | collective-permute-start | bytes 122888 | tf_op jit(solution)/shard_map/ppermute | solution.py:19
  44.3 14.8 %collective-permute-start.20 = (bf16[64,2304]{1,0:T(8,128)(2,1)S(1)}, bf16[64,2304]{1,0:T(8,128)(2,1)S(1)}, u32[]{:S(2)}, u32[]{:S(2)}) collective-permute-start(bf16[64,2304]{1,0:T(8,128)(2,1)S(1)} %slice_bitcast_fusion), channel_id=1, source_target_pairs={{0,2},{1,3},{2,0},{3,1},{4,5},{5,4},{6,7},{7,6},{8,10},{9,11},{10,... | collective-permute-start | bytes 884744 | tf_op jit(solution)/shard_map/ppermute | solution.py:55
  47.2 13.0 %collective-permute-start.19 = (bf16[64,2304]{1,0:T(8,128)(2,1)S(1)}, bf16[64,2304]{1,0:T(8,128)(2,1)S(1)}, u32[]{:S(2)}, u32[]{:S(2)}) collective-permute-start(bf16[64,2304]{1,0:T(8,128)(2,1)S(1)} %slice_bitcast_fusion), channel_id=1, source_target_pairs={{0,1},{1,0},{2,3},{3,2},{4,6},{5,7},{6,4},{7,5},{8,9},{9,8},{10,11... | collective-permute-start | bytes 884744 | tf_op jit(solution)/shard_map/ppermute | solution.py:55
  49.1 5.0 %collective-permute-start.14 = (f32[80,128]{1,0:T(8,128)S(1)}, f32[80,128]{1,0:T(8,128)S(1)}, u32[]{:S(2)}, u32[]{:S(2)}) collective-permute-start(f32[80,128]{1,0:T(8,128)S(1)} %add.49), channel_id=1, source_target_pairs={{0,24},{4,28},{8,16},{12,20},{16,8},{20,12},{24,0},{28,4},{1,25},{... | collective-permute-start | bytes 122888 | tf_op jit(solution)/shard_map/ppermute | solution.py:19
  49.2 4.9 %collective-permute-start.13 = (f32[80,128]{1,0:T(8,128)S(1)}, f32[80,128]{1,0:T(8,128)S(1)}, u32[]{:S(2)}, u32[]{:S(2)}) collective-permute-start(f32[80,128]{1,0:T(8,128)S(1)} %add.49), channel_id=1, source_target_pairs={{0,16},{4,20},{8,24},{12,28},{16,0},{20,4},{24,8},{28,12},{1,17},{... | collective-permute-start | bytes 122888 | tf_op jit(solution)/shard_map/ppermute | solution.py:19
  50.2 4.4 %collective-permute-start.12 = (f32[80,128]{1,0:T(8,128)S(1)}, f32[80,128]{1,0:T(8,128)S(1)}, u32[]{:S(2)}, u32[]{:S(2)}) collective-permute-start(f32[80,128]{1,0:T(8,128)S(1)} %add.49), channel_id=1, source_target_pairs={{0,8},{4,12},{8,0},{12,4},{16,24},{20,28},{24,16},{28,20},{1,9},{5... | collective-permute-start | bytes 122888 | tf_op jit(solution)/shard_map/ppermute | solution.py:19
  54.6 9.8 %collective-permute-start.17 = (f32[80,128]{1,0:T(8,128)S(1)}, f32[80,128]{1,0:T(8,128)S(1)}, u32[]{:S(2)}, u32[]{:S(2)}) collective-permute-start(f32[80,128]{1,0:T(8,128)S(1)} %add_add_fusion.1), channel_id=1, source_target_pairs={{0,3},{1,2},{2,1},{3,0},{4,7},{5,6},{6,5},{7,4},{8,11},{9,10},{10,... | collective-permute-start | bytes 122888 | tf_op jit(solution)/shard_map/ppermute | solution.py:19
  55.2 9.3 %collective-permute-start.16 = (f32[80,128]{1,0:T(8,128)S(1)}, f32[80,128]{1,0:T(8,128)S(1)}, u32[]{:S(2)}, u32[]{:S(2)}) collective-permute-start(f32[80,128]{1,0:T(8,128)S(1)} %add_add_fusion.1), channel_id=1, source_target_pairs={{0,2},{1,3},{2,0},{3,1},{4,6},{5,7},{6,4},{7,5},{8,10},{9,11},{10,... | collective-permute-start | bytes 122888 | tf_op jit(solution)/shard_map/ppermute | solution.py:19
  56.3 8.2 %collective-permute-start.15 = (f32[80,128]{1,0:T(8,128)S(1)}, f32[80,128]{1,0:T(8,128)S(1)}, u32[]{:S(2)}, u32[]{:S(2)}) collective-permute-start(f32[80,128]{1,0:T(8,128)S(1)} %add_add_fusion.1), channel_id=1, source_target_pairs={{0,1},{1,0},{2,3},{3,2},{4,5},{5,4},{6,7},{7,6},{8,9},{9,8},{10,11... | collective-permute-start | bytes 122888 | tf_op jit(solution)/shard_map/ppermute | solution.py:19
  60.2 11.2 %collective-permute-start.21 = (bf16[64,2304]{1,0:T(8,128)(2,1)S(1)}, bf16[64,2304]{1,0:T(8,128)(2,1)S(1)}, u32[]{:S(2)}, u32[]{:S(2)}) collective-permute-start(bf16[64,2304]{1,0:T(8,128)(2,1)S(1)} %broadcast_select_fusion), channel_id=1, source_target_pairs={{0,1},{1,0},{2,3},{3,2},{4,5},{5,4},{6,7},{7,6},{8,9},{9,8},{10,11... | collective-permute-start | bytes 884744 | tf_op jit(solution)/shard_map/ppermute | solution.py:19
  64.5 6.9 %collective-permute-start.18 = (f32[80,128]{1,0:T(8,128)S(1)}, f32[80,128]{1,0:T(8,128)S(1)}, u32[]{:S(2)}, u32[]{:S(2)}) collective-permute-start(f32[80,128]{1,0:T(8,128)S(1)} %add_add_fusion.refs_0_), channel_id=1, source_target_pairs={{0,4},{4,0},{8,12},{12,8},{16,20},{20,16},{24,28},{28,24},{1,5},{5... | collective-permute-start | bytes 122888 | tf_op jit(solution)/shard_map/ppermute | solution.py:19

commit v6 on v5

--- a/solution.py
+++ b/solution.py
@@ -47,10 +47,9 @@
 
 def swap_either(value, even_bit, odd_bit):
     slabs, groups = lax.axis_size("slab"), lax.axis_size("lev")
+    bits = [odd_bit if s & 1 else even_bit for s in range(slabs)]
     pairs = [
-        (s * groups + l, s * groups + (l ^ (odd_bit if s & 1 else even_bit)))
-        for s in range(slabs)
-        for l in range(groups)
+        (s * groups + l, s * groups + (l ^ bits[s])) for s in range(slabs) for l in range(groups) if bits[s]
     ]
     return lax.ppermute(value, ("slab", "lev"), pairs)
 
@@ -60,8 +59,10 @@
     if paired_rows(size):
         far_even = swap_either(own, 2, 1)
         far_odd = swap_either(own, 1, 2)
-        passed = jnp.where((lax.axis_index("slab") & 1) == 0, far_even, far_odd)
-        return [far_odd, far_even, swap(passed, "lev", 1)]
+        even = (lax.axis_index("slab") & 1) == 0
+        on_even = swap_either(far_even, 1, 0)
+        on_odd = swap_either(jnp.where(even, own, far_odd), 0, 1)
+        return [far_odd, far_even, jnp.where(even, on_even, on_odd)]
     shards = {0: own}
     for p in row_order(size):
         low = p & -p

time: 77 us -> 76.2 us (0.990)
  waiting for transfers between devices: 26.9 us -> 18.9 us
  starting transfers between devices: 33.5 us -> 40.5 us
    ppermute x18 -> x16, waiting for transfers between devices: 25.8 us -> 9.15 us  [swap(): return lax.ppermute(value, axis, [(i, i ^ bit) for i in range(size)])]
    ppermute x4 -> x8, waiting for transfers between devices: 1.04 us -> 9.74 us  [swap_either(): return lax.ppermute(value, ('slab', 'lev'), pairs)]
    ppermute x4 -> x8, starting transfers between devices: 10.5 us -> 18.2 us  [swap_either(): return lax.ppermute(value, ('slab', 'lev'), pairs)]
    ppermute x18 -> x16, starting transfers between devices: 22.9 us -> 22.2 us  [swap(): return lax.ppermute(value, axis, [(i, i ^ bit) for i in range(size)])]
  transfers between devices with their start and end apart: 22 -> 24, of which waited for: 9 -> 7; matrix products, arithmetic and copies ran while one was open for 0% -> 0% of each run, Pallas kernels for 0% -> 8%
where the time goes in v6:
time: 76.2 us; the launch traced here: 75.9 us
  starting transfers between devices  40.5 us (53%)
  waiting for transfers between devices  18.9 us (25%)
  Pallas kernels  15.3 us (20%)
  between operations  0.93 us (1%)
    ppermute x16, starting transfers between devices, swap(): return lax.ppermute(value, axis, [(i, i ^ bit) for i in range(size)])  22.2 us
    ppermute x8, starting transfers between devices, swap_either(): return lax.ppermute(value, ('slab', 'lev'), pairs)  18.2 us
    ppermute x8, waiting for transfers between devices, swap_either(): return lax.ppermute(value, ('slab', 'lev'), pairs)  9.74 us
    ppermute x16, waiting for transfers between devices, swap(): return lax.ppermute(value, axis, [(i, i ^ bit) for i in range(size)])  9.15 us
    pallas_call x1, Pallas kernels, on_device(): pl.pallas_call(with_place(functools.partial(first_kernel, groups, sizes))...  5.93 us
    pallas_call x1, Pallas kernels, on_device(): pl.pallas_call(with_place(functools.partial(last_kernel, groups)), out_sh...  5.33 us
    pallas_call x1, Pallas kernels, on_device(): pl.pallas_call(with_place(functools.partial(prior_kernel, sizes)), out_sh...  4.08 us
  transfers between devices with their start and end apart: 24, of which 7 were waited for; matrix products, arithmetic and copies ran while one was open for 0% of the time, Pallas kernels for 8%

profile of v6, /device:TPU:0, one launch (start us, length us, event | category | flops | bytes accessed | tf_op | source)
XLA Modules:
  0.0 75.9 jit_solution(14799618202794990592)
XLA Ops:
  0.7 4.1 %cells.1 = (f32[80,128]{1,0:T(8,128)S(1)}, f32[80,128]{1,0:T(8,128)S(1)}) custom-call(s32[1]{0:T(128)} %bitcast.lev_ref, s32[1]{0:T(128)} %bitcast.1.slab_ref, f32[2,256]{1,0:T(2,128)} %refs_0_.3, s32[2,256]{1,0:T(2,128)} %refs_1_.3, f32[80,4,2304]{2,1,0:T(4,128)} %refs_7_.2), custom_call_target="tpu_custom_call" | custom-call | tf_op jit(solution)/shard_map/cells/pallas_call | solution.py:318
  4.8 0.1 collective-permute-start
  4.9 3.1 %collective-permute-start.8 = (bf16[64,2304]{1,0:T(8,128)(2,1)S(1)}, bf16[64,2304]{1,0:T(8,128)(2,1)S(1)}, u32[]{:S(2)}, u32[]{:S(2)}) collective-permute-start(bf16[64,2304]{1,0:T(8,128)(2,1)S(1)} %slice_bitcast_fusion.1), channel_id=1, source_target_pairs={{0,1},{1,0},{2,3},{3,2},{4,6},{5,7},{6,4},{7,5},{8,9},{9,8},{10,11... | collective-permute-start | bytes 884744 | tf_op jit(solution)/shard_map/ppermute | solution.py:54
  8.0 3.1 %collective-permute-start.3 = (f32[80,128]{1,0:T(8,128)S(1)}, f32[80,128]{1,0:T(8,128)S(1)}, u32[]{:S(2)}, u32[]{:S(2)}) collective-permute-start(f32[80,128]{1,0:T(8,128)S(1)} %add.42), channel_id=1, source_target_pairs={{0,3},{1,2},{2,1},{3,0},{4,7},{5,6},{6,5},{7,4},{8,11},{9,10},{10,... | collective-permute-start | bytes 122888 | tf_op jit(solution)/shard_map/ppermute | solution.py:19
  11.2 1.3 %collective-permute-start.1 = (f32[80,128]{1,0:T(8,128)S(1)}, f32[80,128]{1,0:T(8,128)S(1)}, u32[]{:S(2)}, u32[]{:S(2)}) collective-permute-start(f32[80,128]{1,0:T(8,128)S(1)} %add.42), channel_id=1, source_target_pairs={{0,1},{1,0},{2,3},{3,2},{4,5},{5,4},{6,7},{7,6},{8,9},{9,8},{10,11... | collective-permute-start | bytes 122888 | tf_op jit(solution)/shard_map/ppermute | solution.py:19
  12.5 1.7 %collective-permute-start.9 = (bf16[64,2304]{1,0:T(8,128)(2,1)S(1)}, bf16[64,2304]{1,0:T(8,128)(2,1)S(1)}, u32[]{:S(2)}, u32[]{:S(2)}) collective-permute-start(bf16[64,2304]{1,0:T(8,128)(2,1)S(1)} %slice_bitcast_fusion.1), channel_id=1, source_target_pairs={{0,2},{1,3},{2,0},{3,1},{4,5},{5,4},{6,7},{7,6},{8,10},{9,11},{10,... | collective-permute-start | bytes 884744 | tf_op jit(solution)/shard_map/ppermute | solution.py:54
  14.2 4.9 %collective-permute-done.3 = f32[80,128]{1,0:T(8,128)S(1)} collective-permute-done((f32[80,128]{1,0:T(8,128)S(1)}, f32[80,128]{1,0:T(8,128)S(1)}, u32[]{:S(2)}, u32[]{:S(2)}) %collective-permute-start.3) | collective-permute-done | bytes 40992 | tf_op jit(solution)/shard_map/ppermute | solution.py:19
  19.1 1.6 %collective-permute-start.6 = (f32[80,128]{1,0:T(8,128)S(1)}, f32[80,128]{1,0:T(8,128)S(1)}, u32[]{:S(2)}, u32[]{:S(2)}) collective-permute-start(f32[80,128]{1,0:T(8,128)S(1)} %add_add_fusion.3), channel_id=1, source_target_pairs={{0,24},{4,28},{8,16},{12,20},{16,8},{20,12},{24,0},{28,4},{1,25},{... | collective-permute-start | bytes 122888 | tf_op jit(solution)/shard_map/ppermute | solution.py:19
  20.6 0.8 %collective-permute-start.5 = (f32[80,128]{1,0:T(8,128)S(1)}, f32[80,128]{1,0:T(8,128)S(1)}, u32[]{:S(2)}, u32[]{:S(2)}) collective-permute-start(f32[80,128]{1,0:T(8,128)S(1)} %add_add_fusion.3), channel_id=1, source_target_pairs={{0,16},{4,20},{8,24},{12,28},{16,0},{20,4},{24,8},{28,12},{1,17},{... | collective-permute-start | bytes 122888 | tf_op jit(solution)/shard_map/ppermute | solution.py:19
  21.4 1.2 %collective-permute-start.4 = (f32[80,128]{1,0:T(8,128)S(1)}, f32[80,128]{1,0:T(8,128)S(1)}, u32[]{:S(2)}, u32[]{:S(2)}) collective-permute-start(f32[80,128]{1,0:T(8,128)S(1)} %add_add_fusion.3), channel_id=1, source_target_pairs={{0,8},{4,12},{8,0},{12,4},{16,24},{20,28},{24,16},{28,20},{1,9},{5... | collective-permute-start | bytes 122888 | tf_op jit(solution)/shard_map/ppermute | solution.py:19
  22.7 0.7 collective-permute-start.11
  23.4 2.3 %collective-permute-done.9.refs_10_ = bf16[64,2304]{1,0:T(8,128)(2,1)S(1)} collective-permute-done((bf16[64,2304]{1,0:T(8,128)(2,1)S(1)}, bf16[64,2304]{1,0:T(8,128)(2,1)S(1)}, u32[]{:S(2)}, u32[]{:S(2)}) %collective-permute-start.9) | collective-permute-done | bytes 294944 | tf_op jit(solution)/shard_map/ppermute | solution.py:54
  25.7 3.5 %collective-permute-start.10 = (bf16[64,2304]{1,0:T(8,128)(2,1)S(1)}, bf16[64,2304]{1,0:T(8,128)(2,1)S(1)}, u32[]{:S(2)}, u32[]{:S(2)}) collective-permute-start(bf16[64,2304]{1,0:T(8,128)(2,1)S(1)} %collective-permute-done.9.refs_10_), channel_id=1, source_target_pairs={{0,1},{1,0},{2,3},{3,2},{8,9},{9,8},{10,11},{11,10},{16,17},{17,16... | collective-permute-start | bytes 884744 | tf_op jit(solution)/shard_map/ppermute | solution.py:54
  29.2 0.5 collective-permute-start.20
  29.7 5.0 %collective-permute-start.7 = (f32[80,128]{1,0:T(8,128)S(1)}, f32[80,128]{1,0:T(8,128)S(1)}, u32[]{:S(2)}, u32[]{:S(2)}) collective-permute-start(f32[80,128]{1,0:T(8,128)S(1)} %add_add_fusion.2.refs_2_), channel_id=1, source_target_pairs={{0,4},{4,0},{8,12},{12,8},{16,20},{20,16},{24,28},{28,24},{1,5},{5... | collective-permute-start | bytes 122888 | tf_op jit(solution)/shard_map/ppermute | solution.py:19
  34.7 5.2 %collective-permute-done.10 = bf16[64,2304]{1,0:T(8,128)(2,1)S(1)} collective-permute-done((bf16[64,2304]{1,0:T(8,128)(2,1)S(1)}, bf16[64,2304]{1,0:T(8,128)(2,1)S(1)}, u32[]{:S(2)}, u32[]{:S(2)}) %collective-permute-start.10) | collective-permute-done | bytes 294944 | tf_op jit(solution)/shard_map/ppermute | solution.py:54
  40.1 5.9 %block_first.1 = (f32[4,80,2304]{2,1,0:T(8,128)S(1)}, f32[1,256]{1,0:T(1,128)S(1)}, f32[80,128]{1,0:T(8,128)S(1)}, f32[80,128]{1,0:T(8,128)S(1)}) custom-call(s32[1]{0:T(128)} %bitcast.lev_ref, s32[1]{0:T(128)} %bitcast.1.slab_ref, f32[2,256]{1,0:T(2,128)S(1)} %copy-done.3, s32[2,256]{1,0:T(2,128)S(1)} %copy-done.4, f32[80,128]{1,0:T(8,128)S(1)} %add_add_fusion.2.refs_2_, ...), custom_call_target="tpu_custom_call" | custom-call | tf_op jit(solution)/shard_map/block_first/pallas_call | solution.py:331
  46.0 1.1 %collective-permute-start.12 = (f32[80,128]{1,0:T(8,128)S(1)}, f32[80,128]{1,0:T(8,128)S(1)}, u32[]{:S(2)}, u32[]{:S(2)}) collective-permute-start(f32[80,128]{1,0:T(8,128)S(1)} %get-tuple-element.14), channel_id=1, source_target_pairs={{0,4},{4,0},{8,12},{12,8},{16,20},{20,16},{24,28},{28,24},{1,5},{5... | collective-permute-start | bytes 122888 | tf_op jit(solution)/shard_map/ppermute | solution.py:19
  47.1 2.6 %collective-permute-start.21 = (bf16[64,2304]{1,0:T(8,128)(2,1)S(1)}, bf16[64,2304]{1,0:T(8,128)(2,1)S(1)}, u32[]{:S(2)}, u32[]{:S(2)}) collective-permute-start(bf16[64,2304]{1,0:T(8,128)(2,1)S(1)} %slice_bitcast_fusion), channel_id=1, source_target_pairs={{0,2},{1,3},{2,0},{3,1},{4,5},{5,4},{6,7},{7,6},{8,10},{9,11},{10,... | collective-permute-start | bytes 884744 | tf_op jit(solution)/shard_map/ppermute | solution.py:54
  49.7 1.2 %collective-permute-start.15 = (f32[80,128]{1,0:T(8,128)S(1)}, f32[80,128]{1,0:T(8,128)S(1)}, u32[]{:S(2)}, u32[]{:S(2)}) collective-permute-start(f32[80,128]{1,0:T(8,128)S(1)} %add.49), channel_id=1, source_target_pairs={{0,24},{4,28},{8,16},{12,20},{16,8},{20,12},{24,0},{28,4},{1,25},{... | collective-permute-start | bytes 122888 | tf_op jit(solution)/shard_map/ppermute | solution.py:19
  50.9 1.4 %collective-permute-start.14 = (f32[80,128]{1,0:T(8,128)S(1)}, f32[80,128]{1,0:T(8,128)S(1)}, u32[]{:S(2)}, u32[]{:S(2)}) collective-permute-start(f32[80,128]{1,0:T(8,128)S(1)} %add.49), channel_id=1, source_target_pairs={{0,16},{4,20},{8,24},{12,28},{16,0},{20,4},{24,8},{28,12},{1,17},{... | collective-permute-start | bytes 122888 | tf_op jit(solution)/shard_map/ppermute | solution.py:19
  52.2 1.0 %collective-permute-start.13 = (f32[80,128]{1,0:T(8,128)S(1)}, f32[80,128]{1,0:T(8,128)S(1)}, u32[]{:S(2)}, u32[]{:S(2)}) collective-permute-start(f32[80,128]{1,0:T(8,128)S(1)} %add.49), channel_id=1, source_target_pairs={{0,8},{4,12},{8,0},{12,4},{16,24},{20,28},{24,16},{28,20},{1,9},{5... | collective-permute-start | bytes 122888 | tf_op jit(solution)/shard_map/ppermute | solution.py:19
  53.3 0.7 collective-permute-start.23
  54.0 2.2 %collective-permute-done.21.refs_9_ = bf16[64,2304]{1,0:T(8,128)(2,1)S(1)} collective-permute-done((bf16[64,2304]{1,0:T(8,128)(2,1)S(1)}, bf16[64,2304]{1,0:T(8,128)(2,1)S(1)}, u32[]{:S(2)}, u32[]{:S(2)}) %collective-permute-start.21) | collective-permute-done | bytes 294944 | tf_op jit(solution)/shard_map/ppermute | solution.py:54
  56.2 5.5 %collective-permute-start.22 = (bf16[64,2304]{1,0:T(8,128)(2,1)S(1)}, bf16[64,2304]{1,0:T(8,128)(2,1)S(1)}, u32[]{:S(2)}, u32[]{:S(2)}) collective-permute-start(bf16[64,2304]{1,0:T(8,128)(2,1)S(1)} %collective-permute-done.21.refs_9_), channel_id=1, source_target_pairs={{0,1},{1,0},{2,3},{3,2},{8,9},{9,8},{10,11},{11,10},{16,17},{17,16... | collective-permute-start | bytes 884744 | tf_op jit(solution)/shard_map/ppermute | solution.py:54
  61.7 1.8 %collective-permute-start.18 = (f32[80,128]{1,0:T(8,128)S(1)}, f32[80,128]{1,0:T(8,128)S(1)}, u32[]{:S(2)}, u32[]{:S(2)}) collective-permute-start(f32[80,128]{1,0:T(8,128)S(1)} %add_add_fusion.1), channel_id=1, source_target_pairs={{0,3},{1,2},{2,1},{3,0},{4,7},{5,6},{6,5},{7,4},{8,11},{9,10},{10,... | collective-permute-start | bytes 122888 | tf_op jit(solution)/shard_map/ppermute | solution.py:19
  63.5 0.6 collective-permute-start.17
  64.1 2.1 %collective-permute-start.16 = (f32[80,128]{1,0:T(8,128)S(1)}, f32[80,128]{1,0:T(8,128)S(1)}, u32[]{:S(2)}, u32[]{:S(2)}) collective-permute-start(f32[80,128]{1,0:T(8,128)S(1)} %add_add_fusion.1), channel_id=1, source_target_pairs={{0,1},{1,0},{2,3},{3,2},{4,5},{5,4},{6,7},{7,6},{8,9},{9,8},{10,11... | collective-permute-start | bytes 122888 | tf_op jit(solution)/shard_map/ppermute | solution.py:19
  66.2 2.5 %collective-permute-done.18 = f32[80,128]{1,0:T(8,128)S(1)} collective-permute-done((f32[80,128]{1,0:T(8,128)S(1)}, f32[80,128]{1,0:T(8,128)S(1)}, u32[]{:S(2)}, u32[]{:S(2)}) %collective-permute-start.18) | collective-permute-done | bytes 40992 | tf_op jit(solution)/shard_map/ppermute | solution.py:19
  68.7 0.6 collective-permute-done.17
  69.4 1.1 %collective-permute-done.19.refs_1_ = f32[80,128]{1,0:T(8,128)S(1)} collective-permute-done((f32[80,128]{1,0:T(8,128)S(1)}, f32[80,128]{1,0:T(8,128)S(1)}, u32[]{:S(2)}, u32[]{:S(2)}) %collective-permute-start.19) | collective-permute-done | bytes 40992 | tf_op jit(solution)/shard_map/ppermute | solution.py:19
  70.6 5.3 %block_last.1 = (f32[80,4,2304]{2,1,0:T(4,128)}, f32[2,256]{1,0:T(2,128)}) custom-call(s32[1]{0:T(128)} %bitcast.lev_ref, s32[1]{0:T(128)} %bitcast.1.slab_ref, f32[80,128]{1,0:T(8,128)S(1)} %add_add_fusion.refs_0_, f32[80,128]{1,0:T(8,128)S(1)} %collective-permute-done.19.refs_1_, f32[2,256]{1,0:T(2,128)S(1)} %copy-done.1, f32[2,256]{1,0:T(2,128)S(1)} %copy-done.2, ...), custom_call_target="tpu_custom_call" | custom-call | tf_op jit(solution)/shard_map/block_last/pallas_call | solution.py:342
  (45 shorter events, 0.4 us)
Async XLA Ops:
  0.6 4.2 %copy-start.5 = (bf16[2,64,2304]{2,1,0:T(8,128)(2,1)S(1)}, bf16[2,64,2304]{2,1,0:T(8,128)(2,1)}, u32[]{:S(2)}) copy-start(bf16[2,64,2304]{2,1,0:T(8,128)(2,1)} %refs_7_.3) | copy-start | bytes 1769476
  0.6 39.4 %copy-start = (f32[2,256,4]{1,2,0:T(4,128)S(1)}, f32[2,256,4]{1,2,0:T(4,128)}, u32[]{:S(2)}) copy-start(f32[2,256,4]{1,2,0:T(4,128)} %param.13) | copy-start | bytes 24580
  0.7 39.4 %copy-start.1 = (f32[2,256]{1,0:T(2,128)S(1)}, f32[2,256]{1,0:T(2,128)}, u32[]{:S(2)}) copy-start(f32[2,256]{1,0:T(2,128)} %refs_2_.3) | copy-start | bytes 6148
  0.7 39.4 %copy-start.2 = (f32[2,256]{1,0:T(2,128)S(1)}, f32[2,256]{1,0:T(2,128)}, u32[]{:S(2)}) copy-start(f32[2,256]{1,0:T(2,128)} %refs_3_.1) | copy-start | bytes 6148
  0.7 39.4 %copy-start.3 = (f32[2,256]{1,0:T(2,128)S(1)}, f32[2,256]{1,0:T(2,128)}, u32[]{:S(2)}) copy-start(f32[2,256]{1,0:T(2,128)} %refs_0_.3) | copy-start | bytes 6148
  0.7 39.4 %copy-start.4 = (s32[2,256]{1,0:T(2,128)S(1)}, s32[2,256]{1,0:T(2,128)}, u32[]{:S(2)}) copy-start(s32[2,256]{1,0:T(2,128)} %refs_1_.3) | copy-start | bytes 6148
  4.8 3.2 %collective-permute-start = (f32[80,128]{1,0:T(8,128)S(1)}, f32[80,128]{1,0:T(8,128)S(1)}, u32[]{:S(2)}, u32[]{:S(2)}) collective-permute-start(f32[80,128]{1,0:T(8,128)S(1)} %get-tuple-element.12), channel_id=1, source_target_pairs={{0,4},{4,0},{8,12},{12,8},{16,20},{20,16},{24,28},{28,24},{1,5},{5... | collective-permute-start | bytes 122888 | tf_op jit(solution)/shard_map/ppermute | solution.py:19
  4.9 17.7 %collective-permute-start.8 = (bf16[64,2304]{1,0:T(8,128)(2,1)S(1)}, bf16[64,2304]{1,0:T(8,128)(2,1)S(1)}, u32[]{:S(2)}, u32[]{:S(2)}) collective-permute-start(bf16[64,2304]{1,0:T(8,128)(2,1)S(1)} %slice_bitcast_fusion.1), channel_id=1, source_target_pairs={{0,1},{1,0},{2,3},{3,2},{4,6},{5,7},{6,4},{7,5},{8,9},{9,8},{10,11... | collective-permute-start | bytes 884744 | tf_op jit(solution)/shard_map/ppermute | solution.py:54
  8.0 11.0 %collective-permute-start.3 = (f32[80,128]{1,0:T(8,128)S(1)}, f32[80,128]{1,0:T(8,128)S(1)}, u32[]{:S(2)}, u32[]{:S(2)}) collective-permute-start(f32[80,128]{1,0:T(8,128)S(1)} %add.42), channel_id=1, source_target_pairs={{0,3},{1,2},{2,1},{3,0},{4,7},{5,6},{6,5},{7,4},{8,11},{9,10},{10,... | collective-permute-start | bytes 122888 | tf_op jit(solution)/shard_map/ppermute | solution.py:19
  11.2 7.9 %collective-permute-start.2 = (f32[80,128]{1,0:T(8,128)S(1)}, f32[80,128]{1,0:T(8,128)S(1)}, u32[]{:S(2)}, u32[]{:S(2)}) collective-permute-start(f32[80,128]{1,0:T(8,128)S(1)} %add.42), channel_id=1, source_target_pairs={{0,2},{1,3},{2,0},{3,1},{4,6},{5,7},{6,4},{7,5},{8,10},{9,11},{10,... | collective-permute-start | bytes 122888 | tf_op jit(solution)/shard_map/ppermute | solution.py:19
  11.2 7.9 %collective-permute-start.1 = (f32[80,128]{1,0:T(8,128)S(1)}, f32[80,128]{1,0:T(8,128)S(1)}, u32[]{:S(2)}, u32[]{:S(2)}) collective-permute-start(f32[80,128]{1,0:T(8,128)S(1)} %add.42), channel_id=1, source_target_pairs={{0,1},{1,0},{2,3},{3,2},{4,5},{5,4},{6,7},{7,6},{8,9},{9,8},{10,11... | collective-permute-start | bytes 122888 | tf_op jit(solution)/shard_map/ppermute | solution.py:19
  12.5 13.2 %collective-permute-start.9 = (bf16[64,2304]{1,0:T(8,128)(2,1)S(1)}, bf16[64,2304]{1,0:T(8,128)(2,1)S(1)}, u32[]{:S(2)}, u32[]{:S(2)}) collective-permute-start(bf16[64,2304]{1,0:T(8,128)(2,1)S(1)} %slice_bitcast_fusion.1), channel_id=1, source_target_pairs={{0,2},{1,3},{2,0},{3,1},{4,5},{5,4},{6,7},{7,6},{8,10},{9,11},{10,... | collective-permute-start | bytes 884744 | tf_op jit(solution)/shard_map/ppermute | solution.py:54
  19.1 10.1 %collective-permute-start.6 = (f32[80,128]{1,0:T(8,128)S(1)}, f32[80,128]{1,0:T(8,128)S(1)}, u32[]{:S(2)}, u32[]{:S(2)}) collective-permute-start(f32[80,128]{1,0:T(8,128)S(1)} %add_add_fusion.3), channel_id=1, source_target_pairs={{0,24},{4,28},{8,16},{12,20},{16,8},{20,12},{24,0},{28,4},{1,25},{... | collective-permute-start | bytes 122888 | tf_op jit(solution)/shard_map/ppermute | solution.py:19
  20.6 9.1 %collective-permute-start.5 = (f32[80,128]{1,0:T(8,128)S(1)}, f32[80,128]{1,0:T(8,128)S(1)}, u32[]{:S(2)}, u32[]{:S(2)}) collective-permute-start(f32[80,128]{1,0:T(8,128)S(1)} %add_add_fusion.3), channel_id=1, source_target_pairs={{0,16},{4,20},{8,24},{12,28},{16,0},{20,4},{24,8},{28,12},{1,17},{... | collective-permute-start | bytes 122888 | tf_op jit(solution)/shard_map/ppermute | solution.py:19
  21.4 8.3 %collective-permute-start.4 = (f32[80,128]{1,0:T(8,128)S(1)}, f32[80,128]{1,0:T(8,128)S(1)}, u32[]{:S(2)}, u32[]{:S(2)}) collective-permute-start(f32[80,128]{1,0:T(8,128)S(1)} %add_add_fusion.3), channel_id=1, source_target_pairs={{0,8},{4,12},{8,0},{12,4},{16,24},{20,28},{24,16},{28,20},{1,9},{5... | collective-permute-start | bytes 122888 | tf_op jit(solution)/shard_map/ppermute | solution.py:19
  22.7 17.3 %collective-permute-start.11 = (bf16[64,2304]{1,0:T(8,128)(2,1)S(1)}, bf16[64,2304]{1,0:T(8,128)(2,1)S(1)}, u32[]{:S(2)}, u32[]{:S(2)}) collective-permute-start(bf16[64,2304]{1,0:T(8,128)(2,1)S(1)} %broadcast_select_fusion.3), channel_id=1, source_target_pairs={{4,5},{5,4},{6,7},{7,6},{12,13},{13,12},{14,15},{15,14},{20,21},{2... | collective-permute-start | bytes 884744 | tf_op jit(solution)/shard_map/ppermute | solution.py:54
  25.7 14.3 %collective-permute-start.10 = (bf16[64,2304]{1,0:T(8,128)(2,1)S(1)}, bf16[64,2304]{1,0:T(8,128)(2,1)S(1)}, u32[]{:S(2)}, u32[]{:S(2)}) collective-permute-start(bf16[64,2304]{1,0:T(8,128)(2,1)S(1)} %collective-permute-done.9.refs_10_), channel_id=1, source_target_pairs={{0,1},{1,0},{2,3},{3,2},{8,9},{9,8},{10,11},{11,10},{16,17},{17,16... | collective-permute-start | bytes 884744 | tf_op jit(solution)/shard_map/ppermute | solution.py:54
  29.2 24.1 %copy-start.6 = (bf16[2,64,2304]{2,1,0:T(8,128)(2,1)S(1)}, bf16[2,64,2304]{2,1,0:T(8,128)(2,1)}, u32[]{:S(2)}) copy-start(bf16[2,64,2304]{2,1,0:T(8,128)(2,1)} %refs_7_.3) | copy-start | bytes 1769476
  29.2 24.0 %collective-permute-start.20 = (bf16[64,2304]{1,0:T(8,128)(2,1)S(1)}, bf16[64,2304]{1,0:T(8,128)(2,1)S(1)}, u32[]{:S(2)}, u32[]{:S(2)}) collective-permute-start(bf16[64,2304]{1,0:T(8,128)(2,1)S(1)} %slice_bitcast_fusion), channel_id=1, source_target_pairs={{0,1},{1,0},{2,3},{3,2},{4,6},{5,7},{6,4},{7,5},{8,9},{9,8},{10,11... | collective-permute-start | bytes 884744 | tf_op jit(solution)/shard_map/ppermute | solution.py:54
  29.7 10.3 %collective-permute-start.7 = (f32[80,128]{1,0:T(8,128)S(1)}, f32[80,128]{1,0:T(8,128)S(1)}, u32[]{:S(2)}, u32[]{:S(2)}) collective-permute-start(f32[80,128]{1,0:T(8,128)S(1)} %add_add_fusion.2.refs_2_), channel_id=1, source_target_pairs={{0,4},{4,0},{8,12},{12,8},{16,20},{20,16},{24,28},{28,24},{1,5},{5... | collective-permute-start | bytes 122888 | tf_op jit(solution)/shard_map/ppermute | solution.py:19
  46.0 3.7 %collective-permute-start.12 = (f32[80,128]{1,0:T(8,128)S(1)}, f32[80,128]{1,0:T(8,128)S(1)}, u32[]{:S(2)}, u32[]{:S(2)}) collective-permute-start(f32[80,128]{1,0:T(8,128)S(1)} %get-tuple-element.14), channel_id=1, source_target_pairs={{0,4},{4,0},{8,12},{12,8},{16,20},{20,16},{24,28},{28,24},{1,5},{5... | collective-permute-start | bytes 122888 | tf_op jit(solution)/shard_map/ppermute | solution.py:19
  47.1 9.1 %collective-permute-start.21 = (bf16[64,2304]{1,0:T(8,128)(2,1)S(1)}, bf16[64,2304]{1,0:T(8,128)(2,1)S(1)}, u32[]{:S(2)}, u32[]{:S(2)}) collective-permute-start(bf16[64,2304]{1,0:T(8,128)(2,1)S(1)} %slice_bitcast_fusion), channel_id=1, source_target_pairs={{0,2},{1,3},{2,0},{3,1},{4,5},{5,4},{6,7},{7,6},{8,10},{9,11},{10,... | collective-permute-start | bytes 884744 | tf_op jit(solution)/shard_map/ppermute | solution.py:54
  49.7 12.0 %collective-permute-start.15 = (f32[80,128]{1,0:T(8,128)S(1)}, f32[80,128]{1,0:T(8,128)S(1)}, u32[]{:S(2)}, u32[]{:S(2)}) collective-permute-start(f32[80,128]{1,0:T(8,128)S(1)} %add.49), channel_id=1, source_target_pairs={{0,24},{4,28},{8,16},{12,20},{16,8},{20,12},{24,0},{28,4},{1,25},{... | collective-permute-start | bytes 122888 | tf_op jit(solution)/shard_map/ppermute | solution.py:19
  50.9 10.8 %collective-permute-start.14 = (f32[80,128]{1,0:T(8,128)S(1)}, f32[80,128]{1,0:T(8,128)S(1)}, u32[]{:S(2)}, u32[]{:S(2)}) collective-permute-start(f32[80,128]{1,0:T(8,128)S(1)} %add.49), channel_id=1, source_target_pairs={{0,16},{4,20},{8,24},{12,28},{16,0},{20,4},{24,8},{28,12},{1,17},{... | collective-permute-start | bytes 122888 | tf_op jit(solution)/shard_map/ppermute | solution.py:19
  52.2 9.5 %collective-permute-start.13 = (f32[80,128]{1,0:T(8,128)S(1)}, f32[80,128]{1,0:T(8,128)S(1)}, u32[]{:S(2)}, u32[]{:S(2)}) collective-permute-start(f32[80,128]{1,0:T(8,128)S(1)} %add.49), channel_id=1, source_target_pairs={{0,8},{4,12},{8,0},{12,4},{16,24},{20,28},{24,16},{28,20},{1,9},{5... | collective-permute-start | bytes 122888 | tf_op jit(solution)/shard_map/ppermute | solution.py:19
  53.3 16.1 %collective-permute-start.23 = (bf16[64,2304]{1,0:T(8,128)(2,1)S(1)}, bf16[64,2304]{1,0:T(8,128)(2,1)S(1)}, u32[]{:S(2)}, u32[]{:S(2)}) collective-permute-start(bf16[64,2304]{1,0:T(8,128)(2,1)S(1)} %broadcast_select_fusion.1), channel_id=1, source_target_pairs={{4,5},{5,4},{6,7},{7,6},{12,13},{13,12},{14,15},{15,14},{20,21},{2... | collective-permute-start | bytes 884744 | tf_op jit(solution)/shard_map/ppermute | solution.py:54
  56.2 13.2 %collective-permute-start.22 = (bf16[64,2304]{1,0:T(8,128)(2,1)S(1)}, bf16[64,2304]{1,0:T(8,128)(2,1)S(1)}, u32[]{:S(2)}, u32[]{:S(2)}) collective-permute-start(bf16[64,2304]{1,0:T(8,128)(2,1)S(1)} %collective-permute-done.21.refs_9_), channel_id=1, source_target_pairs={{0,1},{1,0},{2,3},{3,2},{8,9},{9,8},{10,11},{11,10},{16,17},{17,16... | collective-permute-start | bytes 884744 | tf_op jit(solution)/shard_map/ppermute | solution.py:54
  61.7 7.0 %collective-permute-start.18 = (f32[80,128]{1,0:T(8,128)S(1)}, f32[80,128]{1,0:T(8,128)S(1)}, u32[]{:S(2)}, u32[]{:S(2)}) collective-permute-start(f32[80,128]{1,0:T(8,128)S(1)} %add_add_fusion.1), channel_id=1, source_target_pairs={{0,3},{1,2},{2,1},{3,0},{4,7},{5,6},{6,5},{7,4},{8,11},{9,10},{10,... | collective-permute-start | bytes 122888 | tf_op jit(solution)/shard_map/ppermute | solution.py:19
  63.5 5.8 %collective-permute-start.17 = (f32[80,128]{1,0:T(8,128)S(1)}, f32[80,128]{1,0:T(8,128)S(1)}, u32[]{:S(2)}, u32[]{:S(2)}) collective-permute-start(f32[80,128]{1,0:T(8,128)S(1)} %add_add_fusion.1), channel_id=1, source_target_pairs={{0,2},{1,3},{2,0},{3,1},{4,6},{5,7},{6,4},{7,5},{8,10},{9,11},{10,... | collective-permute-start | bytes 122888 | tf_op jit(solution)/shard_map/ppermute | solution.py:19
  64.1 5.2 %collective-permute-start.16 = (f32[80,128]{1,0:T(8,128)S(1)}, f32[80,128]{1,0:T(8,128)S(1)}, u32[]{:S(2)}, u32[]{:S(2)}) collective-permute-start(f32[80,128]{1,0:T(8,128)S(1)} %add_add_fusion.1), channel_id=1, source_target_pairs={{0,1},{1,0},{2,3},{3,2},{4,5},{5,4},{6,7},{7,6},{8,9},{9,8},{10,11... | collective-permute-start | bytes 122888 | tf_op jit(solution)/shard_map/ppermute | solution.py:19
  69.3 1.3 %collective-permute-start.19 = (f32[80,128]{1,0:T(8,128)S(1)}, f32[80,128]{1,0:T(8,128)S(1)}, u32[]{:S(2)}, u32[]{:S(2)}) collective-permute-start(f32[80,128]{1,0:T(8,128)S(1)} %add_add_fusion.refs_0_), channel_id=1, source_target_pairs={{0,4},{4,0},{8,12},{12,8},{16,20},{20,16},{24,28},{28,24},{1,5},{5... | collective-permute-start | bytes 122888 | tf_op jit(solution)/shard_map/ppermute | solution.py:19

commit v7 on v5

--- a/solution.py
+++ b/solution.py
@@ -32,10 +32,9 @@
         bit *= 4
 
 
-def add_over(keep, send, lev_first):
+def add_over(keep, send):
     half = keep + swap(send, "slab", 1)
-    rounds = [list(rounds_of("lev", 1)), list(rounds_of("slab", 2))]
-    rounds = sum(rounds if lev_first else rounds[::-1], [])
+    rounds = list(rounds_of("slab", 2)) + list(rounds_of("lev", 1))
     for axis, distances in rounds:
         half = sum([swap(half, axis, d) for d in distances], half)
     return half, swap(half, "slab", 1)
@@ -325,7 +324,7 @@
     )(*place, *far(obs_frac, obs_cell, ensemble))
     later_rows, keep = lax.optimization_barrier((loc_column, keep))
     shards.append(rows_over(later_rows[1]))
-    ours, theirs = add_over(keep, send, True)
+    ours, theirs = add_over(keep, send)
 
     current, mean_first, keep, send = pl.pallas_call(
         with_place(functools.partial(first_kernel, groups, sizes)),
@@ -336,7 +335,7 @@
         compiler_params=pltpu.CompilerParams(vmem_limit_bytes=KERNEL_VMEM),
         name="block_first",
     )(*place, obs_frac, obs_cell, *near(ours, theirs), obs_value, obs_var, levels, *far(ensemble, loc_column), *near(*shards[0]))
-    ours, theirs = add_over(keep, send, False)
+    ours, theirs = add_over(keep, send)
 
     analysis, mean = pl.pallas_call(
         with_place(functools.partial(last_kernel, groups)),

time: 77 us -> 72.5 us (0.942)
  waiting for transfers between devices: 26.9 us -> 19.4 us
  starting transfers between devices: 33.5 us -> 36.4 us
    ppermute x18, waiting for transfers between devices: 25.8 us -> 18 us  [swap(): return lax.ppermute(value, axis, [(i, i ^ bit) for i in range(size)])]
    ppermute x18, starting transfers between devices: 22.9 us -> 25.5 us  [swap(): return lax.ppermute(value, axis, [(i, i ^ bit) for i in range(size)])]
  transfers between devices with their start and end apart: 22 -> 22, of which waited for: 9 -> 10; matrix products, arithmetic and copies ran while one was open for 0% -> 0% of each run, Pallas kernels for 0% -> 0%
where the time goes in v7:
time: 72.5 us; the launch traced here: 72.3 us
  starting transfers between devices  36.4 us (50%)
  waiting for transfers between devices  19.4 us (27%)
  Pallas kernels  15.4 us (21%)
  between operations  0.82 us (1%)
    ppermute x18, starting transfers between devices, swap(): return lax.ppermute(value, axis, [(i, i ^ bit) for i in range(size)])  25.5 us
    ppermute x18, waiting for transfers between devices, swap(): return lax.ppermute(value, axis, [(i, i ^ bit) for i in range(size)])  18 us
    ppermute x4, starting transfers between devices, swap_either(): return lax.ppermute(value, ('slab', 'lev'), pairs)  10.9 us
    pallas_call x1, Pallas kernels, on_device(): pl.pallas_call(with_place(functools.partial(first_kernel, groups, sizes))...  5.93 us
    pallas_call x1, Pallas kernels, on_device(): pl.pallas_call(with_place(functools.partial(last_kernel, groups)), out_sh...  5.4 us
    pallas_call x1, Pallas kernels, on_device(): pl.pallas_call(with_place(functools.partial(prior_kernel, sizes)), out_sh...  4.07 us
    ppermute x4, waiting for transfers between devices, swap_either(): return lax.ppermute(value, ('slab', 'lev'), pairs)  1.45 us
  transfers between devices with their start and end apart: 22, of which 10 were waited for; matrix products, arithmetic and copies ran while one was open for 0% of the time, Pallas kernels for 0%

profile of v7, /device:TPU:0, one launch (start us, length us, event | category | flops | bytes accessed | tf_op | source)
XLA Modules:
  0.0 72.3 jit_solution(5641194764614125567)
XLA Ops:
  0.7 4.1 %cells.1 = (f32[80,128]{1,0:T(8,128)S(1)}, f32[80,128]{1,0:T(8,128)S(1)}) custom-call(s32[1]{0:T(128)} %bitcast.lev_ref, s32[1]{0:T(128)} %bitcast.1.slab_ref, f32[2,256]{1,0:T(2,128)} %refs_0_.3, s32[2,256]{1,0:T(2,128)} %refs_1_.3, f32[80,4,2304]{2,1,0:T(4,128)} %refs_7_.2), custom_call_target="tpu_custom_call" | custom-call | tf_op jit(solution)/shard_map/cells/pallas_call | solution.py:316
  4.9 4.0 %collective-permute-start.9 = (bf16[64,2304]{1,0:T(8,128)(2,1)S(1)}, bf16[64,2304]{1,0:T(8,128)(2,1)S(1)}, u32[]{:S(2)}, u32[]{:S(2)}) collective-permute-start(bf16[64,2304]{1,0:T(8,128)(2,1)S(1)} %slice_bitcast_fusion.1), channel_id=1, source_target_pairs={{0,2},{1,3},{2,0},{3,1},{4,5},{5,4},{6,7},{7,6},{8,10},{9,11},{10,... | collective-permute-start | bytes 884744 | tf_op jit(solution)/shard_map/ppermute | solution.py:54
  8.9 1.7 %collective-permute-start.8 = (bf16[64,2304]{1,0:T(8,128)(2,1)S(1)}, bf16[64,2304]{1,0:T(8,128)(2,1)S(1)}, u32[]{:S(2)}, u32[]{:S(2)}) collective-permute-start(bf16[64,2304]{1,0:T(8,128)(2,1)S(1)} %slice_bitcast_fusion.1), channel_id=1, source_target_pairs={{0,1},{1,0},{2,3},{3,2},{4,6},{5,7},{6,4},{7,5},{8,9},{9,8},{10,11... | collective-permute-start | bytes 884744 | tf_op jit(solution)/shard_map/ppermute | solution.py:54
  10.6 1.3 %collective-permute-start.3 = (f32[80,128]{1,0:T(8,128)S(1)}, f32[80,128]{1,0:T(8,128)S(1)}, u32[]{:S(2)}, u32[]{:S(2)}) collective-permute-start(f32[80,128]{1,0:T(8,128)S(1)} %add.42), channel_id=1, source_target_pairs={{0,24},{4,28},{8,16},{12,20},{16,8},{20,12},{24,0},{28,4},{1,25},{... | collective-permute-start | bytes 122888 | tf_op jit(solution)/shard_map/ppermute | solution.py:19
  12.0 0.8 %collective-permute-start.2 = (f32[80,128]{1,0:T(8,128)S(1)}, f32[80,128]{1,0:T(8,128)S(1)}, u32[]{:S(2)}, u32[]{:S(2)}) collective-permute-start(f32[80,128]{1,0:T(8,128)S(1)} %add.42), channel_id=1, source_target_pairs={{0,16},{4,20},{8,24},{12,28},{16,0},{20,4},{24,8},{28,12},{1,17},{... | collective-permute-start | bytes 122888 | tf_op jit(solution)/shard_map/ppermute | solution.py:19
  12.8 1.4 %collective-permute-start.1 = (f32[80,128]{1,0:T(8,128)S(1)}, f32[80,128]{1,0:T(8,128)S(1)}, u32[]{:S(2)}, u32[]{:S(2)}) collective-permute-start(f32[80,128]{1,0:T(8,128)S(1)} %add.42), channel_id=1, source_target_pairs={{0,8},{4,12},{8,0},{12,4},{16,24},{20,28},{24,16},{28,20},{1,9},{5... | collective-permute-start | bytes 122888 | tf_op jit(solution)/shard_map/ppermute | solution.py:19
  14.2 1.6 %collective-permute-done.3 = f32[80,128]{1,0:T(8,128)S(1)} collective-permute-done((f32[80,128]{1,0:T(8,128)S(1)}, f32[80,128]{1,0:T(8,128)S(1)}, u32[]{:S(2)}, u32[]{:S(2)}) %collective-permute-start.3) | collective-permute-done | bytes 40992 | tf_op jit(solution)/shard_map/ppermute | solution.py:19
  15.8 0.3 collective-permute-done.2
  16.1 0.7 collective-permute-done.1
  16.8 0.5 collective-permute-start.6
  17.4 1.4 %collective-permute-start.5 = (f32[80,128]{1,0:T(8,128)S(1)}, f32[80,128]{1,0:T(8,128)S(1)}, u32[]{:S(2)}, u32[]{:S(2)}) collective-permute-start(f32[80,128]{1,0:T(8,128)S(1)} %add_add_fusion.3), channel_id=1, source_target_pairs={{0,2},{1,3},{2,0},{3,1},{4,6},{5,7},{6,4},{7,5},{8,10},{9,11},{10,... | collective-permute-start | bytes 122888 | tf_op jit(solution)/shard_map/ppermute | solution.py:19
  18.8 2.5 %collective-permute-start.4 = (f32[80,128]{1,0:T(8,128)S(1)}, f32[80,128]{1,0:T(8,128)S(1)}, u32[]{:S(2)}, u32[]{:S(2)}) collective-permute-start(f32[80,128]{1,0:T(8,128)S(1)} %add_add_fusion.3), channel_id=1, source_target_pairs={{0,1},{1,0},{2,3},{3,2},{4,5},{5,4},{6,7},{7,6},{8,9},{9,8},{10,11... | collective-permute-start | bytes 122888 | tf_op jit(solution)/shard_map/ppermute | solution.py:19
  21.3 1.3 %collective-permute-done.8.refs_9_ = bf16[64,2304]{1,0:T(8,128)(2,1)S(1)} collective-permute-done((bf16[64,2304]{1,0:T(8,128)(2,1)S(1)}, bf16[64,2304]{1,0:T(8,128)(2,1)S(1)}, u32[]{:S(2)}, u32[]{:S(2)}) %collective-permute-start.8) | collective-permute-done | bytes 294944 | tf_op jit(solution)/shard_map/ppermute | solution.py:54
  22.7 3.4 %collective-permute-start.10 = (bf16[64,2304]{1,0:T(8,128)(2,1)S(1)}, bf16[64,2304]{1,0:T(8,128)(2,1)S(1)}, u32[]{:S(2)}, u32[]{:S(2)}) collective-permute-start(bf16[64,2304]{1,0:T(8,128)(2,1)S(1)} %broadcast_select_fusion.1), channel_id=1, source_target_pairs={{0,1},{1,0},{2,3},{3,2},{4,5},{5,4},{6,7},{7,6},{8,9},{9,8},{10,11... | collective-permute-start | bytes 884744 | tf_op jit(solution)/shard_map/ppermute | solution.py:19
  26.1 0.4 collective-permute-start.7
  26.5 0.9 %collective-permute-done.7.refs_3_ = f32[80,128]{1,0:T(8,128)S(1)} collective-permute-done((f32[80,128]{1,0:T(8,128)S(1)}, f32[80,128]{1,0:T(8,128)S(1)}, u32[]{:S(2)}, u32[]{:S(2)}) %collective-permute-start.7) | collective-permute-done | bytes 40992 | tf_op jit(solution)/shard_map/ppermute | solution.py:19
  27.4 5.9 %collective-permute-done.10.refs_11_ = bf16[64,2304]{1,0:T(8,128)(2,1)S(1)} collective-permute-done((bf16[64,2304]{1,0:T(8,128)(2,1)S(1)}, bf16[64,2304]{1,0:T(8,128)(2,1)S(1)}, u32[]{:S(2)}, u32[]{:S(2)}) %collective-permute-start.10) | collective-permute-done | bytes 294944 | tf_op jit(solution)/shard_map/ppermute | solution.py:19
  33.3 5.9 %block_first.1 = (f32[4,80,2304]{2,1,0:T(8,128)S(1)}, f32[1,256]{1,0:T(1,128)S(1)}, f32[80,128]{1,0:T(8,128)S(1)}, f32[80,128]{1,0:T(8,128)S(1)}) custom-call(s32[1]{0:T(128)} %bitcast.lev_ref, s32[1]{0:T(128)} %bitcast.1.slab_ref, f32[2,256]{1,0:T(2,128)S(1)} %copy-done.3, s32[2,256]{1,0:T(2,128)S(1)} %copy-done.4, f32[80,128]{1,0:T(8,128)S(1)} %add_add_fusion.2.refs_2_, ...), custom_call_target="tpu_custom_call" | custom-call | tf_op jit(solution)/shard_map/block_first/pallas_call | solution.py:329
  39.4 3.3 %collective-permute-start.20 = (bf16[64,2304]{1,0:T(8,128)(2,1)S(1)}, bf16[64,2304]{1,0:T(8,128)(2,1)S(1)}, u32[]{:S(2)}, u32[]{:S(2)}) collective-permute-start(bf16[64,2304]{1,0:T(8,128)(2,1)S(1)} %slice_bitcast_fusion), channel_id=1, source_target_pairs={{0,2},{1,3},{2,0},{3,1},{4,5},{5,4},{6,7},{7,6},{8,10},{9,11},{10,... | collective-permute-start | bytes 884744 | tf_op jit(solution)/shard_map/ppermute | solution.py:54
  42.7 1.9 %collective-permute-start.19 = (bf16[64,2304]{1,0:T(8,128)(2,1)S(1)}, bf16[64,2304]{1,0:T(8,128)(2,1)S(1)}, u32[]{:S(2)}, u32[]{:S(2)}) collective-permute-start(bf16[64,2304]{1,0:T(8,128)(2,1)S(1)} %slice_bitcast_fusion), channel_id=1, source_target_pairs={{0,1},{1,0},{2,3},{3,2},{4,6},{5,7},{6,4},{7,5},{8,9},{9,8},{10,11... | collective-permute-start | bytes 884744 | tf_op jit(solution)/shard_map/ppermute | solution.py:54
  44.7 1.0 %collective-permute-start.13 = (f32[80,128]{1,0:T(8,128)S(1)}, f32[80,128]{1,0:T(8,128)S(1)}, u32[]{:S(2)}, u32[]{:S(2)}) collective-permute-start(f32[80,128]{1,0:T(8,128)S(1)} %add.49), channel_id=1, source_target_pairs={{0,16},{4,20},{8,24},{12,28},{16,0},{20,4},{24,8},{28,12},{1,17},{... | collective-permute-start | bytes 122888 | tf_op jit(solution)/shard_map/ppermute | solution.py:19
  45.7 2.4 %collective-permute-start.12 = (f32[80,128]{1,0:T(8,128)S(1)}, f32[80,128]{1,0:T(8,128)S(1)}, u32[]{:S(2)}, u32[]{:S(2)}) collective-permute-start(f32[80,128]{1,0:T(8,128)S(1)} %add.49), channel_id=1, source_target_pairs={{0,8},{4,12},{8,0},{12,4},{16,24},{20,28},{24,16},{28,20},{1,9},{5... | collective-permute-start | bytes 122888 | tf_op jit(solution)/shard_map/ppermute | solution.py:19
  48.1 1.4 %collective-permute-done.14 = f32[80,128]{1,0:T(8,128)S(1)} collective-permute-done((f32[80,128]{1,0:T(8,128)S(1)}, f32[80,128]{1,0:T(8,128)S(1)}, u32[]{:S(2)}, u32[]{:S(2)}) %collective-permute-start.14) | collective-permute-done | bytes 40992 | tf_op jit(solution)/shard_map/ppermute | solution.py:19
  49.6 0.6 collective-permute-done.12
  50.1 0.5 collective-permute-start.17
  50.7 1.1 %collective-permute-start.16 = (f32[80,128]{1,0:T(8,128)S(1)}, f32[80,128]{1,0:T(8,128)S(1)}, u32[]{:S(2)}, u32[]{:S(2)}) collective-permute-start(f32[80,128]{1,0:T(8,128)S(1)} %add_add_fusion.1), channel_id=1, source_target_pairs={{0,2},{1,3},{2,0},{3,1},{4,6},{5,7},{6,4},{7,5},{8,10},{9,11},{10,... | collective-permute-start | bytes 122888 | tf_op jit(solution)/shard_map/ppermute | solution.py:19
  51.8 2.8 %collective-permute-start.15 = (f32[80,128]{1,0:T(8,128)S(1)}, f32[80,128]{1,0:T(8,128)S(1)}, u32[]{:S(2)}, u32[]{:S(2)}) collective-permute-start(f32[80,128]{1,0:T(8,128)S(1)} %add_add_fusion.1), channel_id=1, source_target_pairs={{0,1},{1,0},{2,3},{3,2},{4,5},{5,4},{6,7},{7,6},{8,9},{9,8},{10,11... | collective-permute-start | bytes 122888 | tf_op jit(solution)/shard_map/ppermute | solution.py:19
  54.6 0.1 collective-permute-done.19.refs_8_
  54.7 5.2 %collective-permute-start.21 = (bf16[64,2304]{1,0:T(8,128)(2,1)S(1)}, bf16[64,2304]{1,0:T(8,128)(2,1)S(1)}, u32[]{:S(2)}, u32[]{:S(2)}) collective-permute-start(bf16[64,2304]{1,0:T(8,128)(2,1)S(1)} %broadcast_select_fusion), channel_id=1, source_target_pairs={{0,1},{1,0},{2,3},{3,2},{4,5},{5,4},{6,7},{7,6},{8,9},{9,8},{10,11... | collective-permute-start | bytes 884744 | tf_op jit(solution)/shard_map/ppermute | solution.py:19
  60.0 0.4 collective-permute-start.18
  60.3 6.5 %collective-permute-done.21.refs_10_ = bf16[64,2304]{1,0:T(8,128)(2,1)S(1)} collective-permute-done((bf16[64,2304]{1,0:T(8,128)(2,1)S(1)}, bf16[64,2304]{1,0:T(8,128)(2,1)S(1)}, u32[]{:S(2)}, u32[]{:S(2)}) %collective-permute-start.21) | collective-permute-done | bytes 294944 | tf_op jit(solution)/shard_map/ppermute | solution.py:19
  66.9 5.4 %block_last.1 = (f32[80,4,2304]{2,1,0:T(4,128)}, f32[2,256]{1,0:T(2,128)}) custom-call(s32[1]{0:T(128)} %bitcast.lev_ref, s32[1]{0:T(128)} %bitcast.1.slab_ref, f32[80,128]{1,0:T(8,128)S(1)} %add_add_fusion.refs_0_, f32[80,128]{1,0:T(8,128)S(1)} %collective-permute-done.18.refs_1_, f32[2,256]{1,0:T(2,128)S(1)} %copy-done.1, f32[2,256]{1,0:T(2,128)S(1)} %copy-done.2, ...), custom_call_target="tpu_custom_call" | custom-call | tf_op jit(solution)/shard_map/block_last/pallas_call | solution.py:340
  (39 shorter events, 0.5 us)
Async XLA Ops:
  0.6 32.7 %copy-start.3 = (f32[2,256]{1,0:T(2,128)S(1)}, f32[2,256]{1,0:T(2,128)}, u32[]{:S(2)}) copy-start(f32[2,256]{1,0:T(2,128)} %refs_0_.3) | copy-start | bytes 6148
  0.6 32.7 %copy-start.4 = (s32[2,256]{1,0:T(2,128)S(1)}, s32[2,256]{1,0:T(2,128)}, u32[]{:S(2)}) copy-start(s32[2,256]{1,0:T(2,128)} %refs_1_.3) | copy-start | bytes 6148
  0.7 4.2 %copy-start.5 = (bf16[2,64,2304]{2,1,0:T(8,128)(2,1)S(1)}, bf16[2,64,2304]{2,1,0:T(8,128)(2,1)}, u32[]{:S(2)}) copy-start(bf16[2,64,2304]{2,1,0:T(8,128)(2,1)} %refs_7_.3) | copy-start | bytes 1769476
  0.7 32.7 %copy-start.2 = (f32[2,256]{1,0:T(2,128)S(1)}, f32[2,256]{1,0:T(2,128)}, u32[]{:S(2)}) copy-start(f32[2,256]{1,0:T(2,128)} %refs_3_.1) | copy-start | bytes 6148
  0.7 32.7 %copy-start.1 = (f32[2,256]{1,0:T(2,128)S(1)}, f32[2,256]{1,0:T(2,128)}, u32[]{:S(2)}) copy-start(f32[2,256]{1,0:T(2,128)} %refs_2_.3) | copy-start | bytes 6148
  0.7 32.7 %copy-start = (f32[2,256,4]{1,2,0:T(4,128)S(1)}, f32[2,256,4]{1,2,0:T(4,128)}, u32[]{:S(2)}) copy-start(f32[2,256,4]{1,2,0:T(4,128)} %param.13) | copy-start | bytes 24580
  4.8 5.8 %collective-permute-start = (f32[80,128]{1,0:T(8,128)S(1)}, f32[80,128]{1,0:T(8,128)S(1)}, u32[]{:S(2)}, u32[]{:S(2)}) collective-permute-start(f32[80,128]{1,0:T(8,128)S(1)} %get-tuple-element.12), channel_id=1, source_target_pairs={{0,4},{4,0},{8,12},{12,8},{16,20},{20,16},{24,28},{28,24},{1,5},{5... | collective-permute-start | bytes 122888 | tf_op jit(solution)/shard_map/ppermute | solution.py:19
  4.9 16.4 %collective-permute-start.9 = (bf16[64,2304]{1,0:T(8,128)(2,1)S(1)}, bf16[64,2304]{1,0:T(8,128)(2,1)S(1)}, u32[]{:S(2)}, u32[]{:S(2)}) collective-permute-start(bf16[64,2304]{1,0:T(8,128)(2,1)S(1)} %slice_bitcast_fusion.1), channel_id=1, source_target_pairs={{0,2},{1,3},{2,0},{3,1},{4,5},{5,4},{6,7},{7,6},{8,10},{9,11},{10,... | collective-permute-start | bytes 884744 | tf_op jit(solution)/shard_map/ppermute | solution.py:54
  8.9 13.8 %collective-permute-start.8 = (bf16[64,2304]{1,0:T(8,128)(2,1)S(1)}, bf16[64,2304]{1,0:T(8,128)(2,1)S(1)}, u32[]{:S(2)}, u32[]{:S(2)}) collective-permute-start(bf16[64,2304]{1,0:T(8,128)(2,1)S(1)} %slice_bitcast_fusion.1), channel_id=1, source_target_pairs={{0,1},{1,0},{2,3},{3,2},{4,6},{5,7},{6,4},{7,5},{8,9},{9,8},{10,11... | collective-permute-start | bytes 884744 | tf_op jit(solution)/shard_map/ppermute | solution.py:54
  10.6 28.8 %copy-start.6 = (bf16[2,64,2304]{2,1,0:T(8,128)(2,1)S(1)}, bf16[2,64,2304]{2,1,0:T(8,128)(2,1)}, u32[]{:S(2)}) copy-start(bf16[2,64,2304]{2,1,0:T(8,128)(2,1)} %refs_7_.3) | copy-start | bytes 1769476
  10.6 5.2 %collective-permute-start.3 = (f32[80,128]{1,0:T(8,128)S(1)}, f32[80,128]{1,0:T(8,128)S(1)}, u32[]{:S(2)}, u32[]{:S(2)}) collective-permute-start(f32[80,128]{1,0:T(8,128)S(1)} %add.42), channel_id=1, source_target_pairs={{0,24},{4,28},{8,16},{12,20},{16,8},{20,12},{24,0},{28,4},{1,25},{... | collective-permute-start | bytes 122888 | tf_op jit(solution)/shard_map/ppermute | solution.py:19
  12.0 4.1 %collective-permute-start.2 = (f32[80,128]{1,0:T(8,128)S(1)}, f32[80,128]{1,0:T(8,128)S(1)}, u32[]{:S(2)}, u32[]{:S(2)}) collective-permute-start(f32[80,128]{1,0:T(8,128)S(1)} %add.42), channel_id=1, source_target_pairs={{0,16},{4,20},{8,24},{12,28},{16,0},{20,4},{24,8},{28,12},{1,17},{... | collective-permute-start | bytes 122888 | tf_op jit(solution)/shard_map/ppermute | solution.py:19
  12.8 4.0 %collective-permute-start.1 = (f32[80,128]{1,0:T(8,128)S(1)}, f32[80,128]{1,0:T(8,128)S(1)}, u32[]{:S(2)}, u32[]{:S(2)}) collective-permute-start(f32[80,128]{1,0:T(8,128)S(1)} %add.42), channel_id=1, source_target_pairs={{0,8},{4,12},{8,0},{12,4},{16,24},{20,28},{24,16},{28,20},{1,9},{5... | collective-permute-start | bytes 122888 | tf_op jit(solution)/shard_map/ppermute | solution.py:19
  16.8 9.2 %collective-permute-start.6 = (f32[80,128]{1,0:T(8,128)S(1)}, f32[80,128]{1,0:T(8,128)S(1)}, u32[]{:S(2)}, u32[]{:S(2)}) collective-permute-start(f32[80,128]{1,0:T(8,128)S(1)} %add_add_fusion.3), channel_id=1, source_target_pairs={{0,3},{1,2},{2,1},{3,0},{4,7},{5,6},{6,5},{7,4},{8,11},{9,10},{10,... | collective-permute-start | bytes 122888 | tf_op jit(solution)/shard_map/ppermute | solution.py:19
  17.4 8.7 %collective-permute-start.5 = (f32[80,128]{1,0:T(8,128)S(1)}, f32[80,128]{1,0:T(8,128)S(1)}, u32[]{:S(2)}, u32[]{:S(2)}) collective-permute-start(f32[80,128]{1,0:T(8,128)S(1)} %add_add_fusion.3), channel_id=1, source_target_pairs={{0,2},{1,3},{2,0},{3,1},{4,6},{5,7},{6,4},{7,5},{8,10},{9,11},{10,... | collective-permute-start | bytes 122888 | tf_op jit(solution)/shard_map/ppermute | solution.py:19
  18.8 7.3 %collective-permute-start.4 = (f32[80,128]{1,0:T(8,128)S(1)}, f32[80,128]{1,0:T(8,128)S(1)}, u32[]{:S(2)}, u32[]{:S(2)}) collective-permute-start(f32[80,128]{1,0:T(8,128)S(1)} %add_add_fusion.3), channel_id=1, source_target_pairs={{0,1},{1,0},{2,3},{3,2},{4,5},{5,4},{6,7},{7,6},{8,9},{9,8},{10,11... | collective-permute-start | bytes 122888 | tf_op jit(solution)/shard_map/ppermute | solution.py:19
  22.7 10.7 %collective-permute-start.10 = (bf16[64,2304]{1,0:T(8,128)(2,1)S(1)}, bf16[64,2304]{1,0:T(8,128)(2,1)S(1)}, u32[]{:S(2)}, u32[]{:S(2)}) collective-permute-start(bf16[64,2304]{1,0:T(8,128)(2,1)S(1)} %broadcast_select_fusion.1), channel_id=1, source_target_pairs={{0,1},{1,0},{2,3},{3,2},{4,5},{5,4},{6,7},{7,6},{8,9},{9,8},{10,11... | collective-permute-start | bytes 884744 | tf_op jit(solution)/shard_map/ppermute | solution.py:19
  26.1 1.3 %collective-permute-start.7 = (f32[80,128]{1,0:T(8,128)S(1)}, f32[80,128]{1,0:T(8,128)S(1)}, u32[]{:S(2)}, u32[]{:S(2)}) collective-permute-start(f32[80,128]{1,0:T(8,128)S(1)} %add_add_fusion.2.refs_2_), channel_id=1, source_target_pairs={{0,4},{4,0},{8,12},{12,8},{16,20},{20,16},{24,28},{28,24},{1,5},{5... | collective-permute-start | bytes 122888 | tf_op jit(solution)/shard_map/ppermute | solution.py:19
  39.3 5.3 %collective-permute-start.11 = (f32[80,128]{1,0:T(8,128)S(1)}, f32[80,128]{1,0:T(8,128)S(1)}, u32[]{:S(2)}, u32[]{:S(2)}) collective-permute-start(f32[80,128]{1,0:T(8,128)S(1)} %get-tuple-element.14), channel_id=1, source_target_pairs={{0,4},{4,0},{8,12},{12,8},{16,20},{20,16},{24,28},{28,24},{1,5},{5... | collective-permute-start | bytes 122888 | tf_op jit(solution)/shard_map/ppermute | solution.py:19
  39.4 15.2 %collective-permute-start.20 = (bf16[64,2304]{1,0:T(8,128)(2,1)S(1)}, bf16[64,2304]{1,0:T(8,128)(2,1)S(1)}, u32[]{:S(2)}, u32[]{:S(2)}) collective-permute-start(bf16[64,2304]{1,0:T(8,128)(2,1)S(1)} %slice_bitcast_fusion), channel_id=1, source_target_pairs={{0,2},{1,3},{2,0},{3,1},{4,5},{5,4},{6,7},{7,6},{8,10},{9,11},{10,... | collective-permute-start | bytes 884744 | tf_op jit(solution)/shard_map/ppermute | solution.py:54
  42.7 12.0 %collective-permute-start.19 = (bf16[64,2304]{1,0:T(8,128)(2,1)S(1)}, bf16[64,2304]{1,0:T(8,128)(2,1)S(1)}, u32[]{:S(2)}, u32[]{:S(2)}) collective-permute-start(bf16[64,2304]{1,0:T(8,128)(2,1)S(1)} %slice_bitcast_fusion), channel_id=1, source_target_pairs={{0,1},{1,0},{2,3},{3,2},{4,6},{5,7},{6,4},{7,5},{8,9},{9,8},{10,11... | collective-permute-start | bytes 884744 | tf_op jit(solution)/shard_map/ppermute | solution.py:54
  44.6 5.0 %collective-permute-start.14 = (f32[80,128]{1,0:T(8,128)S(1)}, f32[80,128]{1,0:T(8,128)S(1)}, u32[]{:S(2)}, u32[]{:S(2)}) collective-permute-start(f32[80,128]{1,0:T(8,128)S(1)} %add.49), channel_id=1, source_target_pairs={{0,24},{4,28},{8,16},{12,20},{16,8},{20,12},{24,0},{28,4},{1,25},{... | collective-permute-start | bytes 122888 | tf_op jit(solution)/shard_map/ppermute | solution.py:19
  44.7 4.9 %collective-permute-start.13 = (f32[80,128]{1,0:T(8,128)S(1)}, f32[80,128]{1,0:T(8,128)S(1)}, u32[]{:S(2)}, u32[]{:S(2)}) collective-permute-start(f32[80,128]{1,0:T(8,128)S(1)} %add.49), channel_id=1, source_target_pairs={{0,16},{4,20},{8,24},{12,28},{16,0},{20,4},{24,8},{28,12},{1,17},{... | collective-permute-start | bytes 122888 | tf_op jit(solution)/shard_map/ppermute | solution.py:19
  45.7 4.4 %collective-permute-start.12 = (f32[80,128]{1,0:T(8,128)S(1)}, f32[80,128]{1,0:T(8,128)S(1)}, u32[]{:S(2)}, u32[]{:S(2)}) collective-permute-start(f32[80,128]{1,0:T(8,128)S(1)} %add.49), channel_id=1, source_target_pairs={{0,8},{4,12},{8,0},{12,4},{16,24},{20,28},{24,16},{28,20},{1,9},{5... | collective-permute-start | bytes 122888 | tf_op jit(solution)/shard_map/ppermute | solution.py:19
  50.1 9.8 %collective-permute-start.17 = (f32[80,128]{1,0:T(8,128)S(1)}, f32[80,128]{1,0:T(8,128)S(1)}, u32[]{:S(2)}, u32[]{:S(2)}) collective-permute-start(f32[80,128]{1,0:T(8,128)S(1)} %add_add_fusion.1), channel_id=1, source_target_pairs={{0,3},{1,2},{2,1},{3,0},{4,7},{5,6},{6,5},{7,4},{8,11},{9,10},{10,... | collective-permute-start | bytes 122888 | tf_op jit(solution)/shard_map/ppermute | solution.py:19
  50.7 9.3 %collective-permute-start.16 = (f32[80,128]{1,0:T(8,128)S(1)}, f32[80,128]{1,0:T(8,128)S(1)}, u32[]{:S(2)}, u32[]{:S(2)}) collective-permute-start(f32[80,128]{1,0:T(8,128)S(1)} %add_add_fusion.1), channel_id=1, source_target_pairs={{0,2},{1,3},{2,0},{3,1},{4,6},{5,7},{6,4},{7,5},{8,10},{9,11},{10,... | collective-permute-start | bytes 122888 | tf_op jit(solution)/shard_map/ppermute | solution.py:19
  51.8 8.1 %collective-permute-start.15 = (f32[80,128]{1,0:T(8,128)S(1)}, f32[80,128]{1,0:T(8,128)S(1)}, u32[]{:S(2)}, u32[]{:S(2)}) collective-permute-start(f32[80,128]{1,0:T(8,128)S(1)} %add_add_fusion.1), channel_id=1, source_target_pairs={{0,1},{1,0},{2,3},{3,2},{4,5},{5,4},{6,7},{7,6},{8,9},{9,8},{10,11... | collective-permute-start | bytes 122888 | tf_op jit(solution)/shard_map/ppermute | solution.py:19
  54.7 12.1 %collective-permute-start.21 = (bf16[64,2304]{1,0:T(8,128)(2,1)S(1)}, bf16[64,2304]{1,0:T(8,128)(2,1)S(1)}, u32[]{:S(2)}, u32[]{:S(2)}) collective-permute-start(bf16[64,2304]{1,0:T(8,128)(2,1)S(1)} %broadcast_select_fusion), channel_id=1, source_target_pairs={{0,1},{1,0},{2,3},{3,2},{4,5},{5,4},{6,7},{7,6},{8,9},{9,8},{10,11... | collective-permute-start | bytes 884744 | tf_op jit(solution)/shard_map/ppermute | solution.py:19
  60.0 6.9 %collective-permute-start.18 = (f32[80,128]{1,0:T(8,128)S(1)}, f32[80,128]{1,0:T(8,128)S(1)}, u32[]{:S(2)}, u32[]{:S(2)}) collective-permute-start(f32[80,128]{1,0:T(8,128)S(1)} %add_add_fusion.refs_0_), channel_id=1, source_target_pairs={{0,4},{4,0},{8,12},{12,8},{16,20},{20,16},{24,28},{28,24},{1,5},{5... | collective-permute-start | bytes 122888 | tf_op jit(solution)/shard_map/ppermute | solution.py:19

commit v8 on v7

--- a/solution.py
+++ b/solution.py
@@ -34,14 +34,14 @@
 
 def add_over(keep, send):
     half = keep + swap(send, "slab", 1)
-    rounds = list(rounds_of("slab", 2)) + list(rounds_of("lev", 1))
+    rounds = list(rounds_of("lev", 1)) + list(rounds_of("slab", 2))
     for axis, distances in rounds:
         half = sum([swap(half, axis, d) for d in distances], half)
     return half, swap(half, "slab", 1)
 
 
-def paired_rows(groups):
-    return groups == 4
+def paired_rows(groups, b):
+    return groups == 4 and b == 0
 
 
 def swap_either(value, even_bit, odd_bit):
@@ -54,9 +54,9 @@
     return lax.ppermute(value, ("slab", "lev"), pairs)
 
 
-def rows_over(own):
+def rows_over(own, b):
     size = lax.axis_size("lev")
-    if paired_rows(size):
+    if paired_rows(size, b):
         far_even = swap_either(own, 2, 1)
         far_odd = swap_either(own, 1, 2)
         passed = jnp.where((lax.axis_index("slab") & 1) == 0, far_even, far_odd)
@@ -165,7 +165,7 @@
     split_halves(place_ref[1] & 1, sum_ref, keep_ref, send_ref)
 
 
-def regroup(value, lev_index, side, groups):
+def regroup(value, lev_index, side, groups, b):
     total = value.shape[1]
     block = total // groups
     lane = lax.broadcasted_iota(jnp.int32, value.shape, 1)
@@ -177,7 +177,7 @@
         )
         value = jnp.where((lev_index & bit) != 0, other, value)
         bit *= 2
-    if paired_rows(groups):
+    if paired_rows(groups, b):
         low, high = pltpu.roll(value, total - block, 1), pltpu.roll(value, block, 1)
         inner = jnp.where(lane < 2 * block, low, high)
         crossed = (side == 1) & (lane >= block) & (lane < 3 * block)
@@ -201,12 +201,12 @@
     total_var = spread + variance
     shrink = 1.0 / (1.0 + jnp.sqrt(variance / total_var))
     gain = ((value_ref[b : b + 1] - obs_mean) - deviation * shrink) / (total_var * (members - 1.0))
-    gain_ref[...] = regroup(gain, lev_index, side, groups).astype(jnp.bfloat16)
+    gain_ref[...] = regroup(gain, lev_index, side, groups, b).astype(jnp.bfloat16)
     pad = jnp.zeros((LANES - members, n_obs), jnp.float32)
-    dev_all = jnp.concatenate([regroup(deviation, lev_index, side, groups), pad], axis=0)
+    dev_all = jnp.concatenate([regroup(deviation, lev_index, side, groups, b), pad], axis=0)
     dev_ref[...] = dev_all.T[:, :members].astype(jnp.bfloat16)
     level_all = jnp.concatenate(
-        [regroup(level_ref[b], lev_index, side, groups), jnp.zeros((LANES - lev_rows, n_obs), jnp.float32)], axis=0
+        [regroup(level_ref[b], lev_index, side, groups, b), jnp.zeros((LANES - lev_rows, n_obs), jnp.float32)], axis=0
     ).T
     for l in range(lev_rows):
         level_b_ref[l] = jnp.broadcast_to(level_all[:, l : l + 1], (n_obs, LANES))
@@ -311,7 +311,7 @@
     dma = pltpu.SemaphoreType.DMA((lev_rows,))
     one_dma = pltpu.SemaphoreType.DMA
 
-    shards = [rows_over(loc_column[0])]
+    shards = [rows_over(loc_column[0], 0)]
 
     keep, send = pl.pallas_call(
         with_place(functools.partial(prior_kernel, sizes)),
@@ -323,7 +323,7 @@
         name="cells",
     )(*place, *far(obs_frac, obs_cell, ensemble))
     later_rows, keep = lax.optimization_barrier((loc_column, keep))
-    shards.append(rows_over(later_rows[1]))
+    shards.append(rows_over(later_rows[1], 1))
     ours, theirs = add_over(keep, send)
 
     current, mean_first, keep, send = pl.pallas_call(

time: 72.5 us -> 88.1 us (1.22)
  waiting for transfers between devices: 19.4 us -> 42.5 us
  starting transfers between devices: 36.4 us -> 29 us
    ppermute x18 -> x20, waiting for transfers between devices: 18 us -> 42.5 us  [swap(): return lax.ppermute(value, axis, [(i, i ^ bit) for i in range(size)])]
    ppermute x4 -> x2, starting transfers between devices: 10.9 us -> 5.71 us  [swap_either(): return lax.ppermute(value, ('slab', 'lev'), pairs)]
    ppermute x18 -> x20, starting transfers between devices: 25.5 us -> 23.3 us  [swap(): return lax.ppermute(value, axis, [(i, i ^ bit) for i in range(size)])]
    ppermute x4 -> x2, waiting for transfers between devices: 1.45 us -> 0.01 us  [swap_either(): return lax.ppermute(value, ('slab', 'lev'), pairs)]
where the time goes in v8:
time: 88.1 us; the launch traced here: 87.9 us
  waiting for transfers between devices  42.5 us (48%)
  starting transfers between devices  29 us (33%)
  Pallas kernels  15.4 us (17%)
    ppermute x20, waiting for transfers between devices, swap(): return lax.ppermute(value, axis, [(i, i ^ bit) for i in range(size)])  42.5 us
    ppermute x20, starting transfers between devices, swap(): return lax.ppermute(value, axis, [(i, i ^ bit) for i in range(size)])  23.3 us
    pallas_call x1, Pallas kernels, on_device(): pl.pallas_call(with_place(functools.partial(first_kernel, groups, sizes))...  5.93 us
    ppermute x2, starting transfers between devices, swap_either(): return lax.ppermute(value, ('slab', 'lev'), pairs)  5.71 us
    pallas_call x1, Pallas kernels, on_device(): pl.pallas_call(with_place(functools.partial(last_kernel, groups)), out_sh...  5.4 us
    pallas_call x1, Pallas kernels, on_device(): pl.pallas_call(with_place(functools.partial(prior_kernel, sizes)), out_sh...  4.07 us
  transfers between devices with their start and end apart: 22, of which 10 were waited for; matrix products, arithmetic and copies ran while one was open for 0% of the time, Pallas kernels for 0%

profile of v8, /device:TPU:0, one launch (start us, length us, event | category | flops | bytes accessed | tf_op | source)
XLA Modules:
  0.0 87.9 jit_solution(5874395197687434731)
XLA Ops:
  0.7 4.1 %cells.1 = (f32[80,128]{1,0:T(8,128)S(1)}, f32[80,128]{1,0:T(8,128)S(1)}) custom-call(s32[1]{0:T(128)} %bitcast.lev_ref, s32[1]{0:T(128)} %bitcast.1.slab_ref, f32[2,256]{1,0:T(2,128)} %refs_0_.3, s32[2,256]{1,0:T(2,128)} %refs_1_.3, f32[80,4,2304]{2,1,0:T(4,128)} %refs_7_.2), custom_call_target="tpu_custom_call" | custom-call | tf_op jit(solution)/shard_map/cells/pallas_call | solution.py:316
  4.8 0.1 collective-permute-start
  4.9 4.0 %collective-permute-start.9 = (bf16[64,2304]{1,0:T(8,128)(2,1)S(1)}, bf16[64,2304]{1,0:T(8,128)(2,1)S(1)}, u32[]{:S(2)}, u32[]{:S(2)}) collective-permute-start(bf16[64,2304]{1,0:T(8,128)(2,1)S(1)} %slice_bitcast_fusion.1), channel_id=1, source_target_pairs={{0,2},{1,3},{2,0},{3,1},{4,5},{5,4},{6,7},{7,6},{8,10},{9,11},{10,... | collective-permute-start | bytes 884744 | tf_op jit(solution)/shard_map/ppermute | solution.py:54
  8.9 1.7 %collective-permute-start.8 = (bf16[64,2304]{1,0:T(8,128)(2,1)S(1)}, bf16[64,2304]{1,0:T(8,128)(2,1)S(1)}, u32[]{:S(2)}, u32[]{:S(2)}) collective-permute-start(bf16[64,2304]{1,0:T(8,128)(2,1)S(1)} %slice_bitcast_fusion.1), channel_id=1, source_target_pairs={{0,1},{1,0},{2,3},{3,2},{4,6},{5,7},{6,4},{7,5},{8,9},{9,8},{10,11... | collective-permute-start | bytes 884744 | tf_op jit(solution)/shard_map/ppermute | solution.py:54
  10.6 0.5 collective-permute-start.3
  11.2 1.3 %collective-permute-start.2 = (f32[80,128]{1,0:T(8,128)S(1)}, f32[80,128]{1,0:T(8,128)S(1)}, u32[]{:S(2)}, u32[]{:S(2)}) collective-permute-start(f32[80,128]{1,0:T(8,128)S(1)} %add.42), channel_id=1, source_target_pairs={{0,2},{1,3},{2,0},{3,1},{4,6},{5,7},{6,4},{7,5},{8,10},{9,11},{10,... | collective-permute-start | bytes 122888 | tf_op jit(solution)/shard_map/ppermute | solution.py:19
  12.4 2.6 %collective-permute-start.1 = (f32[80,128]{1,0:T(8,128)S(1)}, f32[80,128]{1,0:T(8,128)S(1)}, u32[]{:S(2)}, u32[]{:S(2)}) collective-permute-start(f32[80,128]{1,0:T(8,128)S(1)} %add.42), channel_id=1, source_target_pairs={{0,1},{1,0},{2,3},{3,2},{4,5},{5,4},{6,7},{7,6},{8,9},{9,8},{10,11... | collective-permute-start | bytes 122888 | tf_op jit(solution)/shard_map/ppermute | solution.py:19
  15.1 10.4 %collective-permute-done.3 = f32[80,128]{1,0:T(8,128)S(1)} collective-permute-done((f32[80,128]{1,0:T(8,128)S(1)}, f32[80,128]{1,0:T(8,128)S(1)}, u32[]{:S(2)}, u32[]{:S(2)}) %collective-permute-start.3) | collective-permute-done | bytes 40992 | tf_op jit(solution)/shard_map/ppermute | solution.py:19
  25.5 2.1 %collective-permute-start.6 = (f32[80,128]{1,0:T(8,128)S(1)}, f32[80,128]{1,0:T(8,128)S(1)}, u32[]{:S(2)}, u32[]{:S(2)}) collective-permute-start(f32[80,128]{1,0:T(8,128)S(1)} %add_add_fusion.3), channel_id=1, source_target_pairs={{0,24},{4,28},{8,16},{12,20},{16,8},{20,12},{24,0},{28,4},{1,25},{... | collective-permute-start | bytes 122888 | tf_op jit(solution)/shard_map/ppermute | solution.py:19
  27.6 0.4 collective-permute-start.5
  28.1 1.0 %collective-permute-start.4 = (f32[80,128]{1,0:T(8,128)S(1)}, f32[80,128]{1,0:T(8,128)S(1)}, u32[]{:S(2)}, u32[]{:S(2)}) collective-permute-start(f32[80,128]{1,0:T(8,128)S(1)} %add_add_fusion.3), channel_id=1, source_target_pairs={{0,8},{4,12},{8,0},{12,4},{16,24},{20,28},{24,16},{28,20},{1,9},{5... | collective-permute-start | bytes 122888 | tf_op jit(solution)/shard_map/ppermute | solution.py:19
  29.1 2.0 %collective-permute-start.10 = (bf16[64,2304]{1,0:T(8,128)(2,1)S(1)}, bf16[64,2304]{1,0:T(8,128)(2,1)S(1)}, u32[]{:S(2)}, u32[]{:S(2)}) collective-permute-start(bf16[64,2304]{1,0:T(8,128)(2,1)S(1)} %broadcast_select_fusion), channel_id=1, source_target_pairs={{0,1},{1,0},{2,3},{3,2},{4,5},{5,4},{6,7},{7,6},{8,9},{9,8},{10,11... | collective-permute-start | bytes 884744 | tf_op jit(solution)/shard_map/ppermute | solution.py:19
  31.1 0.6 collective-permute-done.5
  31.8 0.3 collective-permute-done.4
  32.1 0.1 collective-permute-start.7
  32.2 1.2 %collective-permute-done.7.refs_3_ = f32[80,128]{1,0:T(8,128)S(1)} collective-permute-done((f32[80,128]{1,0:T(8,128)S(1)}, f32[80,128]{1,0:T(8,128)S(1)}, u32[]{:S(2)}, u32[]{:S(2)}) %collective-permute-start.7) | collective-permute-done | bytes 40992 | tf_op jit(solution)/shard_map/ppermute | solution.py:19
  33.4 4.8 %collective-permute-done.10.refs_11_ = bf16[64,2304]{1,0:T(8,128)(2,1)S(1)} collective-permute-done((bf16[64,2304]{1,0:T(8,128)(2,1)S(1)}, bf16[64,2304]{1,0:T(8,128)(2,1)S(1)}, u32[]{:S(2)}, u32[]{:S(2)}) %collective-permute-start.10) | collective-permute-done | bytes 294944 | tf_op jit(solution)/shard_map/ppermute | solution.py:19
  38.2 5.9 %block_first.1 = (f32[4,80,2304]{2,1,0:T(8,128)S(1)}, f32[1,256]{1,0:T(1,128)S(1)}, f32[80,128]{1,0:T(8,128)S(1)}, f32[80,128]{1,0:T(8,128)S(1)}) custom-call(s32[1]{0:T(128)} %bitcast.lev_ref, s32[1]{0:T(128)} %bitcast.1.slab_ref, f32[2,256]{1,0:T(2,128)S(1)} %copy-done.3, s32[2,256]{1,0:T(2,128)S(1)} %copy-done.4, f32[80,128]{1,0:T(8,128)S(1)} %add_add_fusion.2.refs_2_, ...), custom_call_target="tpu_custom_call" | custom-call | tf_op jit(solution)/shard_map/block_first/pallas_call | solution.py:329
  44.3 2.9 %collective-permute-start.20 = (bf16[64,2304]{1,0:T(8,128)(2,1)S(1)}, bf16[64,2304]{1,0:T(8,128)(2,1)S(1)}, u32[]{:S(2)}, u32[]{:S(2)}) collective-permute-start(bf16[64,2304]{1,0:T(8,128)(2,1)S(1)} %slice_bitcast_fusion), channel_id=1, source_target_pairs={{0,2},{1,3},{2,0},{3,1},{4,6},{5,7},{6,4},{7,5},{8,10},{9,11},{10,... | collective-permute-start | bytes 884744 | tf_op jit(solution)/shard_map/ppermute | solution.py:19
  47.2 2.4 %collective-permute-start.14 = (f32[80,128]{1,0:T(8,128)S(1)}, f32[80,128]{1,0:T(8,128)S(1)}, u32[]{:S(2)}, u32[]{:S(2)}) collective-permute-start(f32[80,128]{1,0:T(8,128)S(1)} %add.49), channel_id=1, source_target_pairs={{0,3},{1,2},{2,1},{3,0},{4,7},{5,6},{6,5},{7,4},{8,11},{9,10},{10,... | collective-permute-start | bytes 122888 | tf_op jit(solution)/shard_map/ppermute | solution.py:19
  49.6 1.0 %collective-permute-start.13 = (f32[80,128]{1,0:T(8,128)S(1)}, f32[80,128]{1,0:T(8,128)S(1)}, u32[]{:S(2)}, u32[]{:S(2)}) collective-permute-start(f32[80,128]{1,0:T(8,128)S(1)} %add.49), channel_id=1, source_target_pairs={{0,2},{1,3},{2,0},{3,1},{4,6},{5,7},{6,4},{7,5},{8,10},{9,11},{10,... | collective-permute-start | bytes 122888 | tf_op jit(solution)/shard_map/ppermute | solution.py:19
  50.6 1.0 %collective-permute-start.12 = (f32[80,128]{1,0:T(8,128)S(1)}, f32[80,128]{1,0:T(8,128)S(1)}, u32[]{:S(2)}, u32[]{:S(2)}) collective-permute-start(f32[80,128]{1,0:T(8,128)S(1)} %add.49), channel_id=1, source_target_pairs={{0,1},{1,0},{2,3},{3,2},{4,5},{5,4},{6,7},{7,6},{8,9},{9,8},{10,11... | collective-permute-start | bytes 122888 | tf_op jit(solution)/shard_map/ppermute | solution.py:19
  51.6 5.7 %collective-permute-done.14 = f32[80,128]{1,0:T(8,128)S(1)} collective-permute-done((f32[80,128]{1,0:T(8,128)S(1)}, f32[80,128]{1,0:T(8,128)S(1)}, u32[]{:S(2)}, u32[]{:S(2)}) %collective-permute-start.14) | collective-permute-done | bytes 40992 | tf_op jit(solution)/shard_map/ppermute | solution.py:19
  57.4 7.3 %collective-permute-done.13 = f32[80,128]{1,0:T(8,128)S(1)} collective-permute-done((f32[80,128]{1,0:T(8,128)S(1)}, f32[80,128]{1,0:T(8,128)S(1)}, u32[]{:S(2)}, u32[]{:S(2)}) %collective-permute-start.13) | collective-permute-done | bytes 40992 | tf_op jit(solution)/shard_map/ppermute | solution.py:19
  64.7 0.8 collective-permute-start.17
  65.5 0.9 collective-permute-start.16
  66.3 1.9 %collective-permute-start.15 = (f32[80,128]{1,0:T(8,128)S(1)}, f32[80,128]{1,0:T(8,128)S(1)}, u32[]{:S(2)}, u32[]{:S(2)}) collective-permute-start(f32[80,128]{1,0:T(8,128)S(1)} %add_add_fusion.1), channel_id=1, source_target_pairs={{0,8},{4,12},{8,0},{12,4},{16,24},{20,28},{24,16},{28,20},{1,9},{5... | collective-permute-start | bytes 122888 | tf_op jit(solution)/shard_map/ppermute | solution.py:19
  68.2 0.7 collective-permute-start.19
  69.0 1.3 %collective-permute-start.21 = (bf16[64,2304]{1,0:T(8,128)(2,1)S(1)}, bf16[64,2304]{1,0:T(8,128)(2,1)S(1)}, u32[]{:S(2)}, u32[]{:S(2)}) collective-permute-start(bf16[64,2304]{1,0:T(8,128)(2,1)S(1)} %collective-permute-done.20.refs_9_), channel_id=1, source_target_pairs={{0,1},{1,0},{2,3},{3,2},{4,5},{5,4},{6,7},{7,6},{8,9},{9,8},{10,11... | collective-permute-start | bytes 884744 | tf_op jit(solution)/shard_map/ppermute | solution.py:19
  70.4 7.7 %collective-permute-done.19.refs_8_ = bf16[64,2304]{1,0:T(8,128)(2,1)S(1)} collective-permute-done((bf16[64,2304]{1,0:T(8,128)(2,1)S(1)}, bf16[64,2304]{1,0:T(8,128)(2,1)S(1)}, u32[]{:S(2)}, u32[]{:S(2)}) %collective-permute-start.19) | collective-permute-done | bytes 294944 | tf_op jit(solution)/shard_map/ppermute | solution.py:19
  78.1 4.3 %collective-permute-done.21.refs_10_ = bf16[64,2304]{1,0:T(8,128)(2,1)S(1)} collective-permute-done((bf16[64,2304]{1,0:T(8,128)(2,1)S(1)}, bf16[64,2304]{1,0:T(8,128)(2,1)S(1)}, u32[]{:S(2)}, u32[]{:S(2)}) %collective-permute-start.21) | collective-permute-done | bytes 294944 | tf_op jit(solution)/shard_map/ppermute | solution.py:19
  82.5 5.4 %block_last.1 = (f32[80,4,2304]{2,1,0:T(4,128)}, f32[2,256]{1,0:T(2,128)}) custom-call(s32[1]{0:T(128)} %bitcast.lev_ref, s32[1]{0:T(128)} %bitcast.1.slab_ref, f32[80,128]{1,0:T(8,128)S(1)} %add_add_fusion.refs_0_, f32[80,128]{1,0:T(8,128)S(1)} %collective-permute-done.18.refs_1_, f32[2,256]{1,0:T(2,128)S(1)} %copy-done.1, f32[2,256]{1,0:T(2,128)S(1)} %copy-done.2, ...), custom_call_target="tpu_custom_call" | custom-call | tf_op jit(solution)/shard_map/block_last/pallas_call | solution.py:340
  (38 shorter events, 0.4 us)
Async XLA Ops:
  0.6 37.5 %copy-start.3 = (f32[2,256]{1,0:T(2,128)S(1)}, f32[2,256]{1,0:T(2,128)}, u32[]{:S(2)}) copy-start(f32[2,256]{1,0:T(2,128)} %refs_0_.3) | copy-start | bytes 6148
  0.6 37.5 %copy-start.4 = (s32[2,256]{1,0:T(2,128)S(1)}, s32[2,256]{1,0:T(2,128)}, u32[]{:S(2)}) copy-start(s32[2,256]{1,0:T(2,128)} %refs_1_.3) | copy-start | bytes 6148
  0.7 4.2 %copy-start.5 = (bf16[2,64,2304]{2,1,0:T(8,128)(2,1)S(1)}, bf16[2,64,2304]{2,1,0:T(8,128)(2,1)}, u32[]{:S(2)}) copy-start(bf16[2,64,2304]{2,1,0:T(8,128)(2,1)} %refs_7_.3) | copy-start | bytes 1769476
  0.7 37.5 %copy-start.2 = (f32[2,256]{1,0:T(2,128)S(1)}, f32[2,256]{1,0:T(2,128)}, u32[]{:S(2)}) copy-start(f32[2,256]{1,0:T(2,128)} %refs_3_.1) | copy-start | bytes 6148
  0.7 37.5 %copy-start.1 = (f32[2,256]{1,0:T(2,128)S(1)}, f32[2,256]{1,0:T(2,128)}, u32[]{:S(2)}) copy-start(f32[2,256]{1,0:T(2,128)} %refs_2_.3) | copy-start | bytes 6148
  0.7 37.5 %copy-start = (f32[2,256,4]{1,2,0:T(4,128)S(1)}, f32[2,256,4]{1,2,0:T(4,128)}, u32[]{:S(2)}) copy-start(f32[2,256,4]{1,2,0:T(4,128)} %param.13) | copy-start | bytes 24580
  4.8 5.8 %collective-permute-start = (f32[80,128]{1,0:T(8,128)S(1)}, f32[80,128]{1,0:T(8,128)S(1)}, u32[]{:S(2)}, u32[]{:S(2)}) collective-permute-start(f32[80,128]{1,0:T(8,128)S(1)} %get-tuple-element.12), channel_id=1, source_target_pairs={{0,4},{4,0},{8,12},{12,8},{16,20},{20,16},{24,28},{28,24},{1,5},{5... | collective-permute-start | bytes 122888 | tf_op jit(solution)/shard_map/ppermute | solution.py:19
  4.9 24.2 %collective-permute-start.9 = (bf16[64,2304]{1,0:T(8,128)(2,1)S(1)}, bf16[64,2304]{1,0:T(8,128)(2,1)S(1)}, u32[]{:S(2)}, u32[]{:S(2)}) collective-permute-start(bf16[64,2304]{1,0:T(8,128)(2,1)S(1)} %slice_bitcast_fusion.1), channel_id=1, source_target_pairs={{0,2},{1,3},{2,0},{3,1},{4,5},{5,4},{6,7},{7,6},{8,10},{9,11},{10,... | collective-permute-start | bytes 884744 | tf_op jit(solution)/shard_map/ppermute | solution.py:54
  8.9 20.2 %collective-permute-start.8 = (bf16[64,2304]{1,0:T(8,128)(2,1)S(1)}, bf16[64,2304]{1,0:T(8,128)(2,1)S(1)}, u32[]{:S(2)}, u32[]{:S(2)}) collective-permute-start(bf16[64,2304]{1,0:T(8,128)(2,1)S(1)} %slice_bitcast_fusion.1), channel_id=1, source_target_pairs={{0,1},{1,0},{2,3},{3,2},{4,6},{5,7},{6,4},{7,5},{8,9},{9,8},{10,11... | collective-permute-start | bytes 884744 | tf_op jit(solution)/shard_map/ppermute | solution.py:54
  10.6 33.6 %copy-start.6 = (bf16[2,64,2304]{2,1,0:T(8,128)(2,1)S(1)}, bf16[2,64,2304]{2,1,0:T(8,128)(2,1)}, u32[]{:S(2)}) copy-start(bf16[2,64,2304]{2,1,0:T(8,128)(2,1)} %refs_7_.3) | copy-start | bytes 1769476
  10.6 14.9 %collective-permute-start.3 = (f32[80,128]{1,0:T(8,128)S(1)}, f32[80,128]{1,0:T(8,128)S(1)}, u32[]{:S(2)}, u32[]{:S(2)}) collective-permute-start(f32[80,128]{1,0:T(8,128)S(1)} %add.42), channel_id=1, source_target_pairs={{0,3},{1,2},{2,1},{3,0},{4,7},{5,6},{6,5},{7,4},{8,11},{9,10},{10,... | collective-permute-start | bytes 122888 | tf_op jit(solution)/shard_map/ppermute | solution.py:19
  11.2 14.3 %collective-permute-start.2 = (f32[80,128]{1,0:T(8,128)S(1)}, f32[80,128]{1,0:T(8,128)S(1)}, u32[]{:S(2)}, u32[]{:S(2)}) collective-permute-start(f32[80,128]{1,0:T(8,128)S(1)} %add.42), channel_id=1, source_target_pairs={{0,2},{1,3},{2,0},{3,1},{4,6},{5,7},{6,4},{7,5},{8,10},{9,11},{10,... | collective-permute-start | bytes 122888 | tf_op jit(solution)/shard_map/ppermute | solution.py:19
  12.4 13.1 %collective-permute-start.1 = (f32[80,128]{1,0:T(8,128)S(1)}, f32[80,128]{1,0:T(8,128)S(1)}, u32[]{:S(2)}, u32[]{:S(2)}) collective-permute-start(f32[80,128]{1,0:T(8,128)S(1)} %add.42), channel_id=1, source_target_pairs={{0,1},{1,0},{2,3},{3,2},{4,5},{5,4},{6,7},{7,6},{8,9},{9,8},{10,11... | collective-permute-start | bytes 122888 | tf_op jit(solution)/shard_map/ppermute | solution.py:19
  25.5 5.6 %collective-permute-start.6 = (f32[80,128]{1,0:T(8,128)S(1)}, f32[80,128]{1,0:T(8,128)S(1)}, u32[]{:S(2)}, u32[]{:S(2)}) collective-permute-start(f32[80,128]{1,0:T(8,128)S(1)} %add_add_fusion.3), channel_id=1, source_target_pairs={{0,24},{4,28},{8,16},{12,20},{16,8},{20,12},{24,0},{28,4},{1,25},{... | collective-permute-start | bytes 122888 | tf_op jit(solution)/shard_map/ppermute | solution.py:19
  27.6 4.1 %collective-permute-start.5 = (f32[80,128]{1,0:T(8,128)S(1)}, f32[80,128]{1,0:T(8,128)S(1)}, u32[]{:S(2)}, u32[]{:S(2)}) collective-permute-start(f32[80,128]{1,0:T(8,128)S(1)} %add_add_fusion.3), channel_id=1, source_target_pairs={{0,16},{4,20},{8,24},{12,28},{16,0},{20,4},{24,8},{28,12},{1,17},{... | collective-permute-start | bytes 122888 | tf_op jit(solution)/shard_map/ppermute | solution.py:19
  28.1 4.0 %collective-permute-start.4 = (f32[80,128]{1,0:T(8,128)S(1)}, f32[80,128]{1,0:T(8,128)S(1)}, u32[]{:S(2)}, u32[]{:S(2)}) collective-permute-start(f32[80,128]{1,0:T(8,128)S(1)} %add_add_fusion.3), channel_id=1, source_target_pairs={{0,8},{4,12},{8,0},{12,4},{16,24},{20,28},{24,16},{28,20},{1,9},{5... | collective-permute-start | bytes 122888 | tf_op jit(solution)/shard_map/ppermute | solution.py:19
  29.1 9.1 %collective-permute-start.10 = (bf16[64,2304]{1,0:T(8,128)(2,1)S(1)}, bf16[64,2304]{1,0:T(8,128)(2,1)S(1)}, u32[]{:S(2)}, u32[]{:S(2)}) collective-permute-start(bf16[64,2304]{1,0:T(8,128)(2,1)S(1)} %broadcast_select_fusion), channel_id=1, source_target_pairs={{0,1},{1,0},{2,3},{3,2},{4,5},{5,4},{6,7},{7,6},{8,9},{9,8},{10,11... | collective-permute-start | bytes 884744 | tf_op jit(solution)/shard_map/ppermute | solution.py:19
  32.1 1.3 %collective-permute-start.7 = (f32[80,128]{1,0:T(8,128)S(1)}, f32[80,128]{1,0:T(8,128)S(1)}, u32[]{:S(2)}, u32[]{:S(2)}) collective-permute-start(f32[80,128]{1,0:T(8,128)S(1)} %add_add_fusion.2.refs_2_), channel_id=1, source_target_pairs={{0,4},{4,0},{8,12},{12,8},{16,20},{20,16},{24,28},{28,24},{1,5},{5... | collective-permute-start | bytes 122888 | tf_op jit(solution)/shard_map/ppermute | solution.py:19
  44.1 3.0 %collective-permute-start.11 = (f32[80,128]{1,0:T(8,128)S(1)}, f32[80,128]{1,0:T(8,128)S(1)}, u32[]{:S(2)}, u32[]{:S(2)}) collective-permute-start(f32[80,128]{1,0:T(8,128)S(1)} %get-tuple-element.14), channel_id=1, source_target_pairs={{0,4},{4,0},{8,12},{12,8},{16,20},{20,16},{24,28},{28,24},{1,5},{5... | collective-permute-start | bytes 122888 | tf_op jit(solution)/shard_map/ppermute | solution.py:19
  44.3 24.7 %collective-permute-start.20 = (bf16[64,2304]{1,0:T(8,128)(2,1)S(1)}, bf16[64,2304]{1,0:T(8,128)(2,1)S(1)}, u32[]{:S(2)}, u32[]{:S(2)}) collective-permute-start(bf16[64,2304]{1,0:T(8,128)(2,1)S(1)} %slice_bitcast_fusion), channel_id=1, source_target_pairs={{0,2},{1,3},{2,0},{3,1},{4,6},{5,7},{6,4},{7,5},{8,10},{9,11},{10,... | collective-permute-start | bytes 884744 | tf_op jit(solution)/shard_map/ppermute | solution.py:19
  47.2 10.2 %collective-permute-start.14 = (f32[80,128]{1,0:T(8,128)S(1)}, f32[80,128]{1,0:T(8,128)S(1)}, u32[]{:S(2)}, u32[]{:S(2)}) collective-permute-start(f32[80,128]{1,0:T(8,128)S(1)} %add.49), channel_id=1, source_target_pairs={{0,3},{1,2},{2,1},{3,0},{4,7},{5,6},{6,5},{7,4},{8,11},{9,10},{10,... | collective-permute-start | bytes 122888 | tf_op jit(solution)/shard_map/ppermute | solution.py:19
  49.6 15.0 %collective-permute-start.13 = (f32[80,128]{1,0:T(8,128)S(1)}, f32[80,128]{1,0:T(8,128)S(1)}, u32[]{:S(2)}, u32[]{:S(2)}) collective-permute-start(f32[80,128]{1,0:T(8,128)S(1)} %add.49), channel_id=1, source_target_pairs={{0,2},{1,3},{2,0},{3,1},{4,6},{5,7},{6,4},{7,5},{8,10},{9,11},{10,... | collective-permute-start | bytes 122888 | tf_op jit(solution)/shard_map/ppermute | solution.py:19
  50.6 14.0 %collective-permute-start.12 = (f32[80,128]{1,0:T(8,128)S(1)}, f32[80,128]{1,0:T(8,128)S(1)}, u32[]{:S(2)}, u32[]{:S(2)}) collective-permute-start(f32[80,128]{1,0:T(8,128)S(1)} %add.49), channel_id=1, source_target_pairs={{0,1},{1,0},{2,3},{3,2},{4,5},{5,4},{6,7},{7,6},{8,9},{9,8},{10,11... | collective-permute-start | bytes 122888 | tf_op jit(solution)/shard_map/ppermute | solution.py:19
  64.7 5.6 %collective-permute-start.17 = (f32[80,128]{1,0:T(8,128)S(1)}, f32[80,128]{1,0:T(8,128)S(1)}, u32[]{:S(2)}, u32[]{:S(2)}) collective-permute-start(f32[80,128]{1,0:T(8,128)S(1)} %add_add_fusion.1), channel_id=1, source_target_pairs={{0,24},{4,28},{8,16},{12,20},{16,8},{20,12},{24,0},{28,4},{1,25},{... | collective-permute-start | bytes 122888 | tf_op jit(solution)/shard_map/ppermute | solution.py:19
  65.5 4.8 %collective-permute-start.16 = (f32[80,128]{1,0:T(8,128)S(1)}, f32[80,128]{1,0:T(8,128)S(1)}, u32[]{:S(2)}, u32[]{:S(2)}) collective-permute-start(f32[80,128]{1,0:T(8,128)S(1)} %add_add_fusion.1), channel_id=1, source_target_pairs={{0,16},{4,20},{8,24},{12,28},{16,0},{20,4},{24,8},{28,12},{1,17},{... | collective-permute-start | bytes 122888 | tf_op jit(solution)/shard_map/ppermute | solution.py:19
  66.3 4.0 %collective-permute-start.15 = (f32[80,128]{1,0:T(8,128)S(1)}, f32[80,128]{1,0:T(8,128)S(1)}, u32[]{:S(2)}, u32[]{:S(2)}) collective-permute-start(f32[80,128]{1,0:T(8,128)S(1)} %add_add_fusion.1), channel_id=1, source_target_pairs={{0,8},{4,12},{8,0},{12,4},{16,24},{20,28},{24,16},{28,20},{1,9},{5... | collective-permute-start | bytes 122888 | tf_op jit(solution)/shard_map/ppermute | solution.py:19
  68.2 9.9 %collective-permute-start.19 = (bf16[64,2304]{1,0:T(8,128)(2,1)S(1)}, bf16[64,2304]{1,0:T(8,128)(2,1)S(1)}, u32[]{:S(2)}, u32[]{:S(2)}) collective-permute-start(bf16[64,2304]{1,0:T(8,128)(2,1)S(1)} %slice_bitcast_fusion), channel_id=1, source_target_pairs={{0,1},{1,0},{2,3},{3,2},{4,5},{5,4},{6,7},{7,6},{8,9},{9,8},{10,11... | collective-permute-start | bytes 884744 | tf_op jit(solution)/shard_map/ppermute | solution.py:19
  69.0 13.5 %collective-permute-start.21 = (bf16[64,2304]{1,0:T(8,128)(2,1)S(1)}, bf16[64,2304]{1,0:T(8,128)(2,1)S(1)}, u32[]{:S(2)}, u32[]{:S(2)}) collective-permute-start(bf16[64,2304]{1,0:T(8,128)(2,1)S(1)} %collective-permute-done.20.refs_9_), channel_id=1, source_target_pairs={{0,1},{1,0},{2,3},{3,2},{4,5},{5,4},{6,7},{7,6},{8,9},{9,8},{10,11... | collective-permute-start | bytes 884744 | tf_op jit(solution)/shard_map/ppermute | solution.py:19
  70.3 12.1 %collective-permute-start.18 = (f32[80,128]{1,0:T(8,128)S(1)}, f32[80,128]{1,0:T(8,128)S(1)}, u32[]{:S(2)}, u32[]{:S(2)}) collective-permute-start(f32[80,128]{1,0:T(8,128)S(1)} %add_add_fusion.refs_0_), channel_id=1, source_target_pairs={{0,4},{4,0},{8,12},{12,8},{16,20},{20,16},{24,28},{28,24},{1,5},{5... | collective-permute-start | bytes 122888 | tf_op jit(solution)/shard_map/ppermute | solution.py:19
